TPU v7x, 32 devices: a whole 2x2x4 slice. The times are simulated.
32 devices in a mesh: slab: 4 (over y, core), patch: 8 (over z, x).
Axes of the slice: x: 2, y: 2, z: 4, core: 2. Of those that a mesh axis runs over, the one named last changes fastest.
Arguments:
- coarse: float32 [5, 64, 128, 128], P(None, 'slab', 'patch'), may hold values from -1.2 to 7.7, as said below
- fine: float32 [5, 128, 32, 1024], P(None, ('slab', 'patch')), may hold values from -1.2 to 7.7, as said below
- columns: int32 [32, 2], replicated, may hold values from 0 to 5, as said below
- patch_ids: int32 [4, 32], P('slab'), may hold values from 0 to 31, each once within a row
Outputs:
- coarse_out: float32 [5, 64, 128, 128], P(None, 'slab', 'patch')
- fine_out: float32 [5, 128, 32, 1024], P(None, ('slab', 'patch'))
Inputs may be any that keep to these rules, and one draw needn't show every extreme that they name: `coarse`: conserved variables of states with density and pressure between 0.5 and 2 and velocity components between -0.6 and 1.4. `fine`: conserved variables of states with density and pressure between 0.5 and 2 and velocity components between -0.6 and 1.4. `columns`: 32 distinct pairs (gy, gz) with gy below 6 and gz below 6. `patch_ids`: each row is a permutation of the 32 patch numbers of a slab.
All inputs are finite; a program needn't handle non-finite values.
Results may differ from a plain program's by a relative error of at most 0.00005.
Values sent between devices are 32-bit elements; how exact they have to be, the bound alone decides.
No kernel may reach another device: no remote copies, remote signals or barrier semaphores. Data moves between devices by JAX's collectives and lax.ppermute only.
A program may use at most 320 MiB of HBM per device.

v0:
```python
import jax
import jax.numpy as jnp
from jax import lax
from jax.sharding import PartitionSpec as P

P_SIZE = 32
LX = 1
GY = 6
GZ = 6
PYZ = 32
H = 16


heat_ratio = 1.4
fine_rate = 0.1
coarse_rate = 0.05
highest = lax.Precision.HIGHEST


def padded(block, sides, width):
    for axis, dim in sides:
        count = lax.axis_size(axis)
        forward = [(i, i + 1) for i in range(count - 1)]
        backward = [(target, source) for source, target in forward]
        low = lax.ppermute(
            lax.slice_in_dim(block, block.shape[dim] - width, None, axis=dim), axis, forward
        )
        high = lax.ppermute(lax.slice_in_dim(block, 0, width, axis=dim), axis, backward)
        block = jnp.concatenate([low, block, high], axis=dim)
    return block


def euler_flux(fields, normal_axis):
    density = fields[0]
    momentum = fields[1:4]
    energy = fields[4]
    velocity = momentum / density
    pressure = (heat_ratio - 1.0) * (energy - 0.5 * jnp.sum(momentum * velocity, axis=0))
    normal_speed = velocity[normal_axis]
    components = [
        momentum[normal_axis],
        momentum[0] * normal_speed,
        momentum[1] * normal_speed,
        momentum[2] * normal_speed,
        (energy + pressure) * normal_speed,
    ]
    components[1 + normal_axis] = components[1 + normal_axis] + pressure
    signal = jnp.abs(normal_speed) + jnp.sqrt(heat_ratio * pressure / density)
    return (jnp.stack(components), signal)


def rusanov(left_side, right_side, normal_axis):
    left_flux, left_signal = euler_flux(left_side, normal_axis)
    right_flux, right_signal = euler_flux(right_side, normal_axis)
    return 0.5 * (left_flux + right_flux) - 0.5 * jnp.maximum(left_signal, right_signal) * (
        right_side - left_side
    )


def advance(fields, ghosts):
    x_low, x_high, z_low, z_high, y_low, y_high = ghosts
    patch_count = fields.shape[1]
    side_cells = fields.shape[2]
    lane_count = side_cells * side_cells
    cube_view = fields.reshape(5, patch_count, side_cells, side_cells, side_cells)
    along_x = jnp.concatenate(
        [
            x_low.reshape(5, patch_count, 1, lane_count),
            fields,
            x_high.reshape(5, patch_count, 1, lane_count),
        ],
        axis=2,
    )
    flux_x = rusanov(along_x[:, :, :-1], along_x[:, :, 1:], 0)
    lane_index = jnp.arange(lane_count, dtype=jnp.int32)
    y_place = lane_index % side_cells
    z_place = lane_index // side_cells
    z_beyond = jnp.where(
        z_place == side_cells - 1,
        jnp.tile(z_high, (1, 1, 1, side_cells)),
        jnp.roll(fields, -side_cells, axis=3),
    )
    z_upper_flux = rusanov(fields, z_beyond, 2)
    z_edge = rusanov(z_low, cube_view[:, :, :, 0], 2)
    z_lower_flux = jnp.where(
        z_place == 0,
        jnp.tile(z_edge, (1, 1, 1, side_cells)),
        jnp.roll(z_upper_flux, side_cells, axis=3),
    )
    y_beyond = jnp.where(
        y_place == side_cells - 1,
        jnp.repeat(y_high, side_cells, axis=3),
        jnp.roll(fields, -1, axis=3),
    )
    y_upper_flux = rusanov(fields, y_beyond, 1)
    y_edge = rusanov(y_low, cube_view[..., 0], 1)
    y_lower_flux = jnp.where(
        y_place == 0, jnp.repeat(y_edge, side_cells, axis=3), jnp.roll(y_upper_flux, 1, axis=3)
    )
    change = (
        flux_x[:, :, 1:]
        - flux_x[:, :, :-1]
        + (z_upper_flux - z_lower_flux)
        + (y_upper_flux - y_lower_flux)
    )
    updated = fields - fine_rate * change
    y_top = y_upper_flux.reshape(5, patch_count, side_cells, side_cells, side_cells)[
        ..., side_cells - 1
    ]
    z_top = z_upper_flux[..., (side_cells - 1) * side_cells :]
    return (updated, (y_edge, y_top, z_edge, z_top))


def pair_mean(face_cells):
    extents = face_cells.shape
    return face_cells.reshape(extents[0], extents[1], extents[2] // 2, 2, extents[3] // 2, 2).mean(
        axis=(3, 5)
    )


def cell_mean(fields):
    extents = fields.shape
    return fields.reshape(
        extents[0], extents[1], extents[2] // 2, 2, extents[3] // 2, 2, extents[4] // 2, 2
    ).mean(axis=(3, 5, 7))


def upsample(face_cells):
    return jnp.repeat(jnp.repeat(face_cells, 2, axis=-2), 2, axis=-1)


def onehot(indices, extent):
    return (indices[:, None] == jnp.arange(extent, dtype=jnp.int32)[None, :]).astype(jnp.float32)


def neighbours(columns, step_y, step_z):
    matches = (columns[None, :, 0] == columns[:, None, 0] + step_y) & (
        columns[None, :, 1] == columns[:, None, 1] + step_z
    )
    present = jnp.any(matches, axis=1)
    partner = jnp.sum(
        jnp.where(matches, jnp.arange(columns.shape[0], dtype=jnp.int32)[None, :], 0), axis=1
    )
    return (present, partner)


def block_targets(column_y, column_z):
    grid_width = GY + 2
    return (
        (column_z + 1) * grid_width + column_y + 1,
        (column_z + 1) * grid_width + column_y,
        (column_z + 1) * grid_width + column_y + 2,
        column_z * grid_width + column_y + 1,
        (column_z + 2) * grid_width + column_y + 1,
    )


def cover_mask(columns):
    centre = block_targets(columns[:, 0], columns[:, 1])[0]
    occupied = jnp.sum(onehot(centre, (GZ + 2) * (GY + 2)), axis=0)
    return jnp.repeat(jnp.repeat(occupied.reshape(GZ + 2, GY + 2), H, axis=0), H, axis=1)


def block_form(slab):
    layer_depth = slab.shape[1] // H
    shaped = slab.reshape(5, layer_depth, H, GZ + 2, H, GY + 2, H).transpose(0, 1, 2, 4, 6, 3, 5)
    return shaped.reshape(5, layer_depth, H, H, H, (GZ + 2) * (GY + 2))


def slab_form(blocks):
    layer_depth = blocks.shape[1]
    shaped = blocks.reshape(5, layer_depth, H, H, H, GZ + 2, GY + 2).transpose(0, 1, 2, 5, 3, 6, 4)
    return shaped.reshape(5, layer_depth * H, (GZ + 2) * H, (GY + 2) * H)


def slot_order(numbers):
    slot_range = jnp.arange(numbers.shape[0], dtype=jnp.int32)
    found = jnp.sum(
        jnp.where(numbers[:, None] == slot_range[None, :], slot_range[:, None], 0), axis=0
    )
    return jnp.clip(found, 0, numbers.shape[0] - 1)


def coarse_faces(slab, layer_index, column_y, column_z):
    blocks = block_form(slab)
    layer_pick = onehot(layer_index, LX)
    centre, below_y, above_y, below_z, above_z = block_targets(column_y, column_z)
    nblocks = blocks.shape[-1]

    def select(portion, target):
        return jnp.einsum(
            "nl,nb,vlxzb->vnxz", layer_pick, onehot(target, nblocks), portion, precision=highest
        )

    return (
        select(blocks[:, :, :, :, H - 1], below_y),
        select(blocks[:, :, :, :, 0], above_y),
        select(blocks[:, :, :, H - 1], below_z),
        select(blocks[:, :, :, 0], above_z),
    )


def coarse_terms(averaged, face_terms, layer_index, column_y, column_z):
    layer_pick = onehot(layer_index, LX)
    centre, below_y, above_y, below_z, above_z = block_targets(column_y, column_z)
    nblocks = (GZ + 2) * (GY + 2)
    first_row = (jnp.arange(H) == 0).astype(jnp.float32)
    last_row = (jnp.arange(H) == H - 1).astype(jnp.float32)

    def spread(values, target):
        return jnp.einsum(
            "nl,nb,vnxz->vlxzb", layer_pick, onehot(target, nblocks), values, precision=highest
        )

    y_lower, y_upper, z_lower, z_upper = face_terms
    totals = jnp.einsum(
        "nl,nb,vnxzy->vlxzyb", layer_pick, onehot(centre, nblocks), averaged, precision=highest
    )
    totals = totals + spread(y_lower, below_y)[:, :, :, :, None, :] * last_row[:, None]
    totals = totals + spread(y_upper, above_y)[:, :, :, :, None, :] * first_row[:, None]
    totals = totals + spread(z_lower, below_z)[:, :, :, None, :, :] * last_row[:, None, None]
    totals = totals + spread(z_upper, above_z)[:, :, :, None, :, :] * first_row[:, None, None]
    return slab_form(totals)


def local(coarse, fine, columns, patch_ids):
    own_count = fine.shape[1]
    row_count = coarse.shape[2]
    patch_rank = lax.axis_index("patch")
    slab_rank = lax.axis_index("slab")
    slab_total = lax.axis_size("slab")
    numbers = patch_ids[0]
    own_numbers = lax.dynamic_slice_in_dim(numbers, patch_rank * own_count, own_count)
    inverse = slot_order(numbers)
    cube_fields = fine.reshape(5, own_count, P_SIZE, P_SIZE, P_SIZE)
    own_faces = jnp.stack(
        [
            cube_fields[:, :, 0],
            cube_fields[:, :, P_SIZE - 1],
            cube_fields[:, :, :, 0],
            cube_fields[:, :, :, P_SIZE - 1],
            cube_fields[..., 0],
            cube_fields[..., P_SIZE - 1],
        ]
    )
    slab_faces = lax.all_gather(own_faces, "patch", axis=2, tiled=True)
    slab_faces = jnp.take(slab_faces, inverse, axis=2)
    edge_faces = jnp.stack([slab_faces[0, :, :PYZ], slab_faces[1, :, -PYZ:]])
    rim_faces = padded(edge_faces, (("slab", 0),), 1)
    lower_rim = rim_faces[0]
    upper_rim = rim_faces[3]
    lower_source = jnp.where(slab_rank == 0, slab_faces[0, :, :PYZ], lower_rim)
    upper_source = jnp.where(slab_rank == slab_total - 1, slab_faces[1, :, -PYZ:], upper_rim)
    x_lower_table = jnp.concatenate([lower_source, slab_faces[1, :, :-PYZ]], axis=1)
    x_upper_table = jnp.concatenate([slab_faces[0, :, PYZ:], upper_source], axis=1)
    layer_index = own_numbers // PYZ
    column_index = own_numbers % PYZ
    column_y = columns[column_index, 0]
    column_z = columns[column_index, 1]
    whole_slab = lax.all_gather(coarse, "patch", axis=2, tiled=True)
    injected = coarse_faces(whole_slab, layer_index, column_y, column_z)

    def blend_faces(face_id, step_y, step_z, coarse_face):
        present, partner = neighbours(columns, step_y, step_z)
        target = layer_index * PYZ + partner[column_index]
        neighbour_face = jnp.take(slab_faces[face_id], target, axis=1)
        keep_mask = present[column_index][None, :, None, None]
        return jnp.where(keep_mask, neighbour_face, upsample(coarse_face))

    ghosts = (
        jnp.take(x_lower_table, own_numbers, axis=1),
        jnp.take(x_upper_table, own_numbers, axis=1),
        blend_faces(3, 0, -1, injected[2]),
        blend_faces(2, 0, 1, injected[3]),
        blend_faces(5, -1, 0, injected[0]),
        blend_faces(4, 1, 0, injected[1]),
    )
    updated, boundary = advance(fine, ghosts)

    def absent_mask(step_y, step_z):
        gaps = 1.0 - neighbours(columns, step_y, step_z)[0].astype(jnp.float32)
        return gaps[column_index][None, :, None, None]

    y_lower = -coarse_rate * pair_mean(boundary[0]) * absent_mask(-1, 0)
    y_upper = coarse_rate * pair_mean(boundary[1]) * absent_mask(1, 0)
    z_lower = -coarse_rate * pair_mean(boundary[2]) * absent_mask(0, -1)
    z_upper = coarse_rate * pair_mean(boundary[3]) * absent_mask(0, 1)
    averaged = cell_mean(updated.reshape(5, own_count, P_SIZE, P_SIZE, P_SIZE))
    placed = coarse_terms(
        averaged, (y_lower, y_upper, z_lower, z_upper), layer_index, column_y, column_z
    )
    contrib = lax.psum_scatter(placed, "patch", scatter_dimension=2, tiled=True)
    margin_cells = padded(coarse, (("slab", 1), ("patch", 2)), 1)
    before_x = jnp.where(slab_rank == 0, coarse[:, :1], margin_cells[:, :1, 1:-1])
    after_x = jnp.where(slab_rank == slab_total - 1, coarse[:, -1:], margin_cells[:, -1:, 1:-1])
    along_x = jnp.concatenate([before_x, coarse, after_x], axis=1)
    before_z = jnp.where(patch_rank == 0, coarse[:, :, :1], margin_cells[:, 1:-1, :1])
    after_z = jnp.where(
        patch_rank == lax.axis_size("patch") - 1, coarse[:, :, -1:], margin_cells[:, 1:-1, -1:]
    )
    along_z = jnp.concatenate([before_z, coarse, after_z], axis=2)
    along_y = jnp.concatenate([coarse[..., :1], coarse, coarse[..., -1:]], axis=3)
    covered = cover_mask(columns)
    own_cover = lax.dynamic_slice_in_dim(covered, patch_rank * row_count, row_count, 0)
    cover_z = lax.dynamic_slice_in_dim(
        jnp.pad(covered, ((1, 1), (0, 0))), patch_rank * row_count, row_count + 2, 0
    )
    cover_y = jnp.pad(own_cover, ((0, 0), (1, 1)))
    flux_x = rusanov(along_x[:, :-1], along_x[:, 1:], 0) * (1.0 - own_cover)
    flux_z = rusanov(along_z[:, :, :-1], along_z[:, :, 1:], 2) * (
        (1.0 - cover_z[:-1]) * (1.0 - cover_z[1:])
    )
    flux_y = rusanov(along_y[..., :-1], along_y[..., 1:], 1) * (
        (1.0 - cover_y[:, :-1]) * (1.0 - cover_y[:, 1:])
    )
    change = (
        flux_x[:, 1:]
        - flux_x[:, :-1]
        + (flux_z[:, :, 1:] - flux_z[:, :, :-1])
        + (flux_y[..., 1:] - flux_y[..., :-1])
    )
    provisional = coarse - coarse_rate * change
    coarse_out = jnp.where(own_cover > 0, contrib, provisional + contrib)
    return (coarse_out, updated)


def solution(mesh):
    return jax.shard_map(
        local,
        mesh=mesh,
        in_specs=(
            P(None, "slab", "patch", None),
            P(None, ("slab", "patch"), None, None),
            P(),
            P("slab", None),
        ),
        out_specs=(P(None, "slab", "patch", None), P(None, ("slab", "patch"), None, None)),
        check_vma=False,
    )
```

profile of v0, /device:TPU:17, one launch (start us, length us, event | category | flops | bytes accessed | tf_op | source)
XLA Modules:
  0.0 1048.4 jit_solution(5317102842722173065)
XLA Ops:
  7.2 7.9 reshape.643
  20.1 16.2 %fusion.237 = (f32[5,4,32,32,1]{4,3,2,1,0:T(8,128)}, f32[5,4,32,32,1]{4,3,2,1,0:T(8,128)}) fusion(f32[5,4,32,32,32]{4,3,2,1,0:T(8,128)} %reshape.643), kind=kLoop, calls=%fused_computation.640 | loop fusion | bytes 327680 | tf_op jit(solution)/shard_map/slice | solution.py:243
  36.3 6.7 copy.483
  43.0 7.5 copy.484
  68.4 9.0 slice_reduce_fusion
  77.4 6.1 slice.909
  126.6 142.7 %all-gather.3.cloned.1.call-done = f32[6,5,32,32,32]{4,3,1,2,0:T(8,128)} async-done(((f32[6,5,4,32,32]{4,3,1,2,0:T(8,128)}), f32[6,5,32,32,32]{4,3,1,2,0:T(8,128)}) %all-gather.3.cloned.1.call-update) | async-done | bytes 3932176 | tf_op jit(solution)/shard_map/all_gather | solution.py:246
  269.2 13.7 %gather_fusion.2 = f32[32,6,5,32,32]{4,3,2,1,0:T(8,128)} fusion(f32[6,5,32,32,32]{4,3,1,2,0:T(8,128)} %all-gather.3.cloned.1.call-done, s32[1024]{0:T(1024)S(1)} %pad_clamp_fusion.6), kind=kCustom, calls=%fused_computation.8 | custom fusion | bytes 7864448 | tf_op jit(solution)/shard_map/jit(_take)/gather | solution.py:247
  283.0 6.8 copy_bitcast_fusion.1
  300.6 22.8 %collective-permute-done = f32[1,5,32,32,32]{4,3,2,1,0:T(8,128)S(1)} collective-permute-done((f32[1,5,32,32,32]{4,3,2,1,0:T(8,128)S(1)}, f32[1,5,32,32,32]{4,3,2,1,0:T(8,128)S(1)}, u32[]{:S(2)}, u32[]{:S(2)}) %collective-permute-start) | collective-permute-done | bytes 655392 | tf_op jit(solution)/shard_map/ppermute | solution.py:25
  328.2 8.6 select_bitcast_fusion.1
  366.3 24.1 %reshape.646 = f32[5,1,16,8,16,8,16]{6,5,4,3,2,0,1:T(8,128)} reshape(f32[5,16,128,128]{3,2,1,0:T(8,128)} %all-gather.5.cloned.1.call-done) | data formatting | bytes 10485760 | tf_op jit(solution)/shard_map/reshape | solution.py:166
  390.3 29.2 %copy.537 = f32[5,1,16,8,16,8,16]{6,5,3,4,2,0,1:T(8,128)} copy(f32[5,1,16,8,16,8,16]{6,5,4,3,2,0,1:T(8,128)} %reshape.646) | data formatting | bytes 10485760 | tf_op jit(solution)/shard_map/reshape | solution.py:166
  419.5 56.7 %fusion.234 = (f32[5,1,16,16,1,64]{4,5,3,2,0,1:T(8,128)}, f32[5,1,16,16,1,64]{4,5,3,2,0,1:T(8,128)}) fusion(f32[5,1,16,16,16,64]{4,5,3,2,0,1:T(8,128)} %bitcast.634), kind=kLoop, calls=%fused_computation.637 | loop fusion | bytes 1310720 | tf_op jit(solution)/shard_map/slice | solution.py:196
  483.8 23.0 %copy.496 = f32[5,1,16,16,1,64]{5,3,2,0,4,1:T(8,128)S(1)} copy(f32[5,1,16,16,1,64]{4,5,3,2,0,1:T(8,128)} %get-tuple-element.54) | data formatting | bytes 655360
  526.8 9.0 tile.9
  535.8 22.6 %copy.495 = f32[5,1,16,16,1,64]{5,3,2,0,4,1:T(8,128)S(1)} copy(f32[5,1,16,16,1,64]{4,5,3,2,0,1:T(8,128)} %get-tuple-element.55) | data formatting | bytes 655360
  569.9 9.3 reshape.657
  596.5 12.0 %constant_dynamic-update-slice_fusion.1 = (f32[5,4,33,1024]{3,2,1,0:T(8,128)}, f32[5,4,32,1024]{3,2,1,0:T(8,128)}, f32[5,4,32,1024]{3,2,1,0:T(8,128)}) fusion(f32[5,4,32,1024]{3,2,1,0:T(8,128)S(1)} %copy-done.2, f32[5,4,32,1024]{3,2,1,0:T(8,128)} %copy-done.6, f32[4,32,1024]{2,1,0:T(8,128)S(1)} %get-tuple-element.86, ...), kind=kLoop, calls=%fused_computation.344 | loop fusion | flops 6553599 | bytes 27262976
  608.4 8.1 reshape.663
  635.5 10.6 %slice.916 = f32[5,4,32,32,1]{4,3,2,1,0:T(8,128)} slice(f32[5,4,32,32,32]{4,3,2,1,0:T(8,128)} %reshape.663), slice={[0:5], [0:4], [0:32], [0:32], [31:32]} | slice | bytes 163840 | tf_op jit(solution)/shard_map/slice | solution.py:107
  646.2 27.1 %copy.504 = f32[5,4,32,32,1]{0,3,2,1,4:T(8,128)} copy(f32[5,4,32,32,1]{4,3,2,1,0:T(8,128)} %slice.916) | data formatting | bytes 163840
  701.2 9.1 tile.21
  716.1 9.1 reshape.661
  739.1 34.2 %copy.452 = f32[5,4,32,1024]{0,3,2,1:T(8,128)} copy(f32[5,4,32,1024]{3,2,1,0:T(8,128)} %fusion.11) | data formatting | bytes 5242880 | tf_op jit(solution)/shard_map/sub | solution.py:106
  773.4 49.4 %reduce_sum.253 = f32[5,4,16,16,16]{0,4,3,2,1:T(8,128)} reduce(f32[5,4,16,2,16,2,16,2]{0,7,6,5,4,3,2,1:T(2,128)} %bitcast.120, f32[]{:T(128)} %constant.88.clone.1), dimensions={3,5,7}, to_apply=%region_19.21 | reduce | flops 573440 | bytes 2949124 | tf_op jit(solution)/shard_map/reduce_sum | solution.py:125
  822.8 9.3 copy.453
  833.8 23.2 %fusion.2 = f32[5,1,16,16,16,64]{5,4,3,2,0,1:T(8,128)} fusion(f32[16]{0:T(128)S(1)} %copy-done.77, f32[5,16,16,64]{3,2,1,0:T(8,128)S(1)} %copy-done.46, f32[16]{0:T(128)S(1)} %copy-done.78, f32[5,16,16,64]{3,2,1,0:T(8,128)S(1)} %copy-done.47, f32[5,16,16,64]{3,2,1,0:T(8,128)S(1)} %copy-done.48, f32[5,16,16,64]{3,2,1,0:T(8,128)S(1)} %copy-done.49, ...), kind=kOutput, calls=%fused_computation.33 | convolution fusion | flops 73400832 | bytes 6881440 | tf_op jit(solution)/shard_map/nl,nb,vnxzy->vlxzyb/dot_general | solution.py:216
  857.0 24.4 %copy.467 = f32[5,1,16,16,16,64]{4,5,3,2,0,1:T(8,128)} copy(f32[5,1,16,16,16,64]{5,4,3,2,0,1:T(8,128)} %fusion.2) | data formatting | bytes 10485760 | tf_op jit(solution)/shard_map/add | solution.py:222
  881.3 29.1 %copy.468 = f32[5,1,16,8,16,8,16]{6,5,4,3,2,0,1:T(8,128)} copy(f32[5,1,16,8,16,8,16]{6,5,3,4,2,0,1:T(8,128)} %bitcast.637) | data formatting | bytes 10485760 | tf_op jit(solution)/shard_map/transpose | solution.py:172
  910.4 26.5 %reshape.667 = f32[5,16,128,128]{3,2,1,0:T(8,128)} reshape(f32[5,1,16,8,16,8,16]{6,5,4,3,2,0,1:T(8,128)} %copy.468) | data formatting | bytes 10485760 | tf_op jit(solution)/shard_map/reshape | solution.py:173
  957.2 81.5 %reduce-scatter.2.cloned.1.call-done = f32[5,16,16,128]{3,2,1,0:T(8,128)} async-done(((f32[5,16,128,128]{3,2,1,0:T(8,128)}), f32[5,16,16,128]{3,2,1,0:T(8,128)}) %reduce-scatter.2.cloned.1.call-update) | async-done | bytes 655376 | tf_op jit(solution)/shard_map/reduce_scatter | solution.py:292
  (410 shorter events, 257.6 us)
Async XLA Ops:
  7.2 262.1 %all-gather.3.cloned.1.call-start = ((), (), s32[]{:S(2)}) async-start(), calls=%async_computation.1 | async-start | bytes 17694720 | tf_op jit(solution)/shard_map/all_gather | solution.py:246
  43.0 10.7 %copy-start.30 = (f32[5,4,32,32,1]{3,2,0,1,4:T(8,128)}, f32[5,4,32,32,1]{3,2,0,1,4:T(8,128)S(1)}, u32[]{:S(2)}) copy-start(f32[5,4,32,32,1]{3,2,0,1,4:T(8,128)S(1)} %copy.483) | copy-start | bytes 245764
  50.5 6.2 copy-start
  51.8 6.0 copy-start.1
  55.2 311.1 %all-gather.5.cloned.1.call-start = ((), (), s32[]{:S(2)}) async-start(), calls=%async_computation.2 | async-start | bytes 5898240 | tf_op jit(solution)/shard_map/all_gather | solution.py:260
  55.9 982.8 %reduce-scatter.2.cloned.1.call-start = ((), (), s32[]{:S(2)}) async-start(), calls=%async_computation.3 | async-start | bytes 5898240 | tf_op jit(solution)/shard_map/reduce_scatter | solution.py:292
  112.4 13.0 %copy-start.52 = (f32[1,4,32,1,32]{4,3,2,1,0:T(1,128)}, f32[1,4,32,1,32]{4,3,2,1,0:T(1,128)S(1)}, u32[]{:S(2)}) copy-start(f32[1,4,32,1,32]{4,3,2,1,0:T(1,128)S(1)} %get-tuple-element.70) | copy-start | bytes 49156
  120.8 162.2 %copy-start.56 = (f32[4,32,32]{2,1,0:T(8,128)}, f32[4,32,32]{2,1,0:T(8,128)S(1)}, u32[]{:S(2)}) copy-start(f32[4,32,32]{2,1,0:T(8,128)S(1)} %get-tuple-element.161) | copy-start | bytes 49156
  289.8 7.8 copy-start.35
  290.4 33.0 %collective-permute-start = (f32[1,5,32,32,32]{4,3,2,1,0:T(8,128)S(1)}, f32[1,5,32,32,32]{4,3,2,1,0:T(8,128)S(1)}, u32[]{:S(2)}, u32[]{:S(2)}) collective-permute-start(f32[1,5,32,32,32]{4,3,2,1,0:T(8,128)S(1)} %get-tuple-element.62), channel_id=1, source_target_pairs={{0,8},{8,16},{16,24},{1,9},{9,17},{17,25},{2,10},{10,18},{18,26},{... | collective-permute-start | bytes 1966088 | tf_op jit(solution)/shard_map/ppermute | solution.py:25
  294.8 33.4 %collective-permute-start.1 = (f32[1,5,32,32,32]{4,3,2,1,0:T(8,128)S(1)}, f32[1,5,32,32,32]{4,3,2,1,0:T(8,128)}, u32[]{:S(2)}, u32[]{:S(2)}) collective-permute-start(f32[1,5,32,32,32]{4,3,2,1,0:T(8,128)S(1)} %get-tuple-element.63), channel_id=1, source_target_pairs={{8,0},{16,8},{24,16},{9,1},{17,9},{25,17},{10,2},{18,10},{26,18},{... | collective-permute-start | bytes 1966088 | tf_op jit(solution)/shard_map/ppermute | solution.py:28
  350.0 15.3 %copy-start.22 = (f32[5,4,1,1024]{3,2,1,0:T(1,128)}, f32[5,4,1,1024]{3,2,1,0:T(1,128)S(1)}, u32[]{:S(2)}) copy-start(f32[5,4,1,1024]{3,2,1,0:T(1,128)S(1)} %copy.387) | copy-start | bytes 245764
  535.8 22.7 %copy-start.63 = (s32[4]{0:T(128)S(1)}, s32[4]{0:T(128)}, u32[]{:S(2)}) copy-start(s32[4]{0:T(128)} %broadcast_add_fusion) | copy-start | bytes 52
  569.8 9.3 slice-start.1
  569.9 9.4 copy-start.15
  569.9 9.4 copy-start.70
  619.5 6.8 copy-start.28
  619.5 6.8 copy-start.74
  625.1 8.2 copy-start.73
  676.7 6.7 copy-start.71
  677.3 8.2 copy-start.60
  701.2 9.1 copy-start.40
  716.1 9.1 copy-start.20
  716.1 9.1 copy-start.23
  729.2 6.0 copy-start.18
  729.2 6.0 copy-start.41
  729.2 6.0 copy-start.61
  729.2 6.0 copy-start.62
  938.0 8.8 collective-permute-start.2
  939.9 6.9 collective-permute-start.3
  946.9 8.9 collective-permute-start.4
  949.1 6.7 collective-permute-start.5
  (58 other events, 153.3 us)
Sparse Core Ops, SparseCore 0:
  55.3 213.8 all-gather.2
  271.3 84.9 all-gather.4
  937.0 101.6 reduce-scatter.1
where the time goes:
time: 1060 us; the launch traced here: 1050 us
  local copies, waits for them, and re-layouts  560 us (53%)
  waiting for transfers between devices  253 us (24%)
  other arithmetic  155 us (15%)
  matrix products  47.3 us (4%)
  starting transfers between devices  17.3 us (2%)
  between operations  15.5 us (1%)
    all_gather x1, waiting for transfers between devices, local(): slab_faces = lax.all_gather(own_faces, 'patch', axis=2, tiled=True)  143 us
    unnamed x179, local copies, waits for them, and re-layouts  124 us
    reduce_scatter x1, waiting for transfers between devices, local(): contrib = lax.psum_scatter(placed, 'patch', scatter_dimension=2, tiled=True)  81.5 us
    slice x1, local copies, waits for them, and re-layouts, coarse_faces(): blocks[:, :, :, :, H - 1]  56.7 us
    reshape x2, local copies, waits for them, and re-layouts, block_form(): slab.reshape(5, layer_depth, H, GZ + 2, H, GY + 2, H)  53.2 us
    reduce_sum x1, other arithmetic, cell_mean(): return fields.reshape(extents[0], extents[1], extents[2] // 2, 2, extents...  49.4 us
    sub x1, local copies, waits for them, and re-layouts, advance(): updated = fields - fine_rate * change  34.2 us
    transpose x1, local copies, waits for them, and re-layouts, slab_form(): blocks.reshape(5, layer_depth, H, H, H, GZ + 2, GY + 2)  29.1 us
  transfers between devices with their start and end apart: 9, of which 5 were waited for; matrix products, arithmetic and copies ran while one was open for 13% of the time, Pallas kernels for 0%

commit v1 on v0

v1 whole, which is shorter than its diff:
```python
import functools

import jax
import jax.numpy as jnp
from jax import lax
from jax.experimental import pallas as pl
from jax.experimental.pallas import tpu as pltpu
from jax.sharding import PartitionSpec as P

LANES = 128
heat_ratio = 1.4
fine_rate = 0.1
coarse_rate = 0.05
VMEM = pl.BlockSpec(memory_space=pltpu.VMEM)
SMEM = pl.BlockSpec(memory_space=pltpu.SMEM)


def up8(count):
    return -(-count // 8) * 8


class Sizes:
    def __init__(self, n, slabs, fine_shape, coarse_shape, slots):
        self.n, self.slabs, self.S = n, slabs, slots
        self.own = fine_shape[1]
        self.P = fine_shape[2]
        self.cells = fine_shape[3]
        self.H = self.P // 2
        self.G = self.cells // LANES
        self.zg = LANES // self.P
        self.xa = self.P // n
        self.xc = self.H // n
        self.PL = self.cells // n
        self.zcl = self.P // n // 2
        self.NX, self.R, self.NY = coarse_shape[1:]
        self.m = self.H // self.R
        self.NZ = self.R * n
        self.lines = 2 * (self.NY // self.H)
        assert self.NX == self.H and self.NY == LANES and self.H % self.R == 0
        assert self.P % (2 * n) == 0 and 4 * self.P == LANES and slots == self.own * n
        self.lat = 5 * self.xa * self.own
        self.ny = -(-(5 * self.xc * self.R) // LANES)
        self.OY = up8(self.lat)
        self.OZ = self.OY + self.lines * self.ny
        self.RC = up8(self.OZ + 10 * self.xc)
        self.RX = up8(10 * self.own)
        self.RA = 5 * self.H
        self.OFX = self.lat
        self.RF = up8(self.lat + 10 * self.own)
        self.OXQ = 5 * self.xc * self.R
        self.RK = up8(self.OXQ + 10 * self.zcl)
        self.RM = 5 * self.R + 8


def parts(x, count):
    out = []
    for _ in range(count):
        piece = x.astype(jnp.bfloat16)
        out.append(piece)
        x = x - piece.astype(jnp.float32)
    return out


def select_dot(pick, x, count=3, dims=(((1,), (0,)), ((), ()))):
    total = None
    for piece in parts(x, count):
        term = lax.dot_general(pick, piece, dims, preferred_element_type=jnp.float32)
        total = term if total is None else total + term
    return total


def lanes_at(x, index):
    return jnp.take_along_axis(x, index, axis=1, mode="promise_in_bounds")


def derived(U):
    inverse = 1.0 / U[0]
    velocity = [U[1] * inverse, U[2] * inverse, U[3] * inverse]
    kinetic = U[1] * velocity[0] + U[2] * velocity[1] + U[3] * velocity[2]
    pressure = (heat_ratio - 1.0) * (U[4] - 0.5 * kinetic)
    sound = jnp.sqrt(heat_ratio * pressure * inverse)
    return velocity, pressure, sound


def directed(U, speed, pressure, d):
    out = [U[0] * speed if d is None else U[1 + d]]
    out += [U[1 + e] * speed + (pressure if e == d else 0.0) if e == d else U[1 + e] * speed for e in range(3)]
    out.append((U[4] + pressure) * speed)
    return out


def twice_flux(L, dl, R, dr, d):
    fl = directed(L, dl[0], dl[1], d)
    fr = directed(R, dr[0], dr[1], d)
    signal = jnp.maximum(jnp.abs(dl[0]) + dl[2], jnp.abs(dr[0]) + dr[2])
    return [fl[v] + fr[v] - signal * (R[v] - L[v]) for v in range(5)]


def state_flux(L, R, d):
    vl, pl_, cl = derived(L)
    vr, pr, cr = derived(R)
    return twice_flux(L, (vl[d], pl_, cl), R, (vr[d], pr, cr), d)


def extract_kernel(z, fine, coarse, number_row, com, xf, up, dn, pu, pd, scr):
    lane = lax.broadcasted_iota(jnp.int32, (z.P, LANES), 1)
    pick = z.P * ((lane % z.P) % z.zg) + jnp.where(lane >= 3 * z.P, z.P - 1, 0)
    group = jnp.where(lane >= 2 * z.P, (lane % z.P) // z.zg, -1)
    for q in range(z.own):
        for v in range(5):
            first = fine[v, q, :, :LANES]
            last = fine[v, q, :, (z.G - 1) * LANES :]
            face = jnp.where(lane < z.P, first, pltpu.roll(last, 2 * z.P, 1))
            for g in range(z.G):
                chunk = fine[v, q, :, g * LANES : (g + 1) * LANES]
                face = jnp.where(group == g, lanes_at(chunk, pick), face)
            scr[v % 2] = face
            for a in range(z.xa):
                com[pl.ds((v * z.xa + a) * z.own + q, z.n, stride=z.RC), :] = scr[v % 2, pl.ds(a, z.n, stride=z.xa), :]
            for side in range(2):
                row = fine[v, q, side * (z.P - 1) : side * (z.P - 1) + 1, :]
                place = (side * 5 + v) * z.own + q
                for j in range(z.n):
                    xf[j * z.RX + place : j * z.RX + place + 1, : z.PL] = row[:, j * z.PL : (j + 1) * z.PL]
    line = lax.broadcasted_iota(jnp.int32, (z.lines, LANES), 0)
    at = lax.broadcasted_iota(jnp.int32, (z.lines, LANES), 1)
    chosen = (at == z.H * (line // 2) + (z.H - 1) * (line % 2)).astype(jnp.bfloat16)
    width = 5 * z.xc * z.R
    for j in range(z.n):
        block = coarse[:, j * z.xc : (j + 1) * z.xc].reshape(width, LANES)
        lines = select_dot(chosen, block, 3, (((1,), (1,)), ((), ())))
        for t in range(z.ny):
            extent = min(LANES, width - t * LANES)
            com[j * z.RC + z.OY + t * z.lines : j * z.RC + z.OY + (t + 1) * z.lines, :extent] = lines[
                :, t * LANES : t * LANES + extent
            ]
        for v in range(5):
            for x in range(z.xc):
                row = j * z.RC + z.OZ + (v * z.xc + x) * 2
                com[row : row + 1, :] = coarse[v, j * z.xc + x, 0:1, :]
                com[row + 1 : row + 2, :] = coarse[v, j * z.xc + x, z.R - 1 : z.R, :]
    for v in range(5):
        up[v * z.R : (v + 1) * z.R, :] = coarse[v, z.NX - 1]
        dn[v * z.R : (v + 1) * z.R, :] = coarse[v, 0]
        for x in range(z.NX):
            row = v * z.NX + x
            pu[row : row + 1, :] = coarse[v, x, z.R - 1 : z.R, :]
            pd[row : row + 1, :] = coarse[v, x, 0:1, :]
    numbers = jnp.broadcast_to(number_row[...], (8, LANES))
    up[5 * z.R : 5 * z.R + 8, :] = numbers
    dn[5 * z.R : 5 * z.R + 8, :] = numbers


def advance_kernel(z, fine, updated, avg, der, zflux, sums):
    lane = lax.broadcasted_iota(jnp.int32, (z.P, LANES), 1)
    row = lax.broadcasted_iota(jnp.int32, (z.P, LANES), 0)
    inner_x = row < z.P - 1
    inner_y = lane % z.P < z.P - 1
    high = lane >= LANES - z.P

    def first_pass(step, carry):
        q = step // z.G
        g = step % z.G
        at = pl.ds(pl.multiple_of(g * LANES, LANES), LANES)
        U = [fine[v, q, :, at] for v in range(5)]
        velocity, pressure, sound = derived(U)
        for k, value in enumerate(velocity + [pressure, sound]):
            der[k, q, :, at] = value
        return carry

    lax.fori_loop(0, z.own * z.G, first_pass, 0)

    def second_pass(step, carry):
        q = step // z.G
        g = step % z.G
        at = pl.ds(pl.multiple_of(g * LANES, LANES), LANES)
        nxt = pl.ds(pl.multiple_of(jnp.minimum(g + 1, z.G - 1) * LANES, LANES), LANES)
        U = [fine[v, q, :, at] for v in range(5)]
        D = [der[k, q, :, at] for k in range(5)]
        change = None
        for d in (0, 1):
            if d == 0:
                move = lambda a: pltpu.roll(a, z.P - 1, 0)
                back = lambda a: pltpu.roll(a, 1, 0)
                inner = inner_x
            else:
                move = lambda a: pltpu.roll(a, LANES - 1, 1)
                back = lambda a: pltpu.roll(a, 1, 1)
                inner = inner_y
            f = directed(U, D[d], D[3], d)
            s = jnp.abs(D[d]) + D[4]
            signal = jnp.maximum(s, move(s))
            up = []
            for v in range(5):
                face = f[v] + move(f[v]) - signal * (move(U[v]) - U[v])
                face = jnp.where(inner, face, 0.0)
                up.append(face - back(face))
            change = up if change is None else [change[v] + up[v] for v in range(5)]
        f = directed(U, D[2], D[3], 2)
        s = jnp.abs(D[2]) + D[4]
        UN = [fine[v, q, :, nxt] for v in range(5)]
        DN = [der[k, q, :, nxt] for k in (2, 3, 4)]
        fn = directed(UN, DN[0], DN[1], 2)
        sn = jnp.abs(DN[0]) + DN[2]
        beyond = lambda a, b: jnp.where(high, pltpu.roll(b, LANES - z.P, 1), pltpu.roll(a, LANES - z.P, 1))
        signal = jnp.maximum(s, beyond(s, sn))
        inner_z = jnp.logical_or(lane < LANES - z.P, g < z.G - 1)
        for v in range(5):
            face = f[v] + beyond(f[v], fn[v]) - signal * (beyond(U[v], UN[v]) - U[v])
            face = jnp.where(inner_z, face, 0.0)
            rolled = pltpu.roll(face, z.P, 1)
            before = jnp.where(g == 0, 0.0, zflux[v])
            zflux[v] = rolled
            total = change[v] + (face - jnp.where(lane < z.P, before, rolled))
            new = U[v] - (0.5 * fine_rate) * total
            updated[v, q, :, at] = new
            sums[pl.ds(pl.multiple_of(((v * z.own + q) * z.G + g) * z.P, z.P), z.P), :] = new
        return carry

    lax.fori_loop(0, z.own * z.G, second_pass, 0)
    spot = lax.broadcasted_iota(jnp.int32, (z.n, LANES), 1)
    half = z.zg // 2

    def average(step, carry):
        v = step // z.G
        g = step % z.G
        out = [jnp.zeros((z.n, LANES), jnp.float32) for _ in range(half)]
        for q in range(z.own):
            base = pl.multiple_of(((v * z.own + q) * z.G + g) * z.P, z.P)
            for x in range(z.xc):
                pair = sums[pl.ds(base + 2 * x, z.n, stride=z.xa), :] + sums[pl.ds(base + 2 * x + 1, z.n, stride=z.xa), :]
                pair = pair + pltpu.roll(pair, LANES - 1, 1)
                pair = pair + pltpu.roll(pair, LANES - z.P, 1)
                for h in range(half):
                    out[h] = jnp.where(
                        spot // z.H == x * z.own + q, lanes_at(pair, 2 * z.P * h + 2 * (spot % z.H)), out[h]
                    )
        for h in range(half):
            avg[pl.ds(v * z.H + half * g + h, z.n, stride=z.RA), :] = 0.125 * out[h]
        return carry

    lax.fori_loop(0, 5 * z.G, average, 0)


def coverage(columns, block_z, block_y, count):
    def step(k, found):
        return jnp.logical_or(found, (block_y == columns[k, 0] + 1) & (block_z == columns[k, 1] + 1)).astype(jnp.int32)

    return lax.fori_loop(0, count, step, jnp.zeros(block_z.shape, jnp.int32))


def provisional_kernel(z, info, columns, coarse, below, above, lower, upper, out, pad):
    slab, rank = info[0], info[1]
    row = lax.broadcasted_iota(jnp.int32, (z.R, LANES), 0)
    lane = lax.broadcasted_iota(jnp.int32, (z.R, LANES), 1)
    place = row + rank * z.R
    block = lambda a: (a + z.H) // z.H - 1
    count = columns.shape[0]
    cover = lambda dz, dy: coverage(columns, block(place + dz), block(lane + dy), count)
    own, zu, zd, yu, yd = [1.0 - cover(*s).astype(jnp.float32) for s in ((0, 0), (1, 0), (-1, 0), (0, 1), (0, -1))]
    for v in range(5):
        pad[v, 1 : z.NX + 1] = coarse[v]
        pad[v, 0] = jnp.where(slab == 0, coarse[v, 0], below[v * z.R : (v + 1) * z.R, :])
        pad[v, z.NX + 1] = jnp.where(slab == z.slabs - 1, coarse[v, z.NX - 1], above[v * z.R : (v + 1) * z.R, :])

    def layer(x, carry):
        U = [pad[v, x + 1] for v in range(5)]
        XL = [pad[v, x] for v in range(5)]
        XU = [pad[v, x + 2] for v in range(5)]
        ZL, ZU, YL, YU = [], [], [], []
        for v in range(5):
            low = jnp.where(rank == 0, U[v][0:1], lower[pl.ds(v * z.NX + x, 1), :])
            top = jnp.where(rank == z.n - 1, U[v][z.R - 1 :], upper[pl.ds(v * z.NX + x, 1), :])
            ZL.append(jnp.where(row == 0, low, pltpu.roll(U[v], 1, 0)))
            ZU.append(jnp.where(row == z.R - 1, top, pltpu.roll(U[v], z.R - 1, 0)))
            YL.append(jnp.where(lane == 0, U[v], pltpu.roll(U[v], 1, 1)))
            YU.append(jnp.where(lane == LANES - 1, U[v], pltpu.roll(U[v], LANES - 1, 1)))
        fx = [a - b for a, b in zip(state_flux(U, XU, 0), state_flux(XL, U, 0))]
        fz = [a * zu - b * zd for a, b in zip(state_flux(U, ZU, 2), state_flux(ZL, U, 2))]
        fy = [a * yu - b * yd for a, b in zip(state_flux(U, YU, 1), state_flux(YL, U, 1))]
        for v in range(5):
            value = U[v] - (0.5 * coarse_rate) * (fx[v] + fz[v] + fy[v])
            out[v, x] = jnp.where(own > 0.0, value, 0.0)
        return carry

    lax.fori_loop(0, z.NX, layer, 0)


def middle_kernel(z, info, spots, ctab, rtab, com, xo, xb, xu, below, above, avg, outf, outc, lat, ghost, xs, canvas):
    slab = info[0]
    S, f_of = z.S, z.P
    gy, gz, number = ctab[:, 0:1], ctab[:, 1:2], ctab[:, 2:3]
    gyr, gzr = rtab[0:1, :], rtab[1:2, :]
    lane = lax.broadcasted_iota(jnp.int32, (S, LANES), 1)
    kind = lane // f_of
    even = kind % 2 == 0
    steps = ((0, -1), (0, 1), (-1, 0), (1, 0))
    flags = [((gyr == gy + dy) & (gzr == gz + dz)).astype(jnp.float32) for dy, dz in steps]
    turned = [((gy == gyr + dy) & (gz == gzr + dz)).astype(jnp.float32) for dy, dz in steps]
    absent_row = [1.0 - jnp.sum(t, axis=0, keepdims=True) for t in turned]
    here = jnp.zeros((S, LANES), jnp.float32)
    for k in range(4):
        here = jnp.where(kind == k, jnp.sum(flags[k], axis=1, keepdims=True), here)
    picks = jnp.concatenate(flags, axis=1).astype(jnp.bfloat16)

    for i in range(z.n):
        for k in range(5 * z.xa):
            lat[k * S + i * z.own : k * S + (i + 1) * z.own, :] = com[i * z.RC + k * z.own : i * z.RC + (k + 1) * z.own, :]

    def onehot(index, extent):
        return (lax.broadcasted_iota(jnp.int32, (S, extent), 1) == index).astype(jnp.bfloat16)

    vx = 5 * z.xc
    low_lines = jnp.concatenate([com[pl.ds(z.OZ + 2 * k + 1, z.n, stride=z.RC), :] for k in range(vx)], axis=1)
    top_lines = jnp.concatenate([com[pl.ds(z.OZ + 2 * k, z.n, stride=z.RC), :] for k in range(vx)], axis=1)
    low_rows = select_dot(onehot(gz * z.m + z.m - 1, z.n), low_lines)
    top_rows = select_dot(onehot((gz + 2) * z.m, z.n), top_lines)
    y_index = z.H * (gy + 1) + (lane % f_of) // 2
    half = (lane % f_of) // 2
    y_rows = {}
    for t in range(z.ny):
        table = jnp.concatenate(
            [com[i * z.RC + z.OY + t * z.lines : i * z.RC + z.OY + (t + 1) * z.lines, :] for i in range(z.n)], axis=0
        )
        for h in range(z.m):
            for f, line in ((2, 2 * gy + 1), (3, 2 * (gy + 2))):
                y_rows[t, h, f] = select_dot(onehot(((gz + 1) * z.m + h) * z.lines + line, z.n * z.lines), table)
    for v in range(5):
        swapped = []
        for a in range(z.xa):
            T = lat[(v * z.xa + a) * S : (v * z.xa + a + 1) * S, :]
            T = jnp.where(even, pltpu.roll(T, LANES - f_of, 1), pltpu.roll(T, f_of, 1))
            swapped.append(jnp.concatenate([jnp.where(kind == k, T, 0.0) for k in range(4)], axis=0))
        near = select_dot(picks, jnp.concatenate(swapped, axis=1))
        for x in range(z.xc):
            k = v * z.xc + x
            at = slice(k * LANES, (k + 1) * LANES)
            c = jnp.where(kind == 0, lanes_at(low_rows[:, at], y_index), lanes_at(top_rows[:, at], y_index))
            start = k * z.R
            for f in (2, 3):
                for h in range(z.m):
                    got = lanes_at(y_rows[start // LANES, h, f], start % LANES + half % z.R)
                    c = jnp.where((kind == f) & (half // z.R == h), got, c)
            for a in (2 * x, 2 * x + 1):
                ghost[(v * z.xa + a) * S : (v * z.xa + a + 1) * S, :] = jnp.where(
                    here > 0.0, near[:, a * LANES : (a + 1) * LANES], c
                )

    is_z = kind < 2
    sign = jnp.where(even, 0.5 * fine_rate, -0.5 * fine_rate)
    for a in range(z.xa):
        at = [slice((v * z.xa + a) * S, (v * z.xa + a + 1) * S) for v in range(5)]
        own = [lat[s, :] for s in at]
        far = [ghost[s, :] for s in at]
        L = [jnp.where(even, far[v], own[v]) for v in range(5)]
        R = [jnp.where(even, own[v], far[v]) for v in range(5)]
        vl, pl_, cl = derived(L)
        vr, pr, cr = derived(R)
        sl = jnp.where(is_z, vl[2], vl[1])
        sr = jnp.where(is_z, vr[2], vr[1])
        F = twice_flux(L, (sl, pl_, cl), R, (sr, pr, cr), None)
        both = pl_ + pr
        F[2] = F[2] + jnp.where(is_z, 0.0, both)
        F[3] = F[3] + jnp.where(is_z, both, 0.0)
        for v in range(5):
            C = sign * F[v]
            ghost[at[v], :] = C
            for d in range(z.n):
                k = d * z.RF + (v * z.xa + a) * z.own
                outf[k : k + z.own, :] = C[d * z.own : (d + 1) * z.own]

    zrow = lax.broadcasted_iota(jnp.int32, (z.NZ, S), 0)
    base = z.H * (gzr + 1)
    zmat = jnp.concatenate(
        [
            (zrow == base).astype(jnp.float32) - absent_row[0] * (zrow == base - 1).astype(jnp.float32),
            (zrow == base + z.H - 1).astype(jnp.float32) - absent_row[1] * (zrow == base + z.H).astype(jnp.float32),
        ],
        axis=1,
    ).astype(jnp.bfloat16)
    ybase = z.H * (gy + 1)
    absent = [1.0 - jnp.sum(flags[k], axis=1, keepdims=True) for k in (2, 3)]
    ymat = jnp.concatenate(
        [
            (lane == ybase).astype(jnp.float32) - absent[0] * (lane == ybase - 1).astype(jnp.float32),
            (lane == ybase + z.H - 1).astype(jnp.float32) - absent[1] * (lane == ybase + z.H).astype(jnp.float32),
        ],
        axis=0,
    ).astype(jnp.bfloat16)
    in_y = lane // z.H == gy + 1
    in_z = lane // z.H == gz + 1
    for v in range(5):
        for x in range(z.xc):
            k = v * z.xc + x
            r = (v * z.xa + 2 * x) * S
            Q = ghost[r : r + S, :] + ghost[r + S : r + 2 * S, :]
            Q = 0.125 * (Q + pltpu.roll(Q, LANES - 1, 1))
            got = [lanes_at(Q, f_of * f + 2 * (lane % z.H)) for f in range(4)]
            zq = jnp.concatenate([jnp.where(in_y, got[f], 0.0) for f in (0, 1)], axis=0)
            yq = jnp.concatenate([jnp.where(in_z, got[f], 0.0) for f in (2, 3)], axis=0)
            total = select_dot(zmat, zq, 2)
            for piece in parts(yq.T, 2):
                total = total + jnp.dot(piece, ymat, preferred_element_type=jnp.float32)
            canvas[k * z.NZ : (k + 1) * z.NZ, :] = total

    spot = lax.broadcasted_iota(jnp.int32, (z.H, LANES), 1) // z.H

    def place(k, carry):
        i = k // z.own
        q = k % z.own
        sy = spots[0, k] + 1
        sz = spots[1, k] + 1
        inside = spot == sy
        for v in range(5):
            block = avg[pl.ds(pl.multiple_of(i * z.RA + v * z.H, 8), z.H), :]
            for x in range(z.xc):
                shift = lax.rem(z.H * (sy - (x * z.own + q)) + 2 * LANES, LANES)
                rows = pl.ds(pl.multiple_of((v * z.xc + x) * z.NZ + z.H * sz, z.H), z.H)
                canvas[rows, :] = canvas[rows, :] + jnp.where(inside, pltpu.roll(block, shift, 1), 0.0)
        return carry

    lax.fori_loop(0, S, place, 0)
    for d in range(z.n):
        for k in range(vx):
            outc[d * z.RK + k * z.R : d * z.RK + (k + 1) * z.R, :] = canvas[k * z.NZ + d * z.R : k * z.NZ + (d + 1) * z.R, :]

    tables = ((xo, 0), (xo, 5), (xb, 5), (xu, 0))
    for w, (source, offset) in enumerate(tables):
        for i in range(z.n):
            for v in range(5):
                k = (w * 5 + v) * S + i * z.own
                r = i * z.RX + (offset + v) * z.own
                xs[k : k + z.own, :] = source[r : r + z.own, :]
    value = number.astype(jnp.float32)
    zb = (
        lax.broadcasted_iota(jnp.int32, (z.n, S), 0) // z.m == gzr + 1
    ).astype(jnp.bfloat16)
    for side, (margin, edge) in enumerate(((below, slab == 0), (above, slab == z.slabs - 1))):
        match = (value == margin[5 * z.R : 5 * z.R + 1, :S]).astype(jnp.bfloat16)
        own = [xs[(side * 5 + v) * S : (side * 5 + v + 1) * S, :] for v in range(5)]
        far = select_dot(
            match, jnp.concatenate([xs[((2 + side) * 5 + v) * S : ((2 + side) * 5 + v + 1) * S, :] for v in range(5)], axis=1)
        )
        far = [jnp.where(edge, own[v], far[:, v * LANES : (v + 1) * LANES]) for v in range(5)]
        F = state_flux(far, own, 0) if side == 0 else state_flux(own, far, 0)
        for v in range(5):
            C = (0.5 * fine_rate if side == 0 else -0.5 * fine_rate) * F[v]
            for d in range(z.n):
                k = d * z.RF + z.OFX + (side * 5 + v) * z.own
                outf[k : k + z.own, :] = C[d * z.own : (d + 1) * z.own]
            Q = C + pltpu.roll(C, LANES - 1, 1)
            Q = 0.125 * (Q + pltpu.roll(Q, LANES - z.P, 1))
            for h in range(z.zcl):
                got = jnp.where(in_y, lanes_at(Q, 2 * z.P * h + 2 * (lane % z.H)), 0.0)
                outc[pl.ds(z.OXQ + (v * 2 + side) * z.zcl + h, z.n, stride=z.RK), :] = select_dot(zb, got, 2)


def fine_kernel(z, updated, recv, out, scr):
    lane = lax.broadcasted_iota(jnp.int32, (z.P, LANES), 1)
    y = lane % z.P
    edge = (y == 0) | (y == z.P - 1)
    pick = jnp.where(y == 0, 2 * z.P, 3 * z.P) + lane // z.P
    for v in range(5):
        for q in range(z.own):
            for a in range(z.xa):
                scr[q % 2, pl.ds(a, z.n, stride=z.xa), :] = recv[pl.ds((v * z.xa + a) * z.own + q, z.n, stride=z.RF), :]
            face = scr[q % 2]
            for g in range(z.G):
                at = slice(g * LANES, (g + 1) * LANES)
                add = jnp.where(edge, lanes_at(face, jnp.where(edge, pick + z.zg * g, 0)), 0.0)
                if g == 0:
                    add = add + jnp.where(lane < z.P, face, 0.0)
                if g == z.G - 1:
                    add = add + jnp.where(lane >= LANES - z.P, pltpu.roll(face, 2 * z.P, 1), 0.0)
                out[v, q, :, at] = updated[v, q, :, at] + add
            for side in range(2):
                x = side * (z.P - 1)
                for j in range(z.n):
                    r = j * z.RF + z.OFX + (side * 5 + v) * z.own + q
                    at = slice(j * z.PL, (j + 1) * z.PL)
                    out[v, q, x : x + 1, at] = out[v, q, x : x + 1, at] + recv[r : r + 1, : z.PL]


def coarse_kernel(z, info, prov, recv, out):
    for j in range(z.n):
        for v in range(5):
            for x in range(z.xc):
                r = j * z.RK + (v * z.xc + x) * z.R
                out[v, j * z.xc + x] = prov[v, j * z.xc + x] + recv[r : r + z.R, :]
    offset = 0 if z.m == 1 else lax.rem(info[1], z.m) * z.R
    for v in range(5):
        for side in range(2):
            x = side * (z.NX - 1)
            for zl in range(z.R):
                zc = zl + offset
                r = (zc // z.zcl) * z.RK + z.OXQ + (v * 2 + side) * z.zcl + zc % z.zcl
                out[v, x, zl : zl + 1, :] = out[v, x, zl : zl + 1, :] + recv[pl.ds(r, 1), :]


def call(kernel, z, outs, ins, scratch=(), aliases=None, name=None):
    return pl.pallas_call(
        functools.partial(kernel, z),
        out_shape=[jax.ShapeDtypeStruct(s, jnp.float32) for s in outs],
        in_specs=[SMEM if space == "s" else VMEM for space, _ in ins],
        out_specs=[VMEM] * len(outs),
        scratch_shapes=[pltpu.VMEM(s, jnp.float32) for s in scratch],
        input_output_aliases=aliases or {},
        compiler_params=pltpu.CompilerParams(vmem_limit_bytes=56 * 1024 * 1024),
        name=name,
    )(*[a for _, a in ins])


def local(n, slabs, coarse, fine, columns, patch_ids):
    numbers = patch_ids[0]
    slots = numbers.shape[0]
    assert columns.shape[0] == slots
    z = Sizes(n, slabs, fine.shape, coarse.shape, slots)
    info = jnp.stack([lax.axis_index("slab"), lax.axis_index("patch")]).astype(jnp.int32)
    held = numbers[:, None] == jnp.arange(slots, dtype=jnp.int32)[None, :]
    spots = jnp.sum(jnp.where(held[None], columns.T[:, None, :], 0), axis=2).astype(jnp.int32)
    rtab = jnp.concatenate([spots, numbers[None]], axis=0)
    ctab = rtab.T
    number_row = jnp.pad(numbers.astype(jnp.float32), (0, LANES - slots))[None]

    exchange = lambda a: lax.all_to_all(a, "patch", 0, 0, tiled=True)
    ahead = lambda count: [(i, i + 1) for i in range(count - 1)]
    back = lambda count: [(i + 1, i) for i in range(count - 1)]

    com, xf, up, dn, pu, pd = call(
        extract_kernel,
        z,
        [(n * z.RC, LANES), (n * z.RX, LANES), (z.RM, LANES), (z.RM, LANES), (5 * z.NX, LANES), (5 * z.NX, LANES)],
        [("v", fine), ("v", coarse), ("v", number_row)],
        [(2, z.P, LANES)],
        name="extract",
    )
    xo = exchange(xf)
    below = lax.ppermute(up, "slab", ahead(slabs))
    above = lax.ppermute(dn, "slab", back(slabs))
    lower = lax.ppermute(pu, "patch", ahead(n))
    upper = lax.ppermute(pd, "patch", back(n))
    xb = lax.ppermute(xo, "slab", ahead(slabs))
    xu = lax.ppermute(xo, "slab", back(slabs))
    com = exchange(com)
    updated, avg = call(
        advance_kernel,
        z,
        [fine.shape, (n * z.RA, LANES)],
        [("v", fine)],
        [fine.shape, (5, z.P, LANES), (5 * z.own * z.G * z.P, LANES)],
        name="advance",
    )
    avg = exchange(avg)
    (prov,) = call(
        provisional_kernel,
        z,
        [coarse.shape],
        [("s", info), ("s", columns), ("v", coarse), ("v", below), ("v", above), ("v", lower), ("v", upper)],
        [(5, z.NX + 2, z.R, LANES)],
        name="provisional",
    )
    outf, outc = call(
        middle_kernel,
        z,
        [(n * z.RF, LANES), (n * z.RK, LANES)],
        [("s", info), ("s", spots), ("v", ctab), ("v", rtab)]
        + [("v", a) for a in (com, xo, xb, xu, below, above, avg)],
        [(5 * z.xa * slots, LANES), (5 * z.xa * slots, LANES), (20 * slots, LANES), (5 * z.xc * z.NZ, LANES)],
        name="middle",
    )
    outf = exchange(outf)
    outc = exchange(outc)
    (fine_out,) = call(
        fine_kernel, z, [fine.shape], [("v", updated), ("v", outf)], [(2, z.P, LANES)], {0: 0}, name="fine_edges"
    )
    (coarse_out,) = call(
        coarse_kernel, z, [coarse.shape], [("s", info), ("v", prov), ("v", outc)], name="coarse_sum"
    )
    return coarse_out, fine_out


def solution(mesh):
    n, slabs = mesh.shape["patch"], mesh.shape["slab"]
    return jax.shard_map(
        functools.partial(local, n, slabs),
        mesh=mesh,
        in_specs=(
            P(None, "slab", "patch", None),
            P(None, ("slab", "patch"), None, None),
            P(),
            P("slab", None),
        ),
        out_specs=(P(None, "slab", "patch", None), P(None, ("slab", "patch"), None, None)),
        check_vma=False,
    )
```

time: 1060 us -> 141 us (0.13)
  local copies, waits for them, and re-layouts: 560 us -> 4.83 us
  waiting for transfers between devices: 253 us -> 15.6 us
  other arithmetic: 155 us -> 2.03 us
  Pallas kernels: 0 us -> 52.2 us
  matrix products: 47.3 us -> 0 us
  blocking collectives: 0 us -> 29.9 us
  starting transfers between devices: 17.3 us -> 34.4 us
  between operations: 15.5 us -> 0.8 us
    all_gather x2 -> x0, waiting for transfers between devices: 143 us -> none  [the longest x1 143 us: local(): slab_faces = lax.all_gather(own_faces, 'patch', axis=2, tiled=True)]
    reshape x23 -> x0, local copies, waits for them, and re-layouts: 121 us -> none  [the longest x2 53.2 us: block_form(): slab.reshape(5, layer_depth, H, GZ + 2, H, GY + 2, H)]
    unnamed x179 -> x33, local copies, waits for them, and re-layouts: 124 us -> 3.63 us
    slice x22 -> x0, local copies, waits for them, and re-layouts: 119 us -> none  [the longest x1 56.7 us: coarse_faces(): blocks[:, :, :, :, H - 1]]
    reduce_scatter x1 -> x0, waiting for transfers between devices: 81.5 us -> none  [local(): contrib = lax.psum_scatter(placed, 'patch', scatter_dimension=2, tiled=True)]
    reduce_sum x20 -> x1, other arithmetic: 70.1 us -> 0.11 us  [local(): jnp.sum(jnp.where(held[None], columns.T[:, None, :], 0), axis=2)]
    pallas_call x0 -> x6, Pallas kernels: none -> 52.2 us  [call(): pl.pallas_call(functools.partial(kernel, z), out_shape=[jax.ShapeDtypeStr...]
    dot_general x9 -> x0, matrix products: 47.3 us -> none  [the longest x1 23.2 us: coarse_terms(): jnp.einsum('nl,nb,vnxzy->vlxzyb', layer_pick, onehot(centre, nblocks), av...]
  transfers between devices with their start and end apart: 9 -> 9, of which waited for: 5 -> 2; matrix products, arithmetic and copies ran while one was open for 13% -> 2% of each run, Pallas kernels for 0% -> 27%
where the time goes in v1:
time: 141 us; the launch traced here: 140 us
  Pallas kernels  52.2 us (37%)
  starting transfers between devices  34.4 us (24%)
  blocking collectives  29.9 us (21%)
  waiting for transfers between devices  15.6 us (11%)
  local copies, waits for them, and re-layouts  4.83 us (3%)
  other arithmetic  2.03 us (1%)
    pallas_call x6, Pallas kernels, call(): pl.pallas_call(functools.partial(kernel, z), out_shape=[jax.ShapeDtypeStr...  52.2 us
    all_to_all x2, blocking collectives, local(): exchange = lambda a: lax.all_to_all(a, 'patch', 0, 0, tiled=True)  29.9 us
    all_to_all x3, starting transfers between devices, local(): exchange = lambda a: lax.all_to_all(a, 'patch', 0, 0, tiled=True)  15.5 us
    ppermute x1, waiting for transfers between devices, local(): lower = lax.ppermute(pu, 'patch', ahead(n))  12.7 us
    ppermute x1, starting transfers between devices, local(): below = lax.ppermute(up, 'slab', ahead(slabs))  5.19 us
    ppermute x1, starting transfers between devices, local(): xb = lax.ppermute(xo, 'slab', ahead(slabs))  3.64 us
    unnamed x33, local copies, waits for them, and re-layouts  3.63 us
    ppermute x1, starting transfers between devices, local(): lower = lax.ppermute(pu, 'patch', ahead(n))  3.09 us
  transfers between devices with their start and end apart: 9, of which 2 were waited for; matrix products, arithmetic and copies ran while one was open for 2% of the time, Pallas kernels for 27%

profile of v1, /device:TPU:17, one launch (start us, length us, event | category | flops | bytes accessed | tf_op | source)
XLA Modules:
  0.0 139.7 jit_solution(6331044016550341853)
XLA Ops:
  0.6 0.7 bitcast_convert_fusion
  1.3 0.5 pad_bitcast_fusion.number_row
  1.8 3.8 %extract.1 = (f32[1088,128]{1,0:T(8,128)}, f32[320,128]{1,0:T(8,128)}, f32[88,128]{1,0:T(8,128)}, f32[88,128]{1,0:T(8,128)}, f32[80,128]{1,0:T(8,128)}, /*index=5*/f32[80,128]{1,0:T(8,128)}) custom-call(f32[5,4,32,1024]{3,2,1,0:T(8,128)} %fine.3, f32[5,16,16,128]{3,2,1,0:T(8,128)} %coarse.3, f32[1,128]{1,0:T(1,128)} %pad_bitcast_fusion.number_row), custom_call_target="tpu_custom_call" | custom-call | tf_op jit(solution)/shard_map/extract/pallas_call | solution.py:501
  5.6 5.7 %all-to-all-start.1 = ((f32[8,40,128]{2,1,0:T(8,128)}), f32[8,40,128]{2,1,0:T(8,128)S(1)}, u32[]{:S(2)}, u32[]{:S(2)}) async-start(f32[8,40,128]{2,1,0:T(8,128)} %bitcast.29), calls=%async_computation.1 | async-start | bytes 327680 | tf_op jit(solution)/shard_map/all_to_all | solution.py:525
  11.3 26.6 %advance.1 = (f32[5,4,32,1024]{3,2,1,0:T(8,128)}, f32[640,128]{1,0:T(8,128)}) custom-call(f32[5,4,32,1024]{3,2,1,0:T(8,128)} %fine.3), custom_call_target="tpu_custom_call" | custom-call | tf_op jit(solution)/shard_map/advance/pallas_call | solution.py:501
  38.0 14.3 %all_to_all.55 = f32[8,80,128]{2,1,0:T(8,128)} all-to-all(f32[8,80,128]{2,1,0:T(8,128)} %bitcast.28), channel_id=1, replica_groups=mesh['slab'=4,'patch'=8] {'patch'}, dimensions={0} | all-to-all | bytes 655360 | tf_op jit(solution)/shard_map/all_to_all | solution.py:525
  52.3 4.8 %all-to-all-start = ((f32[8,136,128]{2,1,0:T(8,128)}), f32[8,136,128]{2,1,0:T(8,128)S(1)}, u32[]{:S(2)}, u32[]{:S(2)}) async-start(f32[8,136,128]{2,1,0:T(8,128)} %bitcast.6), calls=%async_computation | async-start | bytes 1114112 | tf_op jit(solution)/shard_map/all_to_all | solution.py:525
  57.1 5.2 %collective-permute-start = (f32[88,128]{1,0:T(8,128)S(1)}, f32[88,128]{1,0:T(8,128)S(1)}, u32[]{:S(2)}, u32[]{:S(2)}) collective-permute-start(f32[88,128]{1,0:T(8,128)S(1)} %copy-done.13), channel_id=1, source_target_pairs={{0,8},{8,16},{16,24},{1,9},{9,17},{17,25},{2,10},{10,18},{18,26},{... | collective-permute-start | bytes 135176 | tf_op jit(solution)/shard_map/ppermute | solution.py:538
  62.3 1.9 %collective-permute-start.1 = (f32[88,128]{1,0:T(8,128)S(1)}, f32[88,128]{1,0:T(8,128)S(1)}, u32[]{:S(2)}, u32[]{:S(2)}) collective-permute-start(f32[88,128]{1,0:T(8,128)S(1)} %copy-done.12), channel_id=1, source_target_pairs={{8,0},{16,8},{24,16},{9,1},{17,9},{25,17},{10,2},{18,10},{26,18},{... | collective-permute-start | bytes 135176 | tf_op jit(solution)/shard_map/ppermute | solution.py:539
  64.3 0.1 iota_compare_fusion
  64.4 0.1 select_reduce_fusion.spots
  64.5 3.6 %collective-permute-start.4 = (f32[320,128]{1,0:T(8,128)S(1)}, f32[320,128]{1,0:T(8,128)S(1)}, u32[]{:S(2)}, u32[]{:S(2)}) collective-permute-start(f32[320,128]{1,0:T(8,128)S(1)} %bitcast.24), channel_id=1, source_target_pairs={{0,8},{8,16},{16,24},{1,9},{9,17},{17,25},{2,10},{10,18},{18,26},{... | collective-permute-start | bytes 491528 | tf_op jit(solution)/shard_map/ppermute | solution.py:542
  68.1 1.9 %collective-permute-start.5 = (f32[320,128]{1,0:T(8,128)S(1)}, f32[320,128]{1,0:T(8,128)S(1)}, u32[]{:S(2)}, u32[]{:S(2)}) collective-permute-start(f32[320,128]{1,0:T(8,128)S(1)} %bitcast.25), channel_id=1, source_target_pairs={{8,0},{16,8},{24,16},{9,1},{17,9},{25,17},{10,2},{18,10},{26,18},{... | collective-permute-start | bytes 491528 | tf_op jit(solution)/shard_map/ppermute | solution.py:543
  70.1 0.6 pad_add_fusion
  70.7 0.6 pad_add_fusion.1.info
  71.2 0.7 copy.10.ctab
  72.0 2.8 %collective-permute-done.5.xu = f32[320,128]{1,0:T(8,128)S(1)} collective-permute-done((f32[320,128]{1,0:T(8,128)S(1)}, f32[320,128]{1,0:T(8,128)S(1)}, u32[]{:S(2)}, u32[]{:S(2)}) %collective-permute-start.5) | collective-permute-done | bytes 163872 | tf_op jit(solution)/shard_map/ppermute | solution.py:543
  74.8 0.6 copy-done.6
  75.4 0.2 copy-done.1
  75.6 8.7 %middle.1 = (f32[960,128]{1,0:T(8,128)}, f32[1472,128]{1,0:T(8,128)}) custom-call(s32[2]{0:T(128)} %pad_add_fusion.1.info, s32[2,32]{1,0:T(2,128)} %copy-done.9, s32[32,3]{1,0:T(8,128)} %copy.10.ctab, s32[3,32]{1,0:T(4,128)} %get-tuple-element.22.rtab, f32[1088,128]{1,0:T(8,128)} %bitcast.20, f32[320,128]{1,0:T(8,128)} %bitcast.26, f32[320,128]{1,0:T(8,128)} %copy-done.5, ...), custom_call_target="tpu_custom_call" | custom-call | tf_op jit(solution)/shard_map/middle/pallas_call | solution.py:501
  84.3 15.6 %all_to_all.56 = f32[8,120,128]{2,1,0:T(8,128)} all-to-all(f32[8,120,128]{2,1,0:T(8,128)} %bitcast.27), channel_id=1, replica_groups=mesh['slab'=4,'patch'=8] {'patch'}, dimensions={0} | all-to-all | bytes 983040 | tf_op jit(solution)/shard_map/all_to_all | solution.py:525
  99.9 5.0 %all-to-all-start.3 = ((f32[8,184,128]{2,1,0:T(8,128)}), f32[8,184,128]{2,1,0:T(8,128)S(1)}, u32[]{:S(2)}, u32[]{:S(2)}) async-start(f32[8,184,128]{2,1,0:T(8,128)} %bitcast.23), calls=%async_computation.3 | async-start | bytes 1507328 | tf_op jit(solution)/shard_map/all_to_all | solution.py:525
  104.9 3.1 %collective-permute-start.2 = (f32[80,128]{1,0:T(8,128)S(1)}, f32[80,128]{1,0:T(8,128)S(1)}, u32[]{:S(2)}, u32[]{:S(2)}) collective-permute-start(f32[80,128]{1,0:T(8,128)S(1)} %copy-done.15), channel_id=1, source_target_pairs={{0,1},{1,2},{2,3},{3,4},{4,5},{5,6},{6,7},{8,9},{9,10},{10,11},{11... | collective-permute-start | bytes 122888 | tf_op jit(solution)/shard_map/ppermute | solution.py:540
  108.0 3.1 %collective-permute-start.3 = (f32[80,128]{1,0:T(8,128)S(1)}, f32[80,128]{1,0:T(8,128)S(1)}, u32[]{:S(2)}, u32[]{:S(2)}) collective-permute-start(f32[80,128]{1,0:T(8,128)S(1)} %copy-done.14), channel_id=1, source_target_pairs={{1,0},{2,1},{3,2},{4,3},{5,4},{6,5},{7,6},{9,8},{10,9},{11,10},{12... | collective-permute-start | bytes 122888 | tf_op jit(solution)/shard_map/ppermute | solution.py:541
  111.1 0.7 copy.9.columns
  111.8 12.7 %collective-permute-done.2.lower = f32[80,128]{1,0:T(8,128)S(1)} collective-permute-done((f32[80,128]{1,0:T(8,128)S(1)}, f32[80,128]{1,0:T(8,128)S(1)}, u32[]{:S(2)}, u32[]{:S(2)}) %collective-permute-start.2) | collective-permute-done | bytes 40992 | tf_op jit(solution)/shard_map/ppermute | solution.py:540
  124.5 0.6 copy-done.7
  125.2 0.6 copy-done.8
  125.8 5.8 %provisional.1.prov = f32[5,16,16,128]{3,2,1,0:T(8,128)} custom-call(s32[2]{0:T(128)} %pad_add_fusion.1.info, s32[32,2]{1,0:T(8,128)} %copy.9.columns, f32[5,16,16,128]{3,2,1,0:T(8,128)} %coarse.3, f32[88,128]{1,0:T(8,128)} %copy-done.3, f32[88,128]{1,0:T(8,128)} %copy-done.4, f32[80,128]{1,0:T(8,128)} %copy-done.7, f32[80,128]{1,0:T(8,128)} %copy-done.8), custom_call_target="tpu_custom_call" | custom-call | tf_op jit(solution)/shard_map/provisional/pallas_call | solution.py:501
  131.6 5.0 %fine_edges.1 = f32[5,4,32,1024]{3,2,1,0:T(8,128)} custom-call(f32[5,4,32,1024]{3,2,1,0:T(8,128)} %get-tuple-element.20.updated, f32[960,128]{1,0:T(8,128)} %bitcast.21), custom_call_target="tpu_custom_call", output_to_operand_aliasing={{}: (0, {})} | custom-call | tf_op jit(solution)/shard_map/fine_edges/pallas_call | solution.py:501
  136.5 0.9 copy-done
  137.4 2.3 %coarse_sum.1 = f32[5,16,16,128]{3,2,1,0:T(8,128)} custom-call(s32[2]{0:T(128)} %pad_add_fusion.1.info, f32[5,16,16,128]{3,2,1,0:T(8,128)} %provisional.1.prov, f32[1472,128]{1,0:T(8,128)} %bitcast.19), custom_call_target="tpu_custom_call" | custom-call | tf_op jit(solution)/shard_map/coarse_sum/pallas_call | solution.py:501
  (34 shorter events, 0.1 us)
Async XLA Ops:
  5.6 51.5 %copy-start.13 = (f32[88,128]{1,0:T(8,128)S(1)}, f32[88,128]{1,0:T(8,128)}, u32[]{:S(2)}) copy-start(f32[88,128]{1,0:T(8,128)} %get-tuple-element.12) | copy-start | bytes 135172
  5.6 56.7 %copy-start.12 = (f32[88,128]{1,0:T(8,128)S(1)}, f32[88,128]{1,0:T(8,128)}, u32[]{:S(2)}) copy-start(f32[88,128]{1,0:T(8,128)} %get-tuple-element.13) | copy-start | bytes 135172
  5.6 58.7 %copy-start.11 = (s32[1,32]{1,0:T(1,128)S(1)}, s32[1,32]{1,0:T(1,128)}, u32[]{:S(2)}) copy-start(s32[1,32]{1,0:T(1,128)} %param.7) | copy-start | bytes 388
  5.6 58.8 %copy-start.10 = (s32[32,2]{0,1:T(2,128)S(1)}, s32[32,2]{0,1:T(2,128)}, u32[]{:S(2)}) copy-start(s32[32,2]{0,1:T(2,128)} %param.6) | copy-start | bytes 772
  5.6 32.4 %all-to-all-start.1 = ((f32[8,40,128]{2,1,0:T(8,128)}), f32[8,40,128]{2,1,0:T(8,128)S(1)}, u32[]{:S(2)}, u32[]{:S(2)}) async-start(f32[8,40,128]{2,1,0:T(8,128)} %bitcast.29), calls=%async_computation.1 | async-start | bytes 327680 | tf_op jit(solution)/shard_map/all_to_all | solution.py:525
  38.0 36.8 %copy-start.2 = (f32[8,40,128]{2,1,0:T(8,128)}, f32[8,40,128]{2,1,0:T(8,128)S(1)}, u32[]{:S(2)}) copy-start(f32[8,40,128]{2,1,0:T(8,128)S(1)} %all-to-all-done.1) | copy-start | bytes 491524
  52.3 52.6 %copy-start.15 = (f32[80,128]{1,0:T(8,128)S(1)}, f32[80,128]{1,0:T(8,128)}, u32[]{:S(2)}) copy-start(f32[80,128]{1,0:T(8,128)} %get-tuple-element.14) | copy-start | bytes 122884
  52.3 55.7 %copy-start.14 = (f32[80,128]{1,0:T(8,128)S(1)}, f32[80,128]{1,0:T(8,128)}, u32[]{:S(2)}) copy-start(f32[80,128]{1,0:T(8,128)} %get-tuple-element.15) | copy-start | bytes 122884
  52.3 22.5 %all-to-all-start = ((f32[8,136,128]{2,1,0:T(8,128)}), f32[8,136,128]{2,1,0:T(8,128)S(1)}, u32[]{:S(2)}, u32[]{:S(2)}) async-start(f32[8,136,128]{2,1,0:T(8,128)} %bitcast.6), calls=%async_computation | async-start | bytes 1114112 | tf_op jit(solution)/shard_map/all_to_all | solution.py:525
  57.1 14.8 %collective-permute-start = (f32[88,128]{1,0:T(8,128)S(1)}, f32[88,128]{1,0:T(8,128)S(1)}, u32[]{:S(2)}, u32[]{:S(2)}) collective-permute-start(f32[88,128]{1,0:T(8,128)S(1)} %copy-done.13), channel_id=1, source_target_pairs={{0,8},{8,16},{16,24},{1,9},{9,17},{17,25},{2,10},{10,18},{18,26},{... | collective-permute-start | bytes 135176 | tf_op jit(solution)/shard_map/ppermute | solution.py:538
  62.3 9.6 %collective-permute-start.1 = (f32[88,128]{1,0:T(8,128)S(1)}, f32[88,128]{1,0:T(8,128)S(1)}, u32[]{:S(2)}, u32[]{:S(2)}) collective-permute-start(f32[88,128]{1,0:T(8,128)S(1)} %copy-done.12), channel_id=1, source_target_pairs={{8,0},{16,8},{24,16},{9,1},{17,9},{25,17},{10,2},{18,10},{26,18},{... | collective-permute-start | bytes 135176 | tf_op jit(solution)/shard_map/ppermute | solution.py:539
  64.5 10.3 %copy-start.9 = (s32[2,32]{1,0:T(2,128)}, s32[2,32]{1,0:T(2,128)S(1)}, u32[]{:S(2)}) copy-start(s32[2,32]{1,0:T(2,128)S(1)} %select_reduce_fusion.spots) | copy-start | bytes 772
  64.5 7.5 %collective-permute-start.4 = (f32[320,128]{1,0:T(8,128)S(1)}, f32[320,128]{1,0:T(8,128)S(1)}, u32[]{:S(2)}, u32[]{:S(2)}) collective-permute-start(f32[320,128]{1,0:T(8,128)S(1)} %bitcast.24), channel_id=1, source_target_pairs={{0,8},{8,16},{16,24},{1,9},{9,17},{17,25},{2,10},{10,18},{18,26},{... | collective-permute-start | bytes 491528 | tf_op jit(solution)/shard_map/ppermute | solution.py:542
  68.1 6.6 %collective-permute-start.5 = (f32[320,128]{1,0:T(8,128)S(1)}, f32[320,128]{1,0:T(8,128)S(1)}, u32[]{:S(2)}, u32[]{:S(2)}) collective-permute-start(f32[320,128]{1,0:T(8,128)S(1)} %bitcast.25), channel_id=1, source_target_pairs={{8,0},{16,8},{24,16},{9,1},{17,9},{25,17},{10,2},{18,10},{26,18},{... | collective-permute-start | bytes 491528 | tf_op jit(solution)/shard_map/ppermute | solution.py:543
  71.9 2.9 %copy-start.3 = (f32[88,128]{1,0:T(8,128)}, f32[88,128]{1,0:T(8,128)S(1)}, u32[]{:S(2)}) copy-start(f32[88,128]{1,0:T(8,128)S(1)} %collective-permute-done.below) | copy-start | bytes 135172
  71.9 2.9 %copy-start.4 = (f32[88,128]{1,0:T(8,128)}, f32[88,128]{1,0:T(8,128)S(1)}, u32[]{:S(2)}) copy-start(f32[88,128]{1,0:T(8,128)S(1)} %collective-permute-done.1.above) | copy-start | bytes 135172
  72.0 2.8 %copy-start.5 = (f32[320,128]{1,0:T(8,128)}, f32[320,128]{1,0:T(8,128)S(1)}, u32[]{:S(2)}) copy-start(f32[320,128]{1,0:T(8,128)S(1)} %collective-permute-done.4.xb) | copy-start | bytes 491524
  74.8 0.7 copy-start.6
  74.8 0.9 copy-start.1
  99.9 36.6 %all-to-all-start.3 = ((f32[8,184,128]{2,1,0:T(8,128)}), f32[8,184,128]{2,1,0:T(8,128)S(1)}, u32[]{:S(2)}, u32[]{:S(2)}) async-start(f32[8,184,128]{2,1,0:T(8,128)} %bitcast.23), calls=%async_computation.3 | async-start | bytes 1507328 | tf_op jit(solution)/shard_map/all_to_all | solution.py:525
  104.9 19.6 %collective-permute-start.2 = (f32[80,128]{1,0:T(8,128)S(1)}, f32[80,128]{1,0:T(8,128)S(1)}, u32[]{:S(2)}, u32[]{:S(2)}) collective-permute-start(f32[80,128]{1,0:T(8,128)S(1)} %copy-done.15), channel_id=1, source_target_pairs={{0,1},{1,2},{2,3},{3,4},{4,5},{5,6},{6,7},{8,9},{9,10},{10,11},{11... | collective-permute-start | bytes 122888 | tf_op jit(solution)/shard_map/ppermute | solution.py:540
  108.0 16.5 %collective-permute-start.3 = (f32[80,128]{1,0:T(8,128)S(1)}, f32[80,128]{1,0:T(8,128)S(1)}, u32[]{:S(2)}, u32[]{:S(2)}) collective-permute-start(f32[80,128]{1,0:T(8,128)S(1)} %copy-done.14), channel_id=1, source_target_pairs={{1,0},{2,1},{3,2},{4,3},{5,4},{6,5},{7,6},{9,8},{10,9},{11,10},{12... | collective-permute-start | bytes 122888 | tf_op jit(solution)/shard_map/ppermute | solution.py:541
  124.5 0.6 copy-start.7
  125.2 0.6 copy-start.8
  136.5 0.9 copy-start

commit v2 on v1

--- a/solution.py
+++ b/solution.py
@@ -7,7 +7,9 @@
 from jax.experimental.pallas import tpu as pltpu
 from jax.sharding import PartitionSpec as P
 
+
 LANES = 128
+XROWS = 16
 heat_ratio = 1.4
 fine_rate = 0.1
 coarse_rate = 0.05
@@ -42,14 +44,16 @@
         self.ny = -(-(5 * self.xc * self.R) // LANES)
         self.OY = up8(self.lat)
         self.OZ = self.OY + self.lines * self.ny
-        self.RC = up8(self.OZ + 10 * self.xc)
-        self.RX = up8(10 * self.own)
+        self.OX = self.OZ + 10 * self.xc
+        self.RC = up8(self.OX + 10 * self.own)
+        self.OM = up8(n * 5 * self.own)
         self.RA = 5 * self.H
         self.OFX = self.lat
         self.RF = up8(self.lat + 10 * self.own)
         self.OXQ = 5 * self.xc * self.R
         self.RK = up8(self.OXQ + 10 * self.zcl)
         self.RM = 5 * self.R + 8
+        self.RP = self.OM + self.RM
 
 
 def parts(x, count):
@@ -102,7 +106,19 @@
     return twice_flux(L, (vl[d], pl_, cl), R, (vr[d], pr, cr), d)
 
 
-def extract_kernel(z, fine, coarse, number_row, com, xf, up, dn, pu, pd, scr):
+def positions(z, ids, columns):
+    down = lax.broadcasted_iota(jnp.int32, (z.S, z.S), 0)
+    across = lax.broadcasted_iota(jnp.int32, (z.S, z.S), 1)
+    number_row = ids[...].astype(jnp.float32)
+    held = down.astype(jnp.float32) == number_row
+    place = columns[...].astype(jnp.float32)
+    rows = [jnp.sum(jnp.where(held, place[:, k : k + 1], 0.0), axis=0, keepdims=True) for k in range(2)]
+    turn = lambda r: jnp.sum(jnp.where(down == across, r, 0.0), axis=1, keepdims=True)
+    whole = lambda a: a.astype(jnp.int32)
+    return turn(number_row), whole(turn(rows[0])), whole(turn(rows[1])), whole(rows[0]), whole(rows[1])
+
+
+def extract_kernel(z, fine, coarse, com, scr):
     lane = lax.broadcasted_iota(jnp.int32, (z.P, LANES), 1)
     pick = z.P * ((lane % z.P) % z.zg) + jnp.where(lane >= 3 * z.P, z.P - 1, 0)
     group = jnp.where(lane >= 2 * z.P, (lane % z.P) // z.zg, -1)
@@ -119,9 +135,9 @@
                 com[pl.ds((v * z.xa + a) * z.own + q, z.n, stride=z.RC), :] = scr[v % 2, pl.ds(a, z.n, stride=z.xa), :]
             for side in range(2):
                 row = fine[v, q, side * (z.P - 1) : side * (z.P - 1) + 1, :]
-                place = (side * 5 + v) * z.own + q
+                place = z.OX + (side * 5 + v) * z.own + q
                 for j in range(z.n):
-                    xf[j * z.RX + place : j * z.RX + place + 1, : z.PL] = row[:, j * z.PL : (j + 1) * z.PL]
+                    com[j * z.RC + place : j * z.RC + place + 1, : z.PL] = row[:, j * z.PL : (j + 1) * z.PL]
     line = lax.broadcasted_iota(jnp.int32, (z.lines, LANES), 0)
     at = lax.broadcasted_iota(jnp.int32, (z.lines, LANES), 1)
     chosen = (at == z.H * (line // 2) + (z.H - 1) * (line % 2)).astype(jnp.bfloat16)
@@ -139,107 +155,118 @@
                 row = j * z.RC + z.OZ + (v * z.xc + x) * 2
                 com[row : row + 1, :] = coarse[v, j * z.xc + x, 0:1, :]
                 com[row + 1 : row + 2, :] = coarse[v, j * z.xc + x, z.R - 1 : z.R, :]
-    for v in range(5):
-        up[v * z.R : (v + 1) * z.R, :] = coarse[v, z.NX - 1]
-        dn[v * z.R : (v + 1) * z.R, :] = coarse[v, 0]
-        for x in range(z.NX):
-            row = v * z.NX + x
-            pu[row : row + 1, :] = coarse[v, x, z.R - 1 : z.R, :]
-            pd[row : row + 1, :] = coarse[v, x, 0:1, :]
-    numbers = jnp.broadcast_to(number_row[...], (8, LANES))
-    up[5 * z.R : 5 * z.R + 8, :] = numbers
-    dn[5 * z.R : 5 * z.R + 8, :] = numbers
-
-
-def advance_kernel(z, fine, updated, avg, der, zflux, sums):
-    lane = lax.broadcasted_iota(jnp.int32, (z.P, LANES), 1)
-    row = lax.broadcasted_iota(jnp.int32, (z.P, LANES), 0)
-    inner_x = row < z.P - 1
+
+
+def pack_kernel(z, com, coarse, ids, up, dn):
+    for side, margin, layer in ((1, up, z.NX - 1), (0, dn, 0)):
+        for i in range(z.n):
+            k = i * z.RC + z.OX + side * 5 * z.own
+            margin[i * 5 * z.own : (i + 1) * 5 * z.own, :] = com[k : k + 5 * z.own, :]
+        for v in range(5):
+            margin[z.OM + v * z.R : z.OM + (v + 1) * z.R, :] = coarse[v, layer]
+        margin[z.OM + 5 * z.R : z.OM + 5 * z.R + 8, :] = jnp.zeros((8, LANES), jnp.float32)
+        margin[z.OM + 5 * z.R : z.OM + 5 * z.R + 1, : z.S] = ids[...].astype(jnp.float32)
+
+
+def advance_kernel(z, fine, updated, avg, work, xflux, zflux, sums):
+    count = z.own
+    patch = pl.program_id(0)
+    X = min(XROWS, z.P)
+    lane = lax.broadcasted_iota(jnp.int32, (X, LANES), 1)
+    row = lax.broadcasted_iota(jnp.int32, (X, LANES), 0)
     inner_y = lane % z.P < z.P - 1
-    high = lane >= LANES - z.P
-
-    def first_pass(step, carry):
-        q = step // z.G
-        g = step % z.G
-        at = pl.ds(pl.multiple_of(g * LANES, LANES), LANES)
-        U = [fine[v, q, :, at] for v in range(5)]
+    first_z = lane < z.P
+
+    def first_pass(i, carry):
+        at = pl.ds(pl.multiple_of(i * LANES, LANES), LANES)
+        U = [fine[v, 0, :, at] for v in range(5)]
         velocity, pressure, sound = derived(U)
-        for k, value in enumerate(velocity + [pressure, sound]):
-            der[k, q, :, at] = value
+        for k, value in enumerate(U + velocity + [pressure, sound]):
+            work[k, i, : z.P, :] = value
         return carry
 
-    lax.fori_loop(0, z.own * z.G, first_pass, 0)
-
-    def second_pass(step, carry):
-        q = step // z.G
-        g = step % z.G
-        at = pl.ds(pl.multiple_of(g * LANES, LANES), LANES)
-        nxt = pl.ds(pl.multiple_of(jnp.minimum(g + 1, z.G - 1) * LANES, LANES), LANES)
-        U = [fine[v, q, :, at] for v in range(5)]
-        D = [der[k, q, :, at] for k in range(5)]
-        change = None
-        for d in (0, 1):
-            if d == 0:
-                move = lambda a: pltpu.roll(a, z.P - 1, 0)
-                back = lambda a: pltpu.roll(a, 1, 0)
-                inner = inner_x
-            else:
-                move = lambda a: pltpu.roll(a, LANES - 1, 1)
-                back = lambda a: pltpu.roll(a, 1, 1)
-                inner = inner_y
-            f = directed(U, D[d], D[3], d)
-            s = jnp.abs(D[d]) + D[4]
-            signal = jnp.maximum(s, move(s))
-            up = []
+    lax.fori_loop(0, z.G, first_pass, 0)
+    xflux[:, :8, :] = jnp.zeros((5, 8, LANES), jnp.float32)
+
+    def second_pass(i, carry):
+        at = pl.ds(pl.multiple_of(i * LANES, LANES), LANES)
+        nxt = jnp.minimum(i + 1, z.G - 1)
+        inner_z = jnp.logical_or(lane < LANES - z.P, i < z.G - 1)
+        for r in range(0, z.P, X):
+            rows = slice(r, r + X)
+            U = [work[k, i, rows, :] for k in range(5)]
+            D = [work[k, i, rows, :] for k in range(5, 10)]
+            XU = [work[k, i, r + 1 : r + 1 + X, :] for k in range(5)]
+            XD = [work[k, i, r + 1 : r + 1 + X, :] for k in (5, 8, 9)]
+            F = twice_flux(U, (D[0], D[3], D[4]), XU, XD, 0)
+            change = []
             for v in range(5):
-                face = f[v] + move(f[v]) - signal * (move(U[v]) - U[v])
-                face = jnp.where(inner, face, 0.0)
-                up.append(face - back(face))
-            change = up if change is None else [change[v] + up[v] for v in range(5)]
-        f = directed(U, D[2], D[3], 2)
-        s = jnp.abs(D[2]) + D[4]
-        UN = [fine[v, q, :, nxt] for v in range(5)]
-        DN = [der[k, q, :, nxt] for k in (2, 3, 4)]
-        fn = directed(UN, DN[0], DN[1], 2)
-        sn = jnp.abs(DN[0]) + DN[2]
-        beyond = lambda a, b: jnp.where(high, pltpu.roll(b, LANES - z.P, 1), pltpu.roll(a, LANES - z.P, 1))
-        signal = jnp.maximum(s, beyond(s, sn))
-        inner_z = jnp.logical_or(lane < LANES - z.P, g < z.G - 1)
-        for v in range(5):
-            face = f[v] + beyond(f[v], fn[v]) - signal * (beyond(U[v], UN[v]) - U[v])
-            face = jnp.where(inner_z, face, 0.0)
-            rolled = pltpu.roll(face, z.P, 1)
-            before = jnp.where(g == 0, 0.0, zflux[v])
-            zflux[v] = rolled
-            total = change[v] + (face - jnp.where(lane < z.P, before, rolled))
-            new = U[v] - (0.5 * fine_rate) * total
-            updated[v, q, :, at] = new
-            sums[pl.ds(pl.multiple_of(((v * z.own + q) * z.G + g) * z.P, z.P), z.P), :] = new
+                face = jnp.where(row < z.P - 1 - r, F[v], 0.0) if r + X == z.P else F[v]
+                xflux[v, 8 + r : 8 + r + X, :] = face
+                change.append(face - xflux[v, 7 + r : 7 + r + X, :])
+            ahead = lambda a: pltpu.roll(a, LANES - 1, 1)
+            F = twice_flux(U, (D[1], D[3], D[4]), [ahead(a) for a in U], [ahead(D[k]) for k in (1, 3, 4)], 1)
+            for v in range(5):
+                face = jnp.where(inner_y, F[v], 0.0)
+                change[v] = change[v] + (face - pltpu.roll(face, 1, 1))
+            beyond = lambda k, a: pltpu.roll(jnp.where(first_z, work[k, nxt, rows, :], a), LANES - z.P, 1)
+            F = twice_flux(
+                U,
+                (D[2], D[3], D[4]),
+                [beyond(k, U[k]) for k in range(5)],
+                [beyond(5 + k, D[k]) for k in (2, 3, 4)],
+                2,
+            )
+            for v in range(5):
+                face = jnp.where(inner_z, F[v], 0.0)
+                rolled = pltpu.roll(face, z.P, 1)
+                before = jnp.where(i == 0, 0.0, zflux[v, rows, :])
+                zflux[v, rows, :] = rolled
+                new = U[v] - (0.5 * fine_rate) * (change[v] + (face - jnp.where(first_z, before, rolled)))
+                updated[v, 0, rows, at] = new
+                sums[v, patch * z.G + i, rows, :] = new
         return carry
 
-    lax.fori_loop(0, z.own * z.G, second_pass, 0)
-    spot = lax.broadcasted_iota(jnp.int32, (z.n, LANES), 1)
-    half = z.zg // 2
-
-    def average(step, carry):
-        v = step // z.G
-        g = step % z.G
-        out = [jnp.zeros((z.n, LANES), jnp.float32) for _ in range(half)]
-        for q in range(z.own):
-            base = pl.multiple_of(((v * z.own + q) * z.G + g) * z.P, z.P)
+    lax.fori_loop(0, z.G, second_pass, 0)
+
+    @pl.when(patch == count - 1)
+    def _():
+        half = z.zg // 2
+        depth = z.xc * count * LANES
+        source = lax.broadcasted_iota(jnp.int32, (depth, half * LANES), 0)
+        target = lax.broadcasted_iota(jnp.int32, (depth, half * LANES), 1)
+        place = source % LANES
+        piece = source // LANES
+        mean = (
+            (piece == (target % LANES) // z.H)
+            & (place // (2 * z.P) == target // LANES)
+            & ((place % z.P) // 2 == target % z.H)
+        )
+        mean = jnp.where(mean, 0.125, 0.0).astype(jnp.bfloat16)
+
+        def average(v, carry):
+            columns = []
             for x in range(z.xc):
-                pair = sums[pl.ds(base + 2 * x, z.n, stride=z.xa), :] + sums[pl.ds(base + 2 * x + 1, z.n, stride=z.xa), :]
-                pair = pair + pltpu.roll(pair, LANES - 1, 1)
-                pair = pair + pltpu.roll(pair, LANES - z.P, 1)
+                for q in range(count):
+                    blocks = []
+                    for g in range(z.G):
+                        i = q * z.G + g
+                        blocks.append(
+                            sums[v, i, pl.ds(2 * x, z.n, stride=z.xa), :] + sums[v, i, pl.ds(2 * x + 1, z.n, stride=z.xa), :]
+                        )
+                    columns.append(jnp.concatenate(blocks, axis=0))
+            lhs = jnp.concatenate(parts(jnp.concatenate(columns, axis=1), 3), axis=0)
+            got = jnp.dot(lhs, mean, preferred_element_type=jnp.float32)
+            lines = z.G * z.n
+            got = got[:lines] + got[lines : 2 * lines] + got[2 * lines :]
+            for g in range(z.G):
                 for h in range(half):
-                    out[h] = jnp.where(
-                        spot // z.H == x * z.own + q, lanes_at(pair, 2 * z.P * h + 2 * (spot % z.H)), out[h]
-                    )
-        for h in range(half):
-            avg[pl.ds(v * z.H + half * g + h, z.n, stride=z.RA), :] = 0.125 * out[h]
-        return carry
-
-    lax.fori_loop(0, 5 * z.G, average, 0)
+                    rows = pl.ds(v * z.H + half * g + h, z.n, stride=z.RA)
+                    value = got[g * z.n : (g + 1) * z.n, h * LANES : (h + 1) * LANES]
+                    avg[rows, :] = value
+            return carry
+
+        lax.fori_loop(0, 5, average, 0)
 
 
 def coverage(columns, block_z, block_y, count):
@@ -249,8 +276,8 @@
     return lax.fori_loop(0, count, step, jnp.zeros(block_z.shape, jnp.int32))
 
 
-def provisional_kernel(z, info, columns, coarse, below, above, lower, upper, out, pad):
-    slab, rank = info[0], info[1]
+def provisional_kernel(z, columns, coarse, below, above, out, pad):
+    slab, rank = lax.axis_index("slab"), lax.axis_index("patch")
     row = lax.broadcasted_iota(jnp.int32, (z.R, LANES), 0)
     lane = lax.broadcasted_iota(jnp.int32, (z.R, LANES), 1)
     place = row + rank * z.R
@@ -258,23 +285,21 @@
     count = columns.shape[0]
     cover = lambda dz, dy: coverage(columns, block(place + dz), block(lane + dy), count)
     own, zu, zd, yu, yd = [1.0 - cover(*s).astype(jnp.float32) for s in ((0, 0), (1, 0), (-1, 0), (0, 1), (0, -1))]
+    zu = jnp.where(row < z.R - 1, zu, 0.0)
+    zd = jnp.where(row > 0, zd, 0.0)
     for v in range(5):
         pad[v, 1 : z.NX + 1] = coarse[v]
-        pad[v, 0] = jnp.where(slab == 0, coarse[v, 0], below[v * z.R : (v + 1) * z.R, :])
-        pad[v, z.NX + 1] = jnp.where(slab == z.slabs - 1, coarse[v, z.NX - 1], above[v * z.R : (v + 1) * z.R, :])
+        pad[v, 0] = jnp.where(slab == 0, coarse[v, 0], below[z.OM + v * z.R : z.OM + (v + 1) * z.R, :])
+        pad[v, z.NX + 1] = jnp.where(slab == z.slabs - 1, coarse[v, z.NX - 1], above[z.OM + v * z.R : z.OM + (v + 1) * z.R, :])
 
     def layer(x, carry):
         U = [pad[v, x + 1] for v in range(5)]
         XL = [pad[v, x] for v in range(5)]
         XU = [pad[v, x + 2] for v in range(5)]
-        ZL, ZU, YL, YU = [], [], [], []
-        for v in range(5):
-            low = jnp.where(rank == 0, U[v][0:1], lower[pl.ds(v * z.NX + x, 1), :])
-            top = jnp.where(rank == z.n - 1, U[v][z.R - 1 :], upper[pl.ds(v * z.NX + x, 1), :])
-            ZL.append(jnp.where(row == 0, low, pltpu.roll(U[v], 1, 0)))
-            ZU.append(jnp.where(row == z.R - 1, top, pltpu.roll(U[v], z.R - 1, 0)))
-            YL.append(jnp.where(lane == 0, U[v], pltpu.roll(U[v], 1, 1)))
-            YU.append(jnp.where(lane == LANES - 1, U[v], pltpu.roll(U[v], LANES - 1, 1)))
+        ZL = [pltpu.roll(U[v], 1, 0) for v in range(5)]
+        ZU = [pltpu.roll(U[v], z.R - 1, 0) for v in range(5)]
+        YL = [jnp.where(lane == 0, U[v], pltpu.roll(U[v], 1, 1)) for v in range(5)]
+        YU = [jnp.where(lane == LANES - 1, U[v], pltpu.roll(U[v], LANES - 1, 1)) for v in range(5)]
         fx = [a - b for a, b in zip(state_flux(U, XU, 0), state_flux(XL, U, 0))]
         fz = [a * zu - b * zd for a, b in zip(state_flux(U, ZU, 2), state_flux(ZL, U, 2))]
         fy = [a * yu - b * yd for a, b in zip(state_flux(U, YU, 1), state_flux(YL, U, 1))]
@@ -286,18 +311,14 @@
     lax.fori_loop(0, z.NX, layer, 0)
 
 
-def middle_kernel(z, info, spots, ctab, rtab, com, xo, xb, xu, below, above, avg, outf, outc, lat, ghost, xs, canvas):
-    slab = info[0]
+def side_kernel(z, ids, columns, com, ghost, lat):
     S, f_of = z.S, z.P
-    gy, gz, number = ctab[:, 0:1], ctab[:, 1:2], ctab[:, 2:3]
-    gyr, gzr = rtab[0:1, :], rtab[1:2, :]
+    _, gy, gz, gyr, gzr = positions(z, ids, columns)
     lane = lax.broadcasted_iota(jnp.int32, (S, LANES), 1)
     kind = lane // f_of
     even = kind % 2 == 0
     steps = ((0, -1), (0, 1), (-1, 0), (1, 0))
     flags = [((gyr == gy + dy) & (gzr == gz + dz)).astype(jnp.float32) for dy, dz in steps]
-    turned = [((gy == gyr + dy) & (gz == gzr + dz)).astype(jnp.float32) for dy, dz in steps]
-    absent_row = [1.0 - jnp.sum(t, axis=0, keepdims=True) for t in turned]
     here = jnp.zeros((S, LANES), jnp.float32)
     for k in range(4):
         here = jnp.where(kind == k, jnp.sum(flags[k], axis=1, keepdims=True), here)
@@ -365,10 +386,48 @@
         for v in range(5):
             C = sign * F[v]
             ghost[at[v], :] = C
+
+
+def end_kernel(z, ids, columns, com, ghost, below, above, outf, xc, xs):
+    S = z.S
+    slab = lax.axis_index("slab")
+    number = positions(z, ids, columns)[0]
+    for d in range(z.n):
+        for k in range(5 * z.xa):
+            outf[d * z.RF + k * z.own : d * z.RF + (k + 1) * z.own, :] = ghost[k * S + d * z.own : k * S + (d + 1) * z.own, :]
+    for w, (source, pitch, offset) in enumerate(
+        ((com, z.RC, z.OX), (com, z.RC, z.OX + 5 * z.own), (below, 5 * z.own, 0), (above, 5 * z.own, 0))
+    ):
+        for i in range(z.n):
+            for v in range(5):
+                k = (w * 5 + v) * S + i * z.own
+                r = i * pitch + offset + v * z.own
+                xs[k : k + z.own, :] = source[r : r + z.own, :]
+    for side, (margin, edge) in enumerate(((below, slab == 0), (above, slab == z.slabs - 1))):
+        match = (number == margin[z.OM + 5 * z.R : z.OM + 5 * z.R + 1, :S]).astype(jnp.bfloat16)
+        own = [xs[(side * 5 + v) * S : (side * 5 + v + 1) * S, :] for v in range(5)]
+        far = select_dot(
+            match, jnp.concatenate([xs[((2 + side) * 5 + v) * S : ((2 + side) * 5 + v + 1) * S, :] for v in range(5)], axis=1)
+        )
+        far = [jnp.where(edge, own[v], far[:, v * LANES : (v + 1) * LANES]) for v in range(5)]
+        F = state_flux(far, own, 0) if side == 0 else state_flux(own, far, 0)
+        for v in range(5):
+            C = (0.5 * fine_rate if side == 0 else -0.5 * fine_rate) * F[v]
+            xc[(side * 5 + v) * S : (side * 5 + v + 1) * S, :] = C
             for d in range(z.n):
-                k = d * z.RF + (v * z.xa + a) * z.own
+                k = d * z.RF + z.OFX + (side * 5 + v) * z.own
                 outf[k : k + z.own, :] = C[d * z.own : (d + 1) * z.own]
 
+
+def canvas_kernel(z, ids_s, columns_s, ids, columns, com, ghost, xc, avg, outc, canvas):
+    S, f_of = z.S, z.P
+    vx = 5 * z.xc
+    _, gy, gz, gyr, gzr = positions(z, ids, columns)
+    lane = lax.broadcasted_iota(jnp.int32, (S, LANES), 1)
+    steps = ((0, -1), (0, 1), (-1, 0), (1, 0))
+    flags = [((gyr == gy + dy) & (gzr == gz + dz)).astype(jnp.float32) for dy, dz in steps]
+    turned = [((gy == gyr + dy) & (gz == gzr + dz)).astype(jnp.float32) for dy, dz in steps]
+    absent_row = [1.0 - jnp.sum(t, axis=0, keepdims=True) for t in turned]
     zrow = lax.broadcasted_iota(jnp.int32, (z.NZ, S), 0)
     base = z.H * (gzr + 1)
     zmat = jnp.concatenate(
@@ -403,13 +462,33 @@
                 total = total + jnp.dot(piece, ymat, preferred_element_type=jnp.float32)
             canvas[k * z.NZ : (k + 1) * z.NZ, :] = total
 
+    rank = lax.broadcasted_iota(jnp.int32, (z.n, LANES), 0)
+    rank_slot = lax.broadcasted_iota(jnp.int32, (z.n, S), 0)
+    inside_y = in_y.astype(jnp.bfloat16)
+    cover = lambda block: jnp.dot((block == gzr + 1).astype(jnp.bfloat16), inside_y, preferred_element_type=jnp.float32)
+    bare_first = 1.0 - cover((rank_slot * z.R) // z.H)
+    bare_last = 1.0 - cover((rank_slot * z.R + z.R - 1) // z.H)
+    low_mask = bare_first * jnp.where(rank == 0, 1.0, pltpu.roll(bare_last, 1, 0))
+    top_mask = bare_last * jnp.where(rank == z.n - 1, 1.0, pltpu.roll(bare_first, z.n - 1, 0))
+    for x in range(z.xc):
+        lines = [[com[pl.ds(z.OZ + 2 * (v * z.xc + x) + s, z.n, stride=z.RC), :] for v in range(5)] for s in (0, 1)]
+        under = [jnp.where(rank == 0, lines[0][v], pltpu.roll(lines[1][v], 1, 0)) for v in range(5)]
+        over = [jnp.where(rank == z.n - 1, lines[1][v], pltpu.roll(lines[0][v], z.n - 1, 0)) for v in range(5)]
+        low = state_flux(under, lines[0], 2)
+        top = state_flux(lines[1], over, 2)
+        for v in range(5):
+            first = pl.ds((v * z.xc + x) * z.NZ, z.n, stride=z.R)
+            last = pl.ds((v * z.xc + x) * z.NZ + z.R - 1, z.n, stride=z.R)
+            canvas[first, :] = canvas[first, :] + (0.5 * coarse_rate) * low_mask * low[v]
+            canvas[last, :] = canvas[last, :] - (0.5 * coarse_rate) * top_mask * top[v]
+
     spot = lax.broadcasted_iota(jnp.int32, (z.H, LANES), 1) // z.H
 
     def place(k, carry):
         i = k // z.own
         q = k % z.own
-        sy = spots[0, k] + 1
-        sz = spots[1, k] + 1
+        sy = columns_s[ids_s[0, k], 0] + 1
+        sz = columns_s[ids_s[0, k], 1] + 1
         inside = spot == sy
         for v in range(5):
             block = avg[pl.ds(pl.multiple_of(i * z.RA + v * z.H, 8), z.H), :]
@@ -424,30 +503,11 @@
         for k in range(vx):
             outc[d * z.RK + k * z.R : d * z.RK + (k + 1) * z.R, :] = canvas[k * z.NZ + d * z.R : k * z.NZ + (d + 1) * z.R, :]
 
-    tables = ((xo, 0), (xo, 5), (xb, 5), (xu, 0))
-    for w, (source, offset) in enumerate(tables):
-        for i in range(z.n):
-            for v in range(5):
-                k = (w * 5 + v) * S + i * z.own
-                r = i * z.RX + (offset + v) * z.own
-                xs[k : k + z.own, :] = source[r : r + z.own, :]
-    value = number.astype(jnp.float32)
-    zb = (
-        lax.broadcasted_iota(jnp.int32, (z.n, S), 0) // z.m == gzr + 1
-    ).astype(jnp.bfloat16)
-    for side, (margin, edge) in enumerate(((below, slab == 0), (above, slab == z.slabs - 1))):
-        match = (value == margin[5 * z.R : 5 * z.R + 1, :S]).astype(jnp.bfloat16)
-        own = [xs[(side * 5 + v) * S : (side * 5 + v + 1) * S, :] for v in range(5)]
-        far = select_dot(
-            match, jnp.concatenate([xs[((2 + side) * 5 + v) * S : ((2 + side) * 5 + v + 1) * S, :] for v in range(5)], axis=1)
-        )
-        far = [jnp.where(edge, own[v], far[:, v * LANES : (v + 1) * LANES]) for v in range(5)]
-        F = state_flux(far, own, 0) if side == 0 else state_flux(own, far, 0)
-        for v in range(5):
-            C = (0.5 * fine_rate if side == 0 else -0.5 * fine_rate) * F[v]
-            for d in range(z.n):
-                k = d * z.RF + z.OFX + (side * 5 + v) * z.own
-                outf[k : k + z.own, :] = C[d * z.own : (d + 1) * z.own]
+
+    zb = (rank_slot // z.m == gzr + 1).astype(jnp.bfloat16)
+    for side in range(2):
+        for v in range(5):
+            C = xc[(side * 5 + v) * S : (side * 5 + v + 1) * S, :]
             Q = C + pltpu.roll(C, LANES - 1, 1)
             Q = 0.125 * (Q + pltpu.roll(Q, LANES - z.P, 1))
             for h in range(z.zcl):
@@ -481,13 +541,13 @@
                     out[v, q, x : x + 1, at] = out[v, q, x : x + 1, at] + recv[r : r + 1, : z.PL]
 
 
-def coarse_kernel(z, info, prov, recv, out):
+def coarse_kernel(z, prov, recv, out):
     for j in range(z.n):
         for v in range(5):
             for x in range(z.xc):
                 r = j * z.RK + (v * z.xc + x) * z.R
                 out[v, j * z.xc + x] = prov[v, j * z.xc + x] + recv[r : r + z.R, :]
-    offset = 0 if z.m == 1 else lax.rem(info[1], z.m) * z.R
+    offset = 0 if z.m == 1 else lax.rem(lax.axis_index("patch"), z.m) * z.R
     for v in range(5):
         for side in range(2):
             x = side * (z.NX - 1)
@@ -497,7 +557,7 @@
                 out[v, x, zl : zl + 1, :] = out[v, x, zl : zl + 1, :] + recv[pl.ds(r, 1), :]
 
 
-def call(kernel, z, outs, ins, scratch=(), aliases=None, name=None):
+def call(kernel, z, outs, ins, scratch=(), aliases=None):
     return pl.pallas_call(
         functools.partial(kernel, z),
         out_shape=[jax.ShapeDtypeStruct(s, jnp.float32) for s in outs],
@@ -506,76 +566,77 @@
         scratch_shapes=[pltpu.VMEM(s, jnp.float32) for s in scratch],
         input_output_aliases=aliases or {},
         compiler_params=pltpu.CompilerParams(vmem_limit_bytes=56 * 1024 * 1024),
-        name=name,
     )(*[a for _, a in ins])
 
 
+def run_advance(z, fine):
+    block = pl.BlockSpec((5, 1) + fine.shape[2:], lambda i: (0, i, 0, 0))
+    average = (z.n * z.RA, LANES)
+    return pl.pallas_call(
+        functools.partial(advance_kernel, z),
+        grid=(z.own,),
+        out_shape=[jax.ShapeDtypeStruct(fine.shape, jnp.float32), jax.ShapeDtypeStruct(average, jnp.float32)],
+        in_specs=[block],
+        out_specs=[block, pl.BlockSpec(average, lambda i: (0, 0))],
+        scratch_shapes=[
+            pltpu.VMEM(s, jnp.float32)
+            for s in ((10, z.G, z.P + 8, LANES), (5, z.P + 8, LANES), (5, z.P, LANES), (5, z.own * z.G, z.P, LANES))
+        ],
+        compiler_params=pltpu.CompilerParams(vmem_limit_bytes=56 * 1024 * 1024),
+        name="advance",
+    )(fine)
+
+
 def local(n, slabs, coarse, fine, columns, patch_ids):
-    numbers = patch_ids[0]
-    slots = numbers.shape[0]
+    return level_step(n, slabs, coarse, fine, columns, patch_ids)
+
+
+def level_step(n, slabs, coarse, fine, columns, patch_ids):
+    slots = patch_ids.shape[1]
     assert columns.shape[0] == slots
     z = Sizes(n, slabs, fine.shape, coarse.shape, slots)
-    info = jnp.stack([lax.axis_index("slab"), lax.axis_index("patch")]).astype(jnp.int32)
-    held = numbers[:, None] == jnp.arange(slots, dtype=jnp.int32)[None, :]
-    spots = jnp.sum(jnp.where(held[None], columns.T[:, None, :], 0), axis=2).astype(jnp.int32)
-    rtab = jnp.concatenate([spots, numbers[None]], axis=0)
-    ctab = rtab.T
-    number_row = jnp.pad(numbers.astype(jnp.float32), (0, LANES - slots))[None]
-
-    exchange = lambda a: lax.all_to_all(a, "patch", 0, 0, tiled=True)
-    ahead = lambda count: [(i, i + 1) for i in range(count - 1)]
-    back = lambda count: [(i + 1, i) for i in range(count - 1)]
-
-    com, xf, up, dn, pu, pd = call(
-        extract_kernel,
+
+    def exchange(a):
+        return lax.all_to_all(a, "patch", 0, 0, tiled=True)
+
+    def shifted(a, step):
+        pairs = [(i, i + step) for i in range(slabs) if 0 <= i + step < slabs]
+        return lax.ppermute(a, "slab", pairs)
+
+    faces = (5 * z.xa * slots, LANES)
+    (com,) = call(extract_kernel, z, [(n * z.RC, LANES)], [("v", fine), ("v", coarse)], [(2, z.P, LANES)])
+    com = exchange(com)
+    updated, avg = run_advance(z, fine)
+    avg = exchange(avg)
+    up, dn = call(pack_kernel, z, [(z.RP, LANES)] * 2, [("v", com), ("v", coarse), ("v", patch_ids)])
+    below = shifted(up, 1)
+    above = shifted(dn, -1)
+    (ghost,) = call(side_kernel, z, [faces], [("v", a) for a in (patch_ids, columns, com)], [faces])
+    outf, xc = call(
+        end_kernel,
         z,
-        [(n * z.RC, LANES), (n * z.RX, LANES), (z.RM, LANES), (z.RM, LANES), (5 * z.NX, LANES), (5 * z.NX, LANES)],
-        [("v", fine), ("v", coarse), ("v", number_row)],
-        [(2, z.P, LANES)],
-        name="extract",
+        [(n * z.RF, LANES), (10 * slots, LANES)],
+        [("v", a) for a in (patch_ids, columns, com, ghost, below, above)],
+        [(20 * slots, LANES)],
     )
-    xo = exchange(xf)
-    below = lax.ppermute(up, "slab", ahead(slabs))
-    above = lax.ppermute(dn, "slab", back(slabs))
-    lower = lax.ppermute(pu, "patch", ahead(n))
-    upper = lax.ppermute(pd, "patch", back(n))
-    xb = lax.ppermute(xo, "slab", ahead(slabs))
-    xu = lax.ppermute(xo, "slab", back(slabs))
-    com = exchange(com)
-    updated, avg = call(
-        advance_kernel,
-        z,
-        [fine.shape, (n * z.RA, LANES)],
-        [("v", fine)],
-        [fine.shape, (5, z.P, LANES), (5 * z.own * z.G * z.P, LANES)],
-        name="advance",
-    )
-    avg = exchange(avg)
+    outf = exchange(outf)
     (prov,) = call(
         provisional_kernel,
         z,
         [coarse.shape],
-        [("s", info), ("s", columns), ("v", coarse), ("v", below), ("v", above), ("v", lower), ("v", upper)],
+        [("s", columns), ("v", coarse), ("v", below), ("v", above)],
         [(5, z.NX + 2, z.R, LANES)],
-        name="provisional",
     )
-    outf, outc = call(
-        middle_kernel,
+    (outc,) = call(
+        canvas_kernel,
         z,
-        [(n * z.RF, LANES), (n * z.RK, LANES)],
-        [("s", info), ("s", spots), ("v", ctab), ("v", rtab)]
-        + [("v", a) for a in (com, xo, xb, xu, below, above, avg)],
-        [(5 * z.xa * slots, LANES), (5 * z.xa * slots, LANES), (20 * slots, LANES), (5 * z.xc * z.NZ, LANES)],
-        name="middle",
+        [(n * z.RK, LANES)],
+        [("s", patch_ids), ("s", columns)] + [("v", a) for a in (patch_ids, columns, com, ghost, xc, avg)],
+        [(5 * z.xc * z.NZ, LANES)],
     )
-    outf = exchange(outf)
     outc = exchange(outc)
-    (fine_out,) = call(
-        fine_kernel, z, [fine.shape], [("v", updated), ("v", outf)], [(2, z.P, LANES)], {0: 0}, name="fine_edges"
-    )
-    (coarse_out,) = call(
-        coarse_kernel, z, [coarse.shape], [("s", info), ("v", prov), ("v", outc)], name="coarse_sum"
-    )
+    (fine_out,) = call(fine_kernel, z, [fine.shape], [("v", updated), ("v", outf)], [(2, z.P, LANES)])
+    (coarse_out,) = call(coarse_kernel, z, [coarse.shape], [("v", prov), ("v", outc)])
     return coarse_out, fine_out
 
 

time: 141 us -> 94.5 us (0.67)
  the two profiles are of different devices: /device:TPU:17 before, /device:TPU:0 now
where the time goes in v2:
time: 94.5 us; the launch traced here: 93.8 us
  Pallas kernels  43.9 us (46%)
  starting transfers between devices  24.5 us (26%)
  waiting for transfers between devices  21.8 us (23%)
  local copies, waits for them, and re-layouts  2.89 us (3%)
    pallas_call x8, Pallas kernels, call(): pl.pallas_call(functools.partial(kernel, z), out_shape=[jax.ShapeDtypeStr...  31.5 us
    all_to_all x4, waiting for transfers between devices, exchange(): return lax.all_to_all(a, 'patch', 0, 0, tiled=True)  21.8 us
    all_to_all x4, starting transfers between devices, exchange(): return lax.all_to_all(a, 'patch', 0, 0, tiled=True)  21.5 us
    pallas_call x1, Pallas kernels, run_advance(): pl.pallas_call(functools.partial(advance_kernel, z), grid=(z.own,), out_s...  12.4 us
    ppermute x2, starting transfers between devices, shifted(): return lax.ppermute(a, 'slab', pairs)  2.93 us
    unnamed x15, local copies, waits for them, and re-layouts  2.89 us
  transfers between devices with their start and end apart: 6, of which 3 were waited for; matrix products, arithmetic and copies ran while one was open for 1% of the time, Pallas kernels for 40%

profile of v2, /device:TPU:0, one launch (start us, length us, event | category | flops | bytes accessed | tf_op | source)
XLA Modules:
  0.0 93.8 jit_solution(8003711541372692285)
XLA Ops:
  0.6 3.7 %shard_map.59 = f32[1408,128]{1,0:T(8,128)} custom-call(f32[5,4,32,1024]{3,2,1,0:T(8,128)} %fine.3, f32[5,16,16,128]{3,2,1,0:T(8,128)} %coarse.5), custom_call_target="tpu_custom_call" | custom-call | tf_op jit(solution)/shard_map/pallas_call | solution.py:561
  4.3 7.3 %all-to-all-start = ((f32[8,176,128]{2,1,0:T(8,128)}), f32[8,176,128]{2,1,0:T(8,128)S(1)}, u32[]{:S(2)}, u32[]{:S(2)}) async-start(f32[8,176,128]{2,1,0:T(8,128)} %bitcast.14), calls=%async_computation | async-start | bytes 1441792 | tf_op jit(solution)/shard_map/all_to_all | solution.py:600
  11.6 0.0 copy-start.6
  11.6 12.4 %advance.1 = (f32[5,4,32,1024]{3,2,1,0:T(8,128)}, f32[640,128]{1,0:T(8,128)}) custom-call(f32[5,4,32,1024]{3,2,1,0:T(8,128)} %fine.3), custom_call_target="tpu_custom_call" | custom-call | tf_op jit(solution)/shard_map/advance/pallas_call | solution.py:575
  24.0 6.3 %all-to-all-done = f32[8,176,128]{2,1,0:T(8,128)S(1)} async-done(((f32[8,176,128]{2,1,0:T(8,128)}), f32[8,176,128]{2,1,0:T(8,128)S(1)}, u32[]{:S(2)}, u32[]{:S(2)}) %all-to-all-start) | async-done | bytes 720928 | tf_op jit(solution)/shard_map/all_to_all | solution.py:600
  30.3 0.0 copy-start
  30.3 3.6 %all-to-all-start.1 = ((f32[8,80,128]{2,1,0:T(8,128)}), f32[8,80,128]{2,1,0:T(8,128)S(1)}, u32[]{:S(2)}, u32[]{:S(2)}) async-start(f32[8,80,128]{2,1,0:T(8,128)} %bitcast.18), calls=%async_computation.1 | async-start | bytes 655360 | tf_op jit(solution)/shard_map/all_to_all | solution.py:600
  34.0 0.0 copy-done
  34.0 2.0 %shard_map.60 = (f32[248,128]{1,0:T(8,128)}, f32[248,128]{1,0:T(8,128)}) custom-call(f32[1408,128]{1,0:T(8,128)} %bitcast.8, f32[5,16,16,128]{3,2,1,0:T(8,128)} %coarse.5, s32[1,32]{1,0:T(1,128)} %ids.7), custom_call_target="tpu_custom_call" | custom-call | tf_op jit(solution)/shard_map/pallas_call | solution.py:561
  36.0 1.6 %collective-permute-start = (f32[248,128]{1,0:T(8,128)}, f32[248,128]{1,0:T(8,128)S(1)}, u32[]{:S(2)}, u32[]{:S(2)}) collective-permute-start(f32[248,128]{1,0:T(8,128)} %get-tuple-element.8), channel_id=1, source_target_pairs={{0,8},{8,16},{16,24},{1,9},{9,17},{17,25},{2,10},{10,18},{18,26},{... | collective-permute-start | bytes 380936 | tf_op jit(solution)/shard_map/ppermute | solution.py:604
  37.6 1.3 %collective-permute-start.1 = (f32[248,128]{1,0:T(8,128)}, f32[248,128]{1,0:T(8,128)S(1)}, u32[]{:S(2)}, u32[]{:S(2)}) collective-permute-start(f32[248,128]{1,0:T(8,128)} %get-tuple-element.9), channel_id=1, source_target_pairs={{8,0},{16,8},{24,16},{9,1},{17,9},{25,17},{10,2},{18,10},{26,18},{... | collective-permute-start | bytes 380936 | tf_op jit(solution)/shard_map/ppermute | solution.py:604
  38.9 0.0 copy-done.6
  38.9 0.7 copy.6.columns.columns_s
  39.6 3.0 %shard_map.62.ghost = f32[640,128]{1,0:T(8,128)} custom-call(s32[1,32]{1,0:T(1,128)} %ids.7, s32[32,2]{1,0:T(8,128)} %copy.6.columns.columns_s, f32[1408,128]{1,0:T(8,128)} %bitcast.9), custom_call_target="tpu_custom_call" | custom-call | tf_op jit(solution)/shard_map/pallas_call | solution.py:561
  42.6 0.0 collective-permute-done.below
  42.6 0.0 copy-start.4
  42.6 0.0 collective-permute-done.1.above
  42.6 0.6 copy-done.4
  43.3 0.7 copy-done.5
  43.9 2.5 %shard_map.63 = (f32[960,128]{1,0:T(8,128)}, f32[320,128]{1,0:T(8,128)}) custom-call(s32[1,32]{1,0:T(1,128)} %ids.7, s32[32,2]{1,0:T(8,128)} %copy.6.columns.columns_s, f32[1408,128]{1,0:T(8,128)} %bitcast.10, f32[640,128]{1,0:T(8,128)} %shard_map.62.ghost, f32[248,128]{1,0:T(8,128)} %copy-done.4, f32[248,128]{1,0:T(8,128)} %copy-done.5), custom_call_target="tpu_custom_call" | custom-call | tf_op jit(solution)/shard_map/pallas_call | solution.py:561
  46.4 0.0 all-to-all-done.1
  46.4 5.7 %all-to-all-start.3 = ((f32[8,120,128]{2,1,0:T(8,128)}), f32[8,120,128]{2,1,0:T(8,128)S(1)}, u32[]{:S(2)}, u32[]{:S(2)}) async-start(f32[8,120,128]{2,1,0:T(8,128)} %bitcast.17), calls=%async_computation.3 | async-start | bytes 983040 | tf_op jit(solution)/shard_map/all_to_all | solution.py:600
  52.1 0.0 copy-done.3
  52.1 7.4 %shard_map.64 = f32[1472,128]{1,0:T(8,128)} custom-call(s32[1,32]{1,0:T(1,128)} %ids.7, s32[32,2]{1,0:T(8,128)} %copy.6.columns.columns_s, s32[1,32]{1,0:T(1,128)} %ids.7, s32[32,2]{1,0:T(8,128)} %copy.6.columns.columns_s, f32[1408,128]{1,0:T(8,128)} %bitcast.11, f32[640,128]{1,0:T(8,128)} %shard_map.62.ghost, f32[320,128]{1,0:T(8,128)} %get-tuple-element.10.xc, ...), custom_call_target="tpu_custom_call" | custom-call | tf_op jit(solution)/shard_map/pallas_call | solution.py:561
  59.5 6.2 %all-to-all-done.3 = f32[8,120,128]{2,1,0:T(8,128)S(1)} async-done(((f32[8,120,128]{2,1,0:T(8,128)}), f32[8,120,128]{2,1,0:T(8,128)S(1)}, u32[]{:S(2)}, u32[]{:S(2)}) %all-to-all-start.3) | async-done | bytes 491552 | tf_op jit(solution)/shard_map/all_to_all | solution.py:600
  65.7 4.9 %all-to-all-start.2 = ((f32[8,184,128]{2,1,0:T(8,128)}), f32[8,184,128]{2,1,0:T(8,128)S(1)}, u32[]{:S(2)}, u32[]{:S(2)}) async-start(f32[8,184,128]{2,1,0:T(8,128)} %bitcast.12), calls=%async_computation.2 | async-start | bytes 1507328 | tf_op jit(solution)/shard_map/all_to_all | solution.py:600
  70.6 5.7 %shard_map.61.prov = f32[5,16,16,128]{3,2,1,0:T(8,128)} custom-call(s32[32,2]{1,0:T(8,128)} %copy.6.columns.columns_s, f32[5,16,16,128]{3,2,1,0:T(8,128)} %coarse.5, f32[248,128]{1,0:T(8,128)} %copy-done.4, f32[248,128]{1,0:T(8,128)} %copy-done.5), custom_call_target="tpu_custom_call" | custom-call | tf_op jit(solution)/shard_map/pallas_call | solution.py:561
  76.3 0.0 copy-done.2
  76.3 5.0 %shard_map.66 = f32[5,4,32,1024]{3,2,1,0:T(8,128)} custom-call(f32[5,4,32,1024]{3,2,1,0:T(8,128)} %get-tuple-element.12.updated, f32[960,128]{1,0:T(8,128)} %bitcast.15), custom_call_target="tpu_custom_call" | custom-call | tf_op jit(solution)/shard_map/pallas_call | solution.py:561
  81.3 9.3 %all-to-all-done.2 = f32[8,184,128]{2,1,0:T(8,128)S(1)} async-done(((f32[8,184,128]{2,1,0:T(8,128)}), f32[8,184,128]{2,1,0:T(8,128)S(1)}, u32[]{:S(2)}, u32[]{:S(2)}) %all-to-all-start.2) | async-done | bytes 753696 | tf_op jit(solution)/shard_map/all_to_all | solution.py:600
  90.6 0.9 copy-done.1
  91.5 2.3 %shard_map.65 = f32[5,16,16,128]{3,2,1,0:T(8,128)} custom-call(f32[5,16,16,128]{3,2,1,0:T(8,128)} %shard_map.61.prov, f32[1472,128]{1,0:T(8,128)} %bitcast.13), custom_call_target="tpu_custom_call" | custom-call | tf_op jit(solution)/shard_map/pallas_call | solution.py:561
  (4 shorter events, 0.0 us)
Async XLA Ops:
  4.3 26.0 %all-to-all-start = ((f32[8,176,128]{2,1,0:T(8,128)}), f32[8,176,128]{2,1,0:T(8,128)S(1)}, u32[]{:S(2)}, u32[]{:S(2)}) async-start(f32[8,176,128]{2,1,0:T(8,128)} %bitcast.14), calls=%async_computation | async-start | bytes 1441792 | tf_op jit(solution)/shard_map/all_to_all | solution.py:600
  11.6 27.3 %copy-start.6 = (s32[32,2]{0,1:T(2,128)S(1)}, s32[32,2]{0,1:T(2,128)}, u32[]{:S(2)}) copy-start(s32[32,2]{0,1:T(2,128)} %param.6) | copy-start | bytes 772
  30.3 3.6 %copy-start = (f32[8,176,128]{2,1,0:T(8,128)}, f32[8,176,128]{2,1,0:T(8,128)S(1)}, u32[]{:S(2)}) copy-start(f32[8,176,128]{2,1,0:T(8,128)S(1)} %all-to-all-done) | copy-start | bytes 2162692
  30.3 16.1 %all-to-all-start.1 = ((f32[8,80,128]{2,1,0:T(8,128)}), f32[8,80,128]{2,1,0:T(8,128)S(1)}, u32[]{:S(2)}, u32[]{:S(2)}) async-start(f32[8,80,128]{2,1,0:T(8,128)} %bitcast.18), calls=%async_computation.1 | async-start | bytes 655360 | tf_op jit(solution)/shard_map/all_to_all | solution.py:600
  36.0 6.6 %collective-permute-start = (f32[248,128]{1,0:T(8,128)}, f32[248,128]{1,0:T(8,128)S(1)}, u32[]{:S(2)}, u32[]{:S(2)}) collective-permute-start(f32[248,128]{1,0:T(8,128)} %get-tuple-element.8), channel_id=1, source_target_pairs={{0,8},{8,16},{16,24},{1,9},{9,17},{17,25},{2,10},{10,18},{18,26},{... | collective-permute-start | bytes 380936 | tf_op jit(solution)/shard_map/ppermute | solution.py:604
  37.6 5.0 %collective-permute-start.1 = (f32[248,128]{1,0:T(8,128)}, f32[248,128]{1,0:T(8,128)S(1)}, u32[]{:S(2)}, u32[]{:S(2)}) collective-permute-start(f32[248,128]{1,0:T(8,128)} %get-tuple-element.9), channel_id=1, source_target_pairs={{8,0},{16,8},{24,16},{9,1},{17,9},{25,17},{10,2},{18,10},{26,18},{... | collective-permute-start | bytes 380936 | tf_op jit(solution)/shard_map/ppermute | solution.py:604
  42.6 0.7 copy-start.4
  43.3 0.7 copy-start.5
  46.4 5.7 %copy-start.3 = (f32[8,80,128]{2,1,0:T(8,128)}, f32[8,80,128]{2,1,0:T(8,128)S(1)}, u32[]{:S(2)}) copy-start(f32[8,80,128]{2,1,0:T(8,128)S(1)} %all-to-all-done.1) | copy-start | bytes 983044
  46.4 19.3 %all-to-all-start.3 = ((f32[8,120,128]{2,1,0:T(8,128)}), f32[8,120,128]{2,1,0:T(8,128)S(1)}, u32[]{:S(2)}, u32[]{:S(2)}) async-start(f32[8,120,128]{2,1,0:T(8,128)} %bitcast.17), calls=%async_computation.3 | async-start | bytes 983040 | tf_op jit(solution)/shard_map/all_to_all | solution.py:600
  65.7 10.6 %copy-start.2 = (f32[8,120,128]{2,1,0:T(8,128)}, f32[8,120,128]{2,1,0:T(8,128)S(1)}, u32[]{:S(2)}) copy-start(f32[8,120,128]{2,1,0:T(8,128)S(1)} %all-to-all-done.3) | copy-start | bytes 1474564
  65.7 24.8 %all-to-all-start.2 = ((f32[8,184,128]{2,1,0:T(8,128)}), f32[8,184,128]{2,1,0:T(8,128)S(1)}, u32[]{:S(2)}, u32[]{:S(2)}) async-start(f32[8,184,128]{2,1,0:T(8,128)} %bitcast.12), calls=%async_computation.2 | async-start | bytes 1507328 | tf_op jit(solution)/shard_map/all_to_all | solution.py:600
  90.6 0.9 copy-start.1

commit v3 on v2

--- a/solution.py
+++ b/solution.py
@@ -10,6 +10,7 @@
 
 LANES = 128
 XROWS = 16
+VMEM_LIMIT = 24 * 1024 * 1024
 heat_ratio = 1.4
 fine_rate = 0.1
 coarse_rate = 0.05
@@ -157,13 +158,13 @@
                 com[row + 1 : row + 2, :] = coarse[v, j * z.xc + x, z.R - 1 : z.R, :]
 
 
-def pack_kernel(z, com, coarse, ids, up, dn):
-    for side, margin, layer in ((1, up, z.NX - 1), (0, dn, 0)):
+def pack_kernel(z, com, outer, ids, up, dn):
+    for side, margin in ((1, up), (0, dn)):
         for i in range(z.n):
             k = i * z.RC + z.OX + side * 5 * z.own
             margin[i * 5 * z.own : (i + 1) * 5 * z.own, :] = com[k : k + 5 * z.own, :]
         for v in range(5):
-            margin[z.OM + v * z.R : z.OM + (v + 1) * z.R, :] = coarse[v, layer]
+            margin[z.OM + v * z.R : z.OM + (v + 1) * z.R, :] = outer[v, side]
         margin[z.OM + 5 * z.R : z.OM + 5 * z.R + 8, :] = jnp.zeros((8, LANES), jnp.float32)
         margin[z.OM + 5 * z.R : z.OM + 5 * z.R + 1, : z.S] = ids[...].astype(jnp.float32)
 
@@ -223,7 +224,7 @@
                 before = jnp.where(i == 0, 0.0, zflux[v, rows, :])
                 zflux[v, rows, :] = rolled
                 new = U[v] - (0.5 * fine_rate) * (change[v] + (face - jnp.where(first_z, before, rolled)))
-                updated[v, 0, rows, at] = new
+                updated[v, patch, rows, at] = new
                 sums[v, patch * z.G + i, rows, :] = new
         return carry
 
@@ -269,43 +270,54 @@
         lax.fori_loop(0, 5, average, 0)
 
 
-def coverage(columns, block_z, block_y, count):
-    def step(k, found):
-        return jnp.logical_or(found, (block_y == columns[k, 0] + 1) & (block_z == columns[k, 1] + 1)).astype(jnp.int32)
-
-    return lax.fori_loop(0, count, step, jnp.zeros(block_z.shape, jnp.int32))
-
-
-def provisional_kernel(z, columns, coarse, below, above, out, pad):
-    slab, rank = lax.axis_index("slab"), lax.axis_index("patch")
+def provisional_kernel(z, columns, coarse, out, bare, outer, pad):
+    rank = lax.axis_index("patch")
     row = lax.broadcasted_iota(jnp.int32, (z.R, LANES), 0)
     lane = lax.broadcasted_iota(jnp.int32, (z.R, LANES), 1)
-    place = row + rank * z.R
+    S = columns.shape[0]
+    gy = columns[:, 0:1]
+    turn = lax.broadcasted_iota(jnp.int32, (S, S), 0) == lax.broadcasted_iota(jnp.int32, (S, S), 1)
+    gzr = jnp.sum(jnp.where(turn, columns[:, 1:2].astype(jnp.float32), 0.0), axis=0, keepdims=True).astype(jnp.int32)
     block = lambda a: (a + z.H) // z.H - 1
-    count = columns.shape[0]
-    cover = lambda dz, dy: coverage(columns, block(place + dz), block(lane + dy), count)
-    own, zu, zd, yu, yd = [1.0 - cover(*s).astype(jnp.float32) for s in ((0, 0), (1, 0), (-1, 0), (0, 1), (0, -1))]
+    place = lax.broadcasted_iota(jnp.int32, (z.R, S), 0) + rank * z.R
+    across = lax.broadcasted_iota(jnp.int32, (S, LANES), 1)
+
+    def uncovered(dz, dy):
+        rows = (block(place + dz) == gzr + 1).astype(jnp.bfloat16)
+        lanes = (block(across + dy) == gy + 1).astype(jnp.bfloat16)
+        return 1.0 - jnp.dot(rows, lanes, preferred_element_type=jnp.float32)
+
+    own, zu, zd, yu, yd = [uncovered(*shift) for shift in ((0, 0), (1, 0), (-1, 0), (0, 1), (0, -1))]
     zu = jnp.where(row < z.R - 1, zu, 0.0)
     zd = jnp.where(row > 0, zd, 0.0)
+    bare[...] = own
     for v in range(5):
-        pad[v, 1 : z.NX + 1] = coarse[v]
-        pad[v, 0] = jnp.where(slab == 0, coarse[v, 0], below[z.OM + v * z.R : z.OM + (v + 1) * z.R, :])
-        pad[v, z.NX + 1] = jnp.where(slab == z.slabs - 1, coarse[v, z.NX - 1], above[z.OM + v * z.R : z.OM + (v + 1) * z.R, :])
+        outer[v, 0] = coarse[v, 0]
+        outer[v, 1] = coarse[v, z.NX - 1]
 
     def layer(x, carry):
-        U = [pad[v, x + 1] for v in range(5)]
-        XL = [pad[v, x] for v in range(5)]
-        XU = [pad[v, x + 2] for v in range(5)]
-        ZL = [pltpu.roll(U[v], 1, 0) for v in range(5)]
-        ZU = [pltpu.roll(U[v], z.R - 1, 0) for v in range(5)]
-        YL = [jnp.where(lane == 0, U[v], pltpu.roll(U[v], 1, 1)) for v in range(5)]
-        YU = [jnp.where(lane == LANES - 1, U[v], pltpu.roll(U[v], LANES - 1, 1)) for v in range(5)]
-        fx = [a - b for a, b in zip(state_flux(U, XU, 0), state_flux(XL, U, 0))]
-        fz = [a * zu - b * zd for a, b in zip(state_flux(U, ZU, 2), state_flux(ZL, U, 2))]
-        fy = [a * yu - b * yd for a, b in zip(state_flux(U, YU, 1), state_flux(YL, U, 1))]
-        for v in range(5):
-            value = U[v] - (0.5 * coarse_rate) * (fx[v] + fz[v] + fy[v])
-            out[v, x] = jnp.where(own > 0.0, value, 0.0)
+        U = [coarse[v, x] for v in range(5)]
+        vel, pressure, sound = derived(U)
+        last = jnp.minimum(x + 1, z.NX - 1)
+        XU = [coarse[v, last] for v in range(5)]
+        xvel, xp, xs = derived(XU)
+        fx = twice_flux(U, (vel[0], pressure, sound), XU, (xvel[0], xp, xs), 0)
+        inner = jnp.where(x < z.NX - 1, 1.0, 0.0)
+        D = [vel[1], pressure, sound]
+        move = lambda a: jnp.where(lane == LANES - 1, a, pltpu.roll(a, LANES - 1, 1))
+        fy = twice_flux(U, D, [move(a) for a in U], [move(a) for a in D], 1)
+        edge = twice_flux(U, D, U, D, 1)
+        D = [vel[2], pressure, sound]
+        move = lambda a: pltpu.roll(a, z.R - 1, 0)
+        fz = twice_flux(U, D, [move(a) for a in U], [move(a) for a in D], 2)
+        for v in range(5):
+            face = fx[v] * inner
+            below = jnp.where(x == 0, 0.0, pad[v])
+            pad[v] = face
+            ylow = jnp.where(lane == 0, edge[v], pltpu.roll(fy[v], 1, 1))
+            zlow = pltpu.roll(fz[v], 1, 0)
+            total = face - below + (fy[v] * yu - ylow * yd) + (fz[v] * zu - zlow * zd)
+            out[v, x] = jnp.where(own > 0.0, U[v] - (0.5 * coarse_rate) * total, 0.0)
         return carry
 
     lax.fori_loop(0, z.NX, layer, 0)
@@ -419,7 +431,8 @@
                 outf[k : k + z.own, :] = C[d * z.own : (d + 1) * z.own]
 
 
-def canvas_kernel(z, ids_s, columns_s, ids, columns, com, ghost, xc, avg, outc, canvas):
+def canvas_kernel(z, ids_s, columns_s, ids, columns, com, ghost, xc, avg, *rest):
+    outs, (canvas, ends) = rest[: z.n], rest[z.n :]
     S, f_of = z.S, z.P
     vx = 5 * z.xc
     _, gy, gz, gyr, gzr = positions(z, ids, columns)
@@ -448,20 +461,22 @@
     ).astype(jnp.bfloat16)
     in_y = lane // z.H == gy + 1
     in_z = lane // z.H == gz + 1
+    zq, yq = [], []
     for v in range(5):
         for x in range(z.xc):
-            k = v * z.xc + x
             r = (v * z.xa + 2 * x) * S
             Q = ghost[r : r + S, :] + ghost[r + S : r + 2 * S, :]
             Q = 0.125 * (Q + pltpu.roll(Q, LANES - 1, 1))
             got = [lanes_at(Q, f_of * f + 2 * (lane % z.H)) for f in range(4)]
-            zq = jnp.concatenate([jnp.where(in_y, got[f], 0.0) for f in (0, 1)], axis=0)
-            yq = jnp.concatenate([jnp.where(in_z, got[f], 0.0) for f in (2, 3)], axis=0)
-            total = select_dot(zmat, zq, 2)
-            for piece in parts(yq.T, 2):
-                total = total + jnp.dot(piece, ymat, preferred_element_type=jnp.float32)
-            canvas[k * z.NZ : (k + 1) * z.NZ, :] = total
-
+            zq.append(jnp.concatenate([jnp.where(in_y, got[f], 0.0) for f in (0, 1)], axis=0))
+            yq.append(jnp.concatenate([jnp.where(in_z, got[f], 0.0) for f in (2, 3)], axis=0))
+    zsum = select_dot(zmat, jnp.concatenate(zq, axis=1), 2)
+    ysum = None
+    for piece in parts(jnp.concatenate([a.T for a in yq], axis=0), 2):
+        term = jnp.dot(piece, ymat, preferred_element_type=jnp.float32)
+        ysum = term if ysum is None else ysum + term
+    for k in range(vx):
+        canvas[k * z.NZ : (k + 1) * z.NZ, :] = zsum[:, k * LANES : (k + 1) * LANES] + ysum[k * z.NZ : (k + 1) * z.NZ, :]
     rank = lax.broadcasted_iota(jnp.int32, (z.n, LANES), 0)
     rank_slot = lax.broadcasted_iota(jnp.int32, (z.n, S), 0)
     inside_y = in_y.astype(jnp.bfloat16)
@@ -498,75 +513,99 @@
                 canvas[rows, :] = canvas[rows, :] + jnp.where(inside, pltpu.roll(block, shift, 1), 0.0)
         return carry
 
-    lax.fori_loop(0, S, place, 0)
-    for d in range(z.n):
-        for k in range(vx):
-            outc[d * z.RK + k * z.R : d * z.RK + (k + 1) * z.R, :] = canvas[k * z.NZ + d * z.R : k * z.NZ + (d + 1) * z.R, :]
-
-
+    lax.fori_loop(0, S, place, 0, unroll=4)
     zb = (rank_slot // z.m == gzr + 1).astype(jnp.bfloat16)
+    tops = []
     for side in range(2):
         for v in range(5):
             C = xc[(side * 5 + v) * S : (side * 5 + v + 1) * S, :]
             Q = C + pltpu.roll(C, LANES - 1, 1)
             Q = 0.125 * (Q + pltpu.roll(Q, LANES - z.P, 1))
             for h in range(z.zcl):
-                got = jnp.where(in_y, lanes_at(Q, 2 * z.P * h + 2 * (lane % z.H)), 0.0)
-                outc[pl.ds(z.OXQ + (v * 2 + side) * z.zcl + h, z.n, stride=z.RK), :] = select_dot(zb, got, 2)
+                tops.append(jnp.where(in_y, lanes_at(Q, 2 * z.P * h + 2 * (lane % z.H)), 0.0))
+    tops = select_dot(zb, jnp.concatenate(tops, axis=1), 2)
+    for e in range(10 * z.zcl):
+        ends[e] = tops[:, e * LANES : (e + 1) * LANES]
+    rank = lax.axis_index("patch")
+    for k, out in enumerate(outs):
+        d = lax.rem(rank + k, z.n)
+        for e in range(vx):
+            out[e * z.R : (e + 1) * z.R, :] = canvas[pl.ds(pl.multiple_of(e * z.NZ + d * z.R, 8), z.R), :]
+        for e in range(10 * z.zcl):
+            out[z.OXQ + e : z.OXQ + e + 1, :] = ends[e, pl.ds(d, 1), :]
 
 
 def fine_kernel(z, updated, recv, out, scr):
+    q = pl.program_id(0)
     lane = lax.broadcasted_iota(jnp.int32, (z.P, LANES), 1)
     y = lane % z.P
     edge = (y == 0) | (y == z.P - 1)
     pick = jnp.where(y == 0, 2 * z.P, 3 * z.P) + lane // z.P
     for v in range(5):
-        for q in range(z.own):
-            for a in range(z.xa):
-                scr[q % 2, pl.ds(a, z.n, stride=z.xa), :] = recv[pl.ds((v * z.xa + a) * z.own + q, z.n, stride=z.RF), :]
-            face = scr[q % 2]
-            for g in range(z.G):
-                at = slice(g * LANES, (g + 1) * LANES)
-                add = jnp.where(edge, lanes_at(face, jnp.where(edge, pick + z.zg * g, 0)), 0.0)
-                if g == 0:
-                    add = add + jnp.where(lane < z.P, face, 0.0)
-                if g == z.G - 1:
-                    add = add + jnp.where(lane >= LANES - z.P, pltpu.roll(face, 2 * z.P, 1), 0.0)
-                out[v, q, :, at] = updated[v, q, :, at] + add
-            for side in range(2):
-                x = side * (z.P - 1)
-                for j in range(z.n):
-                    r = j * z.RF + z.OFX + (side * 5 + v) * z.own + q
-                    at = slice(j * z.PL, (j + 1) * z.PL)
-                    out[v, q, x : x + 1, at] = out[v, q, x : x + 1, at] + recv[r : r + 1, : z.PL]
-
-
-def coarse_kernel(z, prov, recv, out):
-    for j in range(z.n):
+        for a in range(z.xa):
+            scr[v % 2, pl.ds(a, z.n, stride=z.xa), :] = recv[pl.ds((v * z.xa + a) * z.own + q, z.n, stride=z.RF), :]
+        face = scr[v % 2]
+        for g in range(z.G):
+            at = slice(g * LANES, (g + 1) * LANES)
+            add = jnp.where(edge, lanes_at(face, jnp.where(edge, pick + z.zg * g, 0)), 0.0)
+            if g == 0:
+                add = add + jnp.where(lane < z.P, face, 0.0)
+            if g == z.G - 1:
+                add = add + jnp.where(lane >= LANES - z.P, pltpu.roll(face, 2 * z.P, 1), 0.0)
+            out[v, 0, :, at] = updated[v, q, :, at] + add
+        for side in range(2):
+            x = side * (z.P - 1)
+            for j in range(z.n):
+                r = j * z.RF + z.OFX + (side * 5 + v) * z.own + q
+                at = slice(j * z.PL, (j + 1) * z.PL)
+                out[v, 0, x : x + 1, at] = out[v, 0, x : x + 1, at] + recv[pl.ds(r, 1), : z.PL]
+
+
+def coarse_kernel(z, prov, bare, coarse, below, above, *rest):
+    recv, out = rest[: z.n], rest[z.n]
+    slab, rank = lax.axis_index("slab"), lax.axis_index("patch")
+    offset = lax.rem(rank, z.m) * z.R
+    for k in range(z.n):
+        j = lax.rem(rank + z.n - k, z.n)
         for v in range(5):
             for x in range(z.xc):
-                r = j * z.RK + (v * z.xc + x) * z.R
-                out[v, j * z.xc + x] = prov[v, j * z.xc + x] + recv[r : r + z.R, :]
-    offset = 0 if z.m == 1 else lax.rem(lax.axis_index("patch"), z.m) * z.R
-    for v in range(5):
-        for side in range(2):
-            x = side * (z.NX - 1)
-            for zl in range(z.R):
-                zc = zl + offset
-                r = (zc // z.zcl) * z.RK + z.OXQ + (v * 2 + side) * z.zcl + zc % z.zcl
-                out[v, x, zl : zl + 1, :] = out[v, x, zl : zl + 1, :] + recv[pl.ds(r, 1), :]
-
-
-def call(kernel, z, outs, ins, scratch=(), aliases=None):
+                r = (v * z.xc + x) * z.R
+                out[v, j * z.xc + x] = prov[v, j * z.xc + x] + recv[k][r : r + z.R, :]
+    for side, margin, edge in ((0, below, slab == 0), (1, above, slab == z.slabs - 1)):
+        x = side * (z.NX - 1)
+        own = [coarse[v, side] for v in range(5)]
+        far = [jnp.where(edge, own[v], margin[z.OM + v * z.R : z.OM + (v + 1) * z.R, :]) for v in range(5)]
+        F = state_flux(far, own, 0) if side == 0 else state_flux(own, far, 0)
+        scale = (0.5 if side == 0 else -0.5) * coarse_rate * bare[...]
+        for v in range(5):
+            out[v, x] = out[v, x] + scale * F[v]
+    for k in range(z.n):
+        j = lax.rem(rank + z.n - k, z.n)
+        for h in range(z.zcl):
+            row = j * z.zcl + h - offset
+            inside = (row >= 0) & (row < z.R)
+            row = jnp.clip(row, 0, z.R - 1)
+            for v in range(5):
+                for side in range(2):
+                    x = side * (z.NX - 1)
+                    r = z.OXQ + (side * 5 + v) * z.zcl + h
+                    add = jnp.where(inside, recv[k][r : r + 1, :], 0.0)
+                    out[v, x, pl.ds(row, 1), :] = out[v, x, pl.ds(row, 1), :] + add
+
+
+def held(a):
+    return pltpu.with_memory_space_constraint(a, pltpu.VMEM)
+
+
+def call(kernel, z, outs, ins, scratch=(), keep=True):
     return pl.pallas_call(
         functools.partial(kernel, z),
-        out_shape=[jax.ShapeDtypeStruct(s, jnp.float32) for s in outs],
+        out_shape=[pltpu.VMEM(s, jnp.float32) if keep else jax.ShapeDtypeStruct(s, jnp.float32) for s in outs],
         in_specs=[SMEM if space == "s" else VMEM for space, _ in ins],
         out_specs=[VMEM] * len(outs),
         scratch_shapes=[pltpu.VMEM(s, jnp.float32) for s in scratch],
-        input_output_aliases=aliases or {},
-        compiler_params=pltpu.CompilerParams(vmem_limit_bytes=56 * 1024 * 1024),
-    )(*[a for _, a in ins])
+        compiler_params=pltpu.CompilerParams(vmem_limit_bytes=VMEM_LIMIT),
+    )(*[held(a) if space == "p" else a for space, a in ins])
 
 
 def run_advance(z, fine):
@@ -575,16 +614,30 @@
     return pl.pallas_call(
         functools.partial(advance_kernel, z),
         grid=(z.own,),
-        out_shape=[jax.ShapeDtypeStruct(fine.shape, jnp.float32), jax.ShapeDtypeStruct(average, jnp.float32)],
+        out_shape=[pltpu.VMEM(fine.shape, jnp.float32), pltpu.VMEM(average, jnp.float32)],
         in_specs=[block],
-        out_specs=[block, pl.BlockSpec(average, lambda i: (0, 0))],
+        out_specs=[VMEM, VMEM],
         scratch_shapes=[
             pltpu.VMEM(s, jnp.float32)
             for s in ((10, z.G, z.P + 8, LANES), (5, z.P + 8, LANES), (5, z.P, LANES), (5, z.own * z.G, z.P, LANES))
         ],
-        compiler_params=pltpu.CompilerParams(vmem_limit_bytes=56 * 1024 * 1024),
+        compiler_params=pltpu.CompilerParams(vmem_limit_bytes=VMEM_LIMIT),
         name="advance",
     )(fine)
+
+
+def run_fine(z, updated, recv):
+    block = pl.BlockSpec((5, 1) + updated.shape[2:], lambda i: (0, i, 0, 0))
+    return pl.pallas_call(
+        functools.partial(fine_kernel, z),
+        grid=(z.own,),
+        out_shape=jax.ShapeDtypeStruct(updated.shape, jnp.float32),
+        in_specs=[VMEM, VMEM],
+        out_specs=block,
+        scratch_shapes=[pltpu.VMEM((2, z.P, LANES), jnp.float32)],
+        compiler_params=pltpu.CompilerParams(vmem_limit_bytes=VMEM_LIMIT),
+        name="fine_edges",
+    )(held(updated), held(recv))
 
 
 def local(n, slabs, coarse, fine, columns, patch_ids):
@@ -608,35 +661,39 @@
     com = exchange(com)
     updated, avg = run_advance(z, fine)
     avg = exchange(avg)
-    up, dn = call(pack_kernel, z, [(z.RP, LANES)] * 2, [("v", com), ("v", coarse), ("v", patch_ids)])
+    prov, bare, outer = call(
+        provisional_kernel,
+        z,
+        [coarse.shape, (z.R, LANES), (5, 2, z.R, LANES)],
+        [("v", columns), ("v", coarse)],
+        [(5, z.R, LANES)],
+    )
+    up, dn = call(pack_kernel, z, [(z.RP, LANES)] * 2, [("p", com), ("p", outer), ("v", patch_ids)])
     below = shifted(up, 1)
     above = shifted(dn, -1)
-    (ghost,) = call(side_kernel, z, [faces], [("v", a) for a in (patch_ids, columns, com)], [faces])
+    (ghost,) = call(side_kernel, z, [faces], [("v", patch_ids), ("v", columns), ("p", com)], [faces])
     outf, xc = call(
         end_kernel,
         z,
         [(n * z.RF, LANES), (10 * slots, LANES)],
-        [("v", a) for a in (patch_ids, columns, com, ghost, below, above)],
+        [("v", patch_ids), ("v", columns)] + [("p", a) for a in (com, ghost, below, above)],
         [(20 * slots, LANES)],
     )
     outf = exchange(outf)
-    (prov,) = call(
-        provisional_kernel,
-        z,
-        [coarse.shape],
-        [("s", columns), ("v", coarse), ("v", below), ("v", above)],
-        [(5, z.NX + 2, z.R, LANES)],
-    )
-    (outc,) = call(
+    pieces = list(call(
         canvas_kernel,
         z,
-        [(n * z.RK, LANES)],
-        [("s", patch_ids), ("s", columns)] + [("v", a) for a in (patch_ids, columns, com, ghost, xc, avg)],
-        [(5 * z.xc * z.NZ, LANES)],
+        [(z.RK, LANES)] * n,
+        [("s", patch_ids), ("s", columns), ("v", patch_ids), ("v", columns)]
+        + [("p", a) for a in (com, ghost, xc, avg)],
+        [(5 * z.xc * z.NZ, LANES), (10 * z.zcl, n, LANES)],
+    ))
+    for k in range(1, n):
+        pieces[k] = lax.ppermute(pieces[k], "patch", [(i, (i + k) % n) for i in range(n)])
+    fine_out = run_fine(z, updated, outf)
+    (coarse_out,) = call(
+        coarse_kernel, z, [coarse.shape], [("p", a) for a in (prov, bare, outer, below, above, *pieces)], keep=False
     )
-    outc = exchange(outc)
-    (fine_out,) = call(fine_kernel, z, [fine.shape], [("v", updated), ("v", outf)], [(2, z.P, LANES)])
-    (coarse_out,) = call(coarse_kernel, z, [coarse.shape], [("v", prov), ("v", outc)])
     return coarse_out, fine_out
 
 

time: 94.5 us -> 89 us (0.942)
  the two profiles are of different devices: /device:TPU:0 before, /device:TPU:19 now
where the time goes in v3:
time: 89 us; the launch traced here: 88.4 us
  starting transfers between devices  40.6 us (46%)
  Pallas kernels  25.1 us (28%)
  waiting for transfers between devices  13.2 us (15%)
  local copies, waits for them, and re-layouts  8.8 us (10%)
    all_to_all x3, starting transfers between devices, exchange(): return lax.all_to_all(a, 'patch', 0, 0, tiled=True)  18.4 us
    ppermute x7, starting transfers between devices, level_step(): lax.ppermute(pieces[k], 'patch', [(i, (i + k) % n) for i in range(n)])  16.2 us
    pallas_call x7, Pallas kernels, call(): pl.pallas_call(functools.partial(kernel, z), out_shape=[pltpu.VMEM(s, jnp...  11.5 us
    pallas_call x1, Pallas kernels, run_advance(): pl.pallas_call(functools.partial(advance_kernel, z), grid=(z.own,), out_s...  10.5 us
    unnamed x21, local copies, waits for them, and re-layouts  8.8 us
    ppermute x7, waiting for transfers between devices, level_step(): lax.ppermute(pieces[k], 'patch', [(i, (i + k) % n) for i in range(n)])  7.54 us
    ppermute x2, starting transfers between devices, shifted(): return lax.ppermute(a, 'slab', pairs)  6.01 us
    ppermute x2, waiting for transfers between devices, shifted(): return lax.ppermute(a, 'slab', pairs)  3.13 us
  transfers between devices with their start and end apart: 12, of which 7 were waited for; matrix products, arithmetic and copies ran while one was open for 0% of the time, Pallas kernels for 24%

profile of v3, /device:TPU:19, one launch (start us, length us, event | category | flops | bytes accessed | tf_op | source)
XLA Modules:
  0.0 88.4 jit_solution(2910741760572405925)
XLA Ops:
  0.6 1.7 %copy-done = f32[5,4,32,1024]{3,2,1,0:T(8,128)S(1)} copy-done((f32[5,4,32,1024]{3,2,1,0:T(8,128)S(1)}, f32[5,4,32,1024]{3,2,1,0:T(8,128)}, u32[]{:S(2)}) %copy-start) | copy-done | bytes 2621464
  2.4 1.1 %copy-done.5 = f32[5,16,16,128]{3,2,1,0:T(8,128)S(1)} copy-done((f32[5,16,16,128]{3,2,1,0:T(8,128)S(1)}, f32[5,16,16,128]{3,2,1,0:T(8,128)}, u32[]{:S(2)}) %copy-start.5) | copy-done | bytes 655384
  3.5 0.9 %shard_map.60 = f32[1408,128]{1,0:T(8,128)S(1)} custom-call(f32[5,4,32,1024]{3,2,1,0:T(8,128)S(1)} %copy-done, f32[5,16,16,128]{3,2,1,0:T(8,128)S(1)} %copy-done.5), custom_call_target="tpu_custom_call" | custom-call | tf_op jit(solution)/shard_map/pallas_call | solution.py:601
  4.4 0.8 copy-done.2
  5.3 5.7 %all-to-all-start = ((f32[8,176,128]{2,1,0:T(8,128)}), f32[8,176,128]{2,1,0:T(8,128)S(1)}, u32[]{:S(2)}, u32[]{:S(2)}) async-start(f32[8,176,128]{2,1,0:T(8,128)} %bitcast.10), calls=%async_computation | async-start | bytes 1441792 | tf_op jit(solution)/shard_map/all_to_all | solution.py:653
  10.9 10.5 %advance.1 = (f32[5,4,32,1024]{3,2,1,0:T(8,128)S(1)}, f32[640,128]{1,0:T(8,128)S(1)}) custom-call(f32[5,4,32,1024]{3,2,1,0:T(8,128)S(1)} %copy-done.1), custom_call_target="tpu_custom_call" | custom-call | tf_op jit(solution)/shard_map/advance/pallas_call | solution.py:614
  21.5 1.5 %copy-done.3 = f32[5,4,32,1024]{3,2,1,0:T(8,128)} copy-done((f32[5,4,32,1024]{3,2,1,0:T(8,128)}, f32[5,4,32,1024]{3,2,1,0:T(8,128)S(1)}, u32[]{:S(2)}) %copy-start.3) | copy-done | bytes 2621464
  22.9 0.7 copy-done.7
  23.7 2.5 %all-to-all-done = f32[8,176,128]{2,1,0:T(8,128)S(1)} async-done(((f32[8,176,128]{2,1,0:T(8,128)}), f32[8,176,128]{2,1,0:T(8,128)S(1)}, u32[]{:S(2)}, u32[]{:S(2)}) %all-to-all-start) | async-done | bytes 720928 | tf_op jit(solution)/shard_map/all_to_all | solution.py:653
  26.2 7.3 %all-to-all-start.1 = ((f32[8,80,128]{2,1,0:T(8,128)}), f32[8,80,128]{2,1,0:T(8,128)S(1)}, u32[]{:S(2)}, u32[]{:S(2)}) async-start(f32[8,80,128]{2,1,0:T(8,128)} %bitcast.13), calls=%async_computation.1 | async-start | bytes 655360 | tf_op jit(solution)/shard_map/all_to_all | solution.py:653
  33.5 0.1 copy.6.columns.columns_s
  33.6 1.1 %copy-done.6 = f32[5,16,16,128]{3,2,1,0:T(8,128)S(1)} copy-done((f32[5,16,16,128]{3,2,1,0:T(8,128)S(1)}, f32[5,16,16,128]{3,2,1,0:T(8,128)}, u32[]{:S(2)}) %copy-start.6) | copy-done | bytes 655384
  34.6 3.2 %shard_map.59 = (f32[5,16,16,128]{3,2,1,0:T(8,128)S(1)}, f32[16,128]{1,0:T(8,128)S(1)}, f32[5,2,16,128]{3,2,1,0:T(8,128)S(1)}) custom-call(s32[32,2]{1,0:T(8,128)S(1)} %copy.6.columns.columns_s, f32[5,16,16,128]{3,2,1,0:T(8,128)S(1)} %copy-done.6), custom_call_target="tpu_custom_call" | custom-call | tf_op jit(solution)/shard_map/pallas_call | solution.py:601
  37.9 4.1 %collective-permute-start = (f32[248,128]{1,0:T(8,128)S(1)}, f32[248,128]{1,0:T(8,128)S(1)}, u32[]{:S(2)}, u32[]{:S(2)}) collective-permute-start(f32[248,128]{1,0:T(8,128)S(1)} %get-tuple-element.22), channel_id=1, source_target_pairs={{0,8},{8,16},{16,24},{1,9},{9,17},{17,25},{2,10},{10,18},{18,26},{... | collective-permute-start | bytes 380936 | tf_op jit(solution)/shard_map/ppermute | solution.py:657
  42.0 1.9 %collective-permute-start.1 = (f32[248,128]{1,0:T(8,128)S(1)}, f32[248,128]{1,0:T(8,128)S(1)}, u32[]{:S(2)}, u32[]{:S(2)}) collective-permute-start(f32[248,128]{1,0:T(8,128)S(1)} %get-tuple-element.23), channel_id=1, source_target_pairs={{8,0},{16,8},{24,16},{9,1},{17,9},{25,17},{10,2},{18,10},{26,18},{... | collective-permute-start | bytes 380936 | tf_op jit(solution)/shard_map/ppermute | solution.py:657
  43.9 1.2 %shard_map.62.ghost = f32[640,128]{1,0:T(8,128)S(1)} custom-call(s32[1,32]{1,0:T(1,128)S(1)} %copy-done.8, s32[32,2]{1,0:T(8,128)S(1)} %copy.6.columns.columns_s, f32[1408,128]{1,0:T(8,128)S(1)} %bitcast.7), custom_call_target="tpu_custom_call" | custom-call | tf_op jit(solution)/shard_map/pallas_call | solution.py:601
  45.1 3.1 %collective-permute-done.1.above = f32[248,128]{1,0:T(8,128)S(1)} collective-permute-done((f32[248,128]{1,0:T(8,128)S(1)}, f32[248,128]{1,0:T(8,128)S(1)}, u32[]{:S(2)}, u32[]{:S(2)}) %collective-permute-start.1) | collective-permute-done | bytes 127008 | tf_op jit(solution)/shard_map/ppermute | solution.py:657
  48.2 1.2 %shard_map.63 = (f32[960,128]{1,0:T(8,128)}, f32[320,128]{1,0:T(8,128)S(1)}) custom-call(s32[1,32]{1,0:T(1,128)S(1)} %copy-done.8, s32[32,2]{1,0:T(8,128)S(1)} %copy.6.columns.columns_s, f32[1408,128]{1,0:T(8,128)S(1)} %bitcast.8, f32[640,128]{1,0:T(8,128)S(1)} %shard_map.62.ghost, f32[248,128]{1,0:T(8,128)S(1)} %collective-permute-done.below, ...), custom_call_target="tpu_custom_call" | custom-call | tf_op jit(solution)/shard_map/pallas_call | solution.py:601
  49.4 5.4 %all-to-all-start.2 = ((f32[8,120,128]{2,1,0:T(8,128)}), f32[8,120,128]{2,1,0:T(8,128)S(1)}, u32[]{:S(2)}, u32[]{:S(2)}) async-start(f32[8,120,128]{2,1,0:T(8,128)} %bitcast.4), calls=%async_computation.2 | async-start | bytes 983040 | tf_op jit(solution)/shard_map/all_to_all | solution.py:653
  54.8 3.9 %shard_map.64 = (f32[184,128]{1,0:T(8,128)S(1)}, f32[184,128]{1,0:T(8,128)S(1)}, f32[184,128]{1,0:T(8,128)S(1)}, f32[184,128]{1,0:T(8,128)S(1)}, f32[184,128]{1,...) custom-call(s32[1,32]{1,0:T(1,128)S(1)} %copy-done.8, ...), custom_call_target="tpu_custom_call" | custom-call | tf_op jit(solution)/shard_map/pallas_call | solution.py:601
  58.7 1.2 %collective-permute-start.2 = (f32[184,128]{1,0:T(8,128)S(1)}, f32[184,128]{1,0:T(8,128)S(1)}, u32[]{:S(2)}, u32[]{:S(2)}) collective-permute-start(f32[184,128]{1,0:T(8,128)S(1)} %get-tuple-element.27), channel_id=1, source_target_pairs={{0,1},{1,2},{2,3},{3,4},{4,5},{5,6},{6,7},{7,0},{8,9},{9,10},{10,1... | collective-permute-start | bytes 282632 | tf_op jit(solution)/shard_map/ppermute | solution.py:692
  60.0 1.4 %collective-permute-start.4 = (f32[184,128]{1,0:T(8,128)S(1)}, f32[184,128]{1,0:T(8,128)S(1)}, u32[]{:S(2)}, u32[]{:S(2)}) collective-permute-start(f32[184,128]{1,0:T(8,128)S(1)} %get-tuple-element.29), channel_id=1, source_target_pairs={{0,3},{1,4},{2,5},{3,6},{4,7},{5,0},{6,1},{7,2},{8,11},{9,12},{10,... | collective-permute-start | bytes 282632 | tf_op jit(solution)/shard_map/ppermute | solution.py:692
  61.4 2.1 %collective-permute-start.5 = (f32[184,128]{1,0:T(8,128)S(1)}, f32[184,128]{1,0:T(8,128)S(1)}, u32[]{:S(2)}, u32[]{:S(2)}) collective-permute-start(f32[184,128]{1,0:T(8,128)S(1)} %get-tuple-element.30), channel_id=1, source_target_pairs={{0,4},{1,5},{2,6},{3,7},{4,0},{5,1},{6,2},{7,3},{8,12},{9,13},{10,... | collective-permute-start | bytes 282632 | tf_op jit(solution)/shard_map/ppermute | solution.py:692
  63.5 1.2 %collective-permute-start.6 = (f32[184,128]{1,0:T(8,128)S(1)}, f32[184,128]{1,0:T(8,128)S(1)}, u32[]{:S(2)}, u32[]{:S(2)}) collective-permute-start(f32[184,128]{1,0:T(8,128)S(1)} %get-tuple-element.31), channel_id=1, source_target_pairs={{0,5},{1,6},{2,7},{3,0},{4,1},{5,2},{6,3},{7,4},{8,13},{9,14},{10,... | collective-permute-start | bytes 282632 | tf_op jit(solution)/shard_map/ppermute | solution.py:692
  64.7 10.2 %collective-permute-start.7 = (f32[184,128]{1,0:T(8,128)S(1)}, f32[184,128]{1,0:T(8,128)S(1)}, u32[]{:S(2)}, u32[]{:S(2)}) collective-permute-start(f32[184,128]{1,0:T(8,128)S(1)} %get-tuple-element.32), channel_id=1, source_target_pairs={{0,6},{1,7},{2,0},{3,1},{4,2},{5,3},{6,4},{7,5},{8,14},{9,15},{10,... | collective-permute-start | bytes 282632 | tf_op jit(solution)/shard_map/ppermute | solution.py:692
  74.9 2.5 %collective-permute-done.3.rest_2_ = f32[184,128]{1,0:T(8,128)S(1)} collective-permute-done((f32[184,128]{1,0:T(8,128)S(1)}, f32[184,128]{1,0:T(8,128)S(1)}, u32[]{:S(2)}, u32[]{:S(2)}) %collective-permute-start.3) | collective-permute-done | bytes 94240 | tf_op jit(solution)/shard_map/ppermute | solution.py:692
  77.5 1.4 %collective-permute-done.6.rest_5_ = f32[184,128]{1,0:T(8,128)S(1)} collective-permute-done((f32[184,128]{1,0:T(8,128)S(1)}, f32[184,128]{1,0:T(8,128)S(1)}, u32[]{:S(2)}, u32[]{:S(2)}) %collective-permute-start.6) | collective-permute-done | bytes 94240 | tf_op jit(solution)/shard_map/ppermute | solution.py:692
  78.9 1.0 %collective-permute-done.7.rest_6_ = f32[184,128]{1,0:T(8,128)S(1)} collective-permute-done((f32[184,128]{1,0:T(8,128)S(1)}, f32[184,128]{1,0:T(8,128)S(1)}, u32[]{:S(2)}, u32[]{:S(2)}) %collective-permute-start.7) | collective-permute-done | bytes 94240 | tf_op jit(solution)/shard_map/ppermute | solution.py:692
  80.0 2.5 %collective-permute-done.8.rest_7_ = f32[184,128]{1,0:T(8,128)S(1)} collective-permute-done((f32[184,128]{1,0:T(8,128)S(1)}, f32[184,128]{1,0:T(8,128)S(1)}, u32[]{:S(2)}, u32[]{:S(2)}) %collective-permute-start.8) | collective-permute-done | bytes 94240 | tf_op jit(solution)/shard_map/ppermute | solution.py:692
  82.5 1.1 %shard_map.65 = f32[5,16,16,128]{3,2,1,0:T(8,128)} custom-call(f32[5,16,16,128]{3,2,1,0:T(8,128)S(1)} %get-tuple-element.19.prov, f32[16,128]{1,0:T(8,128)S(1)} %get-tuple-element.20.bare, f32[5,2,16,128]{3,2,1,0:T(8,128)S(1)} %get-tuple-element.21.outer.coarse, f32[248,128]{1,0:T(8,128)S(1)} %collective-permute-done.below, ...), custom_call_target="tpu_custom_call" | custom-call | tf_op jit(solution)/shard_map/pallas_call | solution.py:601
  83.6 1.7 %copy-done.4 = f32[5,4,32,1024]{3,2,1,0:T(8,128)S(1)} copy-done((f32[5,4,32,1024]{3,2,1,0:T(8,128)S(1)}, f32[5,4,32,1024]{3,2,1,0:T(8,128)}, u32[]{:S(2)}) %copy-start.4) | copy-done | bytes 2621464
  85.3 3.1 %fine_edges.1 = f32[5,4,32,1024]{3,2,1,0:T(8,128)} custom-call(f32[5,4,32,1024]{3,2,1,0:T(8,128)S(1)} %copy-done.4, f32[960,128]{1,0:T(8,128)S(1)} %bitcast.11), custom_call_target="tpu_custom_call" | custom-call | tf_op jit(solution)/shard_map/fine_edges/pallas_call | solution.py:631
  (22 shorter events, 0.2 us)
Async XLA Ops:
  0.6 1.7 %copy-start = (f32[5,4,32,1024]{3,2,1,0:T(8,128)S(1)}, f32[5,4,32,1024]{3,2,1,0:T(8,128)}, u32[]{:S(2)}) copy-start(f32[5,4,32,1024]{3,2,1,0:T(8,128)} %fine.3) | copy-start | bytes 7864324
  2.4 1.1 %copy-start.5 = (f32[5,16,16,128]{3,2,1,0:T(8,128)S(1)}, f32[5,16,16,128]{3,2,1,0:T(8,128)}, u32[]{:S(2)}) copy-start(f32[5,16,16,128]{3,2,1,0:T(8,128)} %coarse.3) | copy-start | bytes 1966084
  3.5 7.5 %copy-start.1 = (f32[5,4,32,1024]{3,2,1,0:T(8,128)S(1)}, f32[5,4,32,1024]{3,2,1,0:T(8,128)}, u32[]{:S(2)}) copy-start(f32[5,4,32,1024]{3,2,1,0:T(8,128)} %fine.3) | copy-start | bytes 7864324
  4.4 0.9 copy-start.2
  5.3 28.2 %copy-start.9 = (s32[32,2]{0,1:T(2,128)S(1)}, s32[32,2]{0,1:T(2,128)}, u32[]{:S(2)}) copy-start(s32[32,2]{0,1:T(2,128)} %param.6) | copy-start | bytes 772
  5.3 32.6 %copy-start.8 = (s32[1,32]{1,0:T(1,128)S(1)}, s32[1,32]{1,0:T(1,128)}, u32[]{:S(2)}) copy-start(s32[1,32]{1,0:T(1,128)} %ids.7) | copy-start | bytes 388
  5.3 20.9 %all-to-all-start = ((f32[8,176,128]{2,1,0:T(8,128)}), f32[8,176,128]{2,1,0:T(8,128)S(1)}, u32[]{:S(2)}, u32[]{:S(2)}) async-start(f32[8,176,128]{2,1,0:T(8,128)} %bitcast.10), calls=%async_computation | async-start | bytes 1441792 | tf_op jit(solution)/shard_map/all_to_all | solution.py:653
  21.4 1.5 %copy-start.3 = (f32[5,4,32,1024]{3,2,1,0:T(8,128)}, f32[5,4,32,1024]{3,2,1,0:T(8,128)S(1)}, u32[]{:S(2)}) copy-start(f32[5,4,32,1024]{3,2,1,0:T(8,128)S(1)} %get-tuple-element.34.updated) | copy-start | bytes 7864324
  22.9 0.7 copy-start.7
  26.2 23.2 %all-to-all-start.1 = ((f32[8,80,128]{2,1,0:T(8,128)}), f32[8,80,128]{2,1,0:T(8,128)S(1)}, u32[]{:S(2)}, u32[]{:S(2)}) async-start(f32[8,80,128]{2,1,0:T(8,128)} %bitcast.13), calls=%async_computation.1 | async-start | bytes 655360 | tf_op jit(solution)/shard_map/all_to_all | solution.py:653
  33.6 1.1 %copy-start.6 = (f32[5,16,16,128]{3,2,1,0:T(8,128)S(1)}, f32[5,16,16,128]{3,2,1,0:T(8,128)}, u32[]{:S(2)}) copy-start(f32[5,16,16,128]{3,2,1,0:T(8,128)} %coarse.3) | copy-start | bytes 1966084
  37.9 7.2 %collective-permute-start = (f32[248,128]{1,0:T(8,128)S(1)}, f32[248,128]{1,0:T(8,128)S(1)}, u32[]{:S(2)}, u32[]{:S(2)}) collective-permute-start(f32[248,128]{1,0:T(8,128)S(1)} %get-tuple-element.22), channel_id=1, source_target_pairs={{0,8},{8,16},{16,24},{1,9},{9,17},{17,25},{2,10},{10,18},{18,26},{... | collective-permute-start | bytes 380936 | tf_op jit(solution)/shard_map/ppermute | solution.py:657
  42.0 6.2 %collective-permute-start.1 = (f32[248,128]{1,0:T(8,128)S(1)}, f32[248,128]{1,0:T(8,128)S(1)}, u32[]{:S(2)}, u32[]{:S(2)}) collective-permute-start(f32[248,128]{1,0:T(8,128)S(1)} %get-tuple-element.23), channel_id=1, source_target_pairs={{8,0},{16,8},{24,16},{9,1},{17,9},{25,17},{10,2},{18,10},{26,18},{... | collective-permute-start | bytes 380936 | tf_op jit(solution)/shard_map/ppermute | solution.py:657
  49.4 34.2 %all-to-all-start.2 = ((f32[8,120,128]{2,1,0:T(8,128)}), f32[8,120,128]{2,1,0:T(8,128)S(1)}, u32[]{:S(2)}, u32[]{:S(2)}) async-start(f32[8,120,128]{2,1,0:T(8,128)} %bitcast.4), calls=%async_computation.2 | async-start | bytes 983040 | tf_op jit(solution)/shard_map/all_to_all | solution.py:653
  58.7 6.0 %collective-permute-start.2 = (f32[184,128]{1,0:T(8,128)S(1)}, f32[184,128]{1,0:T(8,128)S(1)}, u32[]{:S(2)}, u32[]{:S(2)}) collective-permute-start(f32[184,128]{1,0:T(8,128)S(1)} %get-tuple-element.27), channel_id=1, source_target_pairs={{0,1},{1,2},{2,3},{3,4},{4,5},{5,6},{6,7},{7,0},{8,9},{9,10},{10,1... | collective-permute-start | bytes 282632 | tf_op jit(solution)/shard_map/ppermute | solution.py:692
  60.0 17.4 %collective-permute-start.3 = (f32[184,128]{1,0:T(8,128)S(1)}, f32[184,128]{1,0:T(8,128)S(1)}, u32[]{:S(2)}, u32[]{:S(2)}) collective-permute-start(f32[184,128]{1,0:T(8,128)S(1)} %get-tuple-element.28), channel_id=1, source_target_pairs={{0,2},{1,3},{2,4},{3,5},{4,6},{5,7},{6,0},{7,1},{8,10},{9,11},{10,... | collective-permute-start | bytes 282632 | tf_op jit(solution)/shard_map/ppermute | solution.py:692
  60.0 17.4 %collective-permute-start.4 = (f32[184,128]{1,0:T(8,128)S(1)}, f32[184,128]{1,0:T(8,128)S(1)}, u32[]{:S(2)}, u32[]{:S(2)}) collective-permute-start(f32[184,128]{1,0:T(8,128)S(1)} %get-tuple-element.29), channel_id=1, source_target_pairs={{0,3},{1,4},{2,5},{3,6},{4,7},{5,0},{6,1},{7,2},{8,11},{9,12},{10,... | collective-permute-start | bytes 282632 | tf_op jit(solution)/shard_map/ppermute | solution.py:692
  61.4 16.0 %collective-permute-start.5 = (f32[184,128]{1,0:T(8,128)S(1)}, f32[184,128]{1,0:T(8,128)S(1)}, u32[]{:S(2)}, u32[]{:S(2)}) collective-permute-start(f32[184,128]{1,0:T(8,128)S(1)} %get-tuple-element.30), channel_id=1, source_target_pairs={{0,4},{1,5},{2,6},{3,7},{4,0},{5,1},{6,2},{7,3},{8,12},{9,13},{10,... | collective-permute-start | bytes 282632 | tf_op jit(solution)/shard_map/ppermute | solution.py:692
  63.5 15.4 %collective-permute-start.6 = (f32[184,128]{1,0:T(8,128)S(1)}, f32[184,128]{1,0:T(8,128)S(1)}, u32[]{:S(2)}, u32[]{:S(2)}) collective-permute-start(f32[184,128]{1,0:T(8,128)S(1)} %get-tuple-element.31), channel_id=1, source_target_pairs={{0,5},{1,6},{2,7},{3,0},{4,1},{5,2},{6,3},{7,4},{8,13},{9,14},{10,... | collective-permute-start | bytes 282632 | tf_op jit(solution)/shard_map/ppermute | solution.py:692
  64.7 15.2 %collective-permute-start.7 = (f32[184,128]{1,0:T(8,128)S(1)}, f32[184,128]{1,0:T(8,128)S(1)}, u32[]{:S(2)}, u32[]{:S(2)}) collective-permute-start(f32[184,128]{1,0:T(8,128)S(1)} %get-tuple-element.32), channel_id=1, source_target_pairs={{0,6},{1,7},{2,0},{3,1},{4,2},{5,3},{6,4},{7,5},{8,14},{9,15},{10,... | collective-permute-start | bytes 282632 | tf_op jit(solution)/shard_map/ppermute | solution.py:692
  77.4 5.1 %collective-permute-start.8 = (f32[184,128]{1,0:T(8,128)S(1)}, f32[184,128]{1,0:T(8,128)S(1)}, u32[]{:S(2)}, u32[]{:S(2)}) collective-permute-start(f32[184,128]{1,0:T(8,128)S(1)} %get-tuple-element.33), channel_id=1, source_target_pairs={{0,7},{1,0},{2,1},{3,2},{4,3},{5,4},{6,5},{7,6},{8,15},{9,8},{10,9... | collective-permute-start | bytes 282632 | tf_op jit(solution)/shard_map/ppermute | solution.py:692
  83.6 1.7 %copy-start.4 = (f32[5,4,32,1024]{3,2,1,0:T(8,128)S(1)}, f32[5,4,32,1024]{3,2,1,0:T(8,128)}, u32[]{:S(2)}) copy-start(f32[5,4,32,1024]{3,2,1,0:T(8,128)} %copy-done.3) | copy-start | bytes 7864324

commit v4 on v3

--- a/solution.py
+++ b/solution.py
@@ -42,9 +42,12 @@
         assert self.NX == self.H and self.NY == LANES and self.H % self.R == 0
         assert self.P % (2 * n) == 0 and 4 * self.P == LANES and slots == self.own * n
         self.lat = 5 * self.xa * self.own
-        self.ny = -(-(5 * self.xc * self.R) // LANES)
+        self.width = 5 * self.xc * self.R
+        self.tail = max(self.width - LANES, 0)
+        assert 4 * self.tail in (0, LANES)
         self.OY = up8(self.lat)
-        self.OZ = self.OY + self.lines * self.ny
+        self.OT = self.OY + self.lines
+        self.OZ = self.OT + (self.lines // 4 if self.tail else 0)
         self.OX = self.OZ + 10 * self.xc
         self.RC = up8(self.OX + 10 * self.own)
         self.OM = up8(n * 5 * self.own)
@@ -142,15 +145,21 @@
     line = lax.broadcasted_iota(jnp.int32, (z.lines, LANES), 0)
     at = lax.broadcasted_iota(jnp.int32, (z.lines, LANES), 1)
     chosen = (at == z.H * (line // 2) + (z.H - 1) * (line % 2)).astype(jnp.bfloat16)
-    width = 5 * z.xc * z.R
+    quarter = z.lines // 4
+    target = lax.broadcasted_iota(jnp.int32, (quarter, LANES), 1) // (LANES // 4)
     for j in range(z.n):
-        block = coarse[:, j * z.xc : (j + 1) * z.xc].reshape(width, LANES)
+        block = coarse[:, j * z.xc : (j + 1) * z.xc].reshape(z.width, LANES)
+        if z.tail:
+            block = jnp.concatenate([block, jnp.zeros((2 * LANES - z.width, LANES), jnp.float32)], axis=0)
         lines = select_dot(chosen, block, 3, (((1,), (1,)), ((), ())))
-        for t in range(z.ny):
-            extent = min(LANES, width - t * LANES)
-            com[j * z.RC + z.OY + t * z.lines : j * z.RC + z.OY + (t + 1) * z.lines, :extent] = lines[
-                :, t * LANES : t * LANES + extent
-            ]
+        extent = min(LANES, z.width)
+        com[j * z.RC + z.OY : j * z.RC + z.OY + z.lines, :extent] = lines[:, :extent]
+        if z.tail:
+            packed = jnp.zeros((quarter, LANES), jnp.float32)
+            for b in range(4):
+                moved = pltpu.roll(lines[:, LANES:], b * z.tail, 1)[b * quarter : (b + 1) * quarter]
+                packed = jnp.where(target == b, moved, packed)
+            com[j * z.RC + z.OT : j * z.RC + z.OT + quarter, :] = packed
         for v in range(5):
             for x in range(z.xc):
                 row = j * z.RC + z.OZ + (v * z.xc + x) * 2
@@ -351,13 +360,16 @@
     y_index = z.H * (gy + 1) + (lane % f_of) // 2
     half = (lane % f_of) // 2
     y_rows = {}
-    for t in range(z.ny):
-        table = jnp.concatenate(
-            [com[i * z.RC + z.OY + t * z.lines : i * z.RC + z.OY + (t + 1) * z.lines, :] for i in range(z.n)], axis=0
-        )
-        for h in range(z.m):
-            for f, line in ((2, 2 * gy + 1), (3, 2 * (gy + 2))):
-                y_rows[t, h, f] = select_dot(onehot(((gz + 1) * z.m + h) * z.lines + line, z.n * z.lines), table)
+    sides = ((2, 2 * gy + 1), (3, 2 * (gy + 2)))
+    table = jnp.concatenate([com[i * z.RC + z.OY : i * z.RC + z.OY + z.lines, :] for i in range(z.n)], axis=0)
+    rest = jnp.concatenate([com[i * z.RC + z.OT : i * z.RC + z.OT + 8, :] for i in range(z.n)], axis=0)
+    quarter = z.lines // 4
+    for h in range(z.m):
+        for f, line in sides:
+            source = (gz + 1) * z.m + h
+            y_rows[0, h, f] = select_dot(onehot(source * z.lines + line, z.n * z.lines), table)
+            if z.tail:
+                y_rows[1, h, f] = select_dot(onehot(source * 8 + line % quarter, z.n * 8), rest)
     for v in range(5):
         swapped = []
         for a in range(z.xa):
@@ -370,9 +382,10 @@
             at = slice(k * LANES, (k + 1) * LANES)
             c = jnp.where(kind == 0, lanes_at(low_rows[:, at], y_index), lanes_at(top_rows[:, at], y_index))
             start = k * z.R
-            for f in (2, 3):
+            for f, line in sides:
+                base = start if start < LANES else start - LANES + (line // quarter) * z.tail
                 for h in range(z.m):
-                    got = lanes_at(y_rows[start // LANES, h, f], start % LANES + half % z.R)
+                    got = lanes_at(y_rows[start // LANES, h, f], base + half % z.R)
                     c = jnp.where((kind == f) & (half // z.R == h), got, c)
             for a in (2 * x, 2 * x + 1):
                 ghost[(v * z.xa + a) * S : (v * z.xa + a + 1) * S, :] = jnp.where(
@@ -593,19 +606,19 @@
                     out[v, x, pl.ds(row, 1), :] = out[v, x, pl.ds(row, 1), :] + add
 
 
-def held(a):
-    return pltpu.with_memory_space_constraint(a, pltpu.VMEM)
-
-
-def call(kernel, z, outs, ins, scratch=(), keep=True):
+def held(a, space=pltpu.VMEM):
+    return pltpu.with_memory_space_constraint(a, space)
+
+
+def call(kernel, z, outs, ins, scratch=(), keep=pltpu.VMEM):
     return pl.pallas_call(
         functools.partial(kernel, z),
-        out_shape=[pltpu.VMEM(s, jnp.float32) if keep else jax.ShapeDtypeStruct(s, jnp.float32) for s in outs],
+        out_shape=[keep(s, jnp.float32) for s in outs],
         in_specs=[SMEM if space == "s" else VMEM for space, _ in ins],
         out_specs=[VMEM] * len(outs),
         scratch_shapes=[pltpu.VMEM(s, jnp.float32) for s in scratch],
         compiler_params=pltpu.CompilerParams(vmem_limit_bytes=VMEM_LIMIT),
-    )(*[held(a) if space == "p" else a for space, a in ins])
+    )(*[{"p": held(a), "h": held(a, pltpu.HBM)}.get(space, a) for space, a in ins])
 
 
 def run_advance(z, fine):
@@ -614,9 +627,9 @@
     return pl.pallas_call(
         functools.partial(advance_kernel, z),
         grid=(z.own,),
-        out_shape=[pltpu.VMEM(fine.shape, jnp.float32), pltpu.VMEM(average, jnp.float32)],
+        out_shape=[pltpu.VMEM(fine.shape, jnp.float32), pltpu.HBM(average, jnp.float32)],
         in_specs=[block],
-        out_specs=[VMEM, VMEM],
+        out_specs=[VMEM, pl.BlockSpec(average, lambda i: (0, 0))],
         scratch_shapes=[
             pltpu.VMEM(s, jnp.float32)
             for s in ((10, z.G, z.P + 8, LANES), (5, z.P + 8, LANES), (5, z.P, LANES), (5, z.own * z.G, z.P, LANES))
@@ -657,7 +670,9 @@
         return lax.ppermute(a, "slab", pairs)
 
     faces = (5 * z.xa * slots, LANES)
-    (com,) = call(extract_kernel, z, [(n * z.RC, LANES)], [("v", fine), ("v", coarse)], [(2, z.P, LANES)])
+    (com,) = call(
+        extract_kernel, z, [(n * z.RC, LANES)], [("h", fine), ("h", coarse)], [(2, z.P, LANES)], keep=pltpu.HBM
+    )
     com = exchange(com)
     updated, avg = run_advance(z, fine)
     avg = exchange(avg)
@@ -692,7 +707,11 @@
         pieces[k] = lax.ppermute(pieces[k], "patch", [(i, (i + k) % n) for i in range(n)])
     fine_out = run_fine(z, updated, outf)
     (coarse_out,) = call(
-        coarse_kernel, z, [coarse.shape], [("p", a) for a in (prov, bare, outer, below, above, *pieces)], keep=False
+        coarse_kernel,
+        z,
+        [coarse.shape],
+        [("p", a) for a in (prov, bare, outer, below, above, *pieces)],
+        keep=jax.ShapeDtypeStruct,
     )
     return coarse_out, fine_out
 

time: 89 us -> 86.8 us (0.975)
  local copies, waits for them, and re-layouts: 8.8 us -> 4.42 us
  Pallas kernels: 25.1 us -> 28.7 us
  waiting for transfers between devices: 13.2 us -> 11.9 us
    unnamed x21 -> x13, local copies, waits for them, and re-layouts: 8.8 us -> 4.42 us
    pallas_call x7, Pallas kernels: 11.5 us -> 14.4 us  [call(): pl.pallas_call(functools.partial(kernel, z), out_shape=[keep(s, jnp.float...]
    all_to_all x3, waiting for transfers between devices: 2.55 us -> 1.16 us  [exchange(): return lax.all_to_all(a, 'patch', 0, 0, tiled=True)]
  transfers between devices with their start and end apart: 12 -> 12, of which waited for: 7 -> 7; matrix products, arithmetic and copies ran while one was open for 0% -> 0% of each run, Pallas kernels for 24% -> 25%
where the time goes in v4:
time: 86.8 us; the launch traced here: 86.3 us
  starting transfers between devices  40.6 us (47%)
  Pallas kernels  28.7 us (33%)
  waiting for transfers between devices  11.9 us (14%)
  local copies, waits for them, and re-layouts  4.42 us (5%)
    all_to_all x3, starting transfers between devices, exchange(): return lax.all_to_all(a, 'patch', 0, 0, tiled=True)  18.4 us
    ppermute x7, starting transfers between devices, level_step(): lax.ppermute(pieces[k], 'patch', [(i, (i + k) % n) for i in range(n)])  16.2 us
    pallas_call x7, Pallas kernels, call(): pl.pallas_call(functools.partial(kernel, z), out_shape=[keep(s, jnp.float...  14.4 us
    pallas_call x1, Pallas kernels, run_advance(): pl.pallas_call(functools.partial(advance_kernel, z), grid=(z.own,), out_s...  11.2 us
    ppermute x7, waiting for transfers between devices, level_step(): lax.ppermute(pieces[k], 'patch', [(i, (i + k) % n) for i in range(n)])  7.54 us
    ppermute x2, starting transfers between devices, shifted(): return lax.ppermute(a, 'slab', pairs)  6.01 us
    unnamed x13, local copies, waits for them, and re-layouts  4.42 us
    ppermute x2, waiting for transfers between devices, shifted(): return lax.ppermute(a, 'slab', pairs)  3.18 us
  transfers between devices with their start and end apart: 12, of which 7 were waited for; matrix products, arithmetic and copies ran while one was open for 0% of the time, Pallas kernels for 25%

profile of v4, /device:TPU:19, one launch (start us, length us, event | category | flops | bytes accessed | tf_op | source)
XLA Modules:
  0.0 86.3 jit_solution(7907175415165779314)
XLA Ops:
  0.6 3.9 %shard_map.60 = f32[1280,128]{1,0:T(8,128)} custom-call(f32[5,4,32,1024]{3,2,1,0:T(8,128)} %fine.3, f32[5,16,16,128]{3,2,1,0:T(8,128)} %coarse.3), custom_call_target="tpu_custom_call" | custom-call | tf_op jit(solution)/shard_map/pallas_call | solution.py:614
  4.6 5.7 %all-to-all-start = ((f32[8,160,128]{2,1,0:T(8,128)}), f32[8,160,128]{2,1,0:T(8,128)S(1)}, u32[]{:S(2)}, u32[]{:S(2)}) async-start(f32[8,160,128]{2,1,0:T(8,128)} %bitcast.12), calls=%async_computation | async-start | bytes 1310720 | tf_op jit(solution)/shard_map/all_to_all | solution.py:666
  10.2 11.2 %advance.1 = (f32[5,4,32,1024]{3,2,1,0:T(8,128)S(1)}, f32[640,128]{1,0:T(8,128)}) custom-call(f32[5,4,32,1024]{3,2,1,0:T(8,128)S(1)} %copy-done), custom_call_target="tpu_custom_call" | custom-call | tf_op jit(solution)/shard_map/advance/pallas_call | solution.py:627
  21.5 1.5 %copy-done.1 = f32[5,4,32,1024]{3,2,1,0:T(8,128)} copy-done((f32[5,4,32,1024]{3,2,1,0:T(8,128)}, f32[5,4,32,1024]{3,2,1,0:T(8,128)S(1)}, u32[]{:S(2)}) %copy-start.1) | copy-done | bytes 2621464
  22.9 1.2 %all-to-all-done = f32[8,160,128]{2,1,0:T(8,128)S(1)} async-done(((f32[8,160,128]{2,1,0:T(8,128)}), f32[8,160,128]{2,1,0:T(8,128)S(1)}, u32[]{:S(2)}, u32[]{:S(2)}) %all-to-all-start) | async-done | bytes 655392 | tf_op jit(solution)/shard_map/all_to_all | solution.py:666
  24.1 7.3 %all-to-all-start.1 = ((f32[8,80,128]{2,1,0:T(8,128)}), f32[8,80,128]{2,1,0:T(8,128)S(1)}, u32[]{:S(2)}, u32[]{:S(2)}) async-start(f32[8,80,128]{2,1,0:T(8,128)} %bitcast.13), calls=%async_computation.1 | async-start | bytes 655360 | tf_op jit(solution)/shard_map/all_to_all | solution.py:666
  31.4 0.1 copy.6.columns.columns_s
  31.4 1.1 %copy-done.3 = f32[5,16,16,128]{3,2,1,0:T(8,128)S(1)} copy-done((f32[5,16,16,128]{3,2,1,0:T(8,128)S(1)}, f32[5,16,16,128]{3,2,1,0:T(8,128)}, u32[]{:S(2)}) %copy-start.3) | copy-done | bytes 655384
  32.5 3.2 %shard_map.59 = (f32[5,16,16,128]{3,2,1,0:T(8,128)S(1)}, f32[16,128]{1,0:T(8,128)S(1)}, f32[5,2,16,128]{3,2,1,0:T(8,128)S(1)}) custom-call(s32[32,2]{1,0:T(8,128)S(1)} %copy.6.columns.columns_s, f32[5,16,16,128]{3,2,1,0:T(8,128)S(1)} %copy-done.3), custom_call_target="tpu_custom_call" | custom-call | tf_op jit(solution)/shard_map/pallas_call | solution.py:614
  35.8 4.1 %collective-permute-start = (f32[248,128]{1,0:T(8,128)S(1)}, f32[248,128]{1,0:T(8,128)S(1)}, u32[]{:S(2)}, u32[]{:S(2)}) collective-permute-start(f32[248,128]{1,0:T(8,128)S(1)} %get-tuple-element.22), channel_id=1, source_target_pairs={{0,8},{8,16},{16,24},{1,9},{9,17},{17,25},{2,10},{10,18},{18,26},{... | collective-permute-start | bytes 380936 | tf_op jit(solution)/shard_map/ppermute | solution.py:670
  39.8 1.9 %collective-permute-start.1 = (f32[248,128]{1,0:T(8,128)S(1)}, f32[248,128]{1,0:T(8,128)S(1)}, u32[]{:S(2)}, u32[]{:S(2)}) collective-permute-start(f32[248,128]{1,0:T(8,128)S(1)} %get-tuple-element.23), channel_id=1, source_target_pairs={{8,0},{16,8},{24,16},{9,1},{17,9},{25,17},{10,2},{18,10},{26,18},{... | collective-permute-start | bytes 380936 | tf_op jit(solution)/shard_map/ppermute | solution.py:670
  41.8 1.1 %shard_map.62.ghost = f32[640,128]{1,0:T(8,128)S(1)} custom-call(s32[1,32]{1,0:T(1,128)S(1)} %copy-done.4, s32[32,2]{1,0:T(8,128)S(1)} %copy.6.columns.columns_s, f32[1280,128]{1,0:T(8,128)S(1)} %bitcast.7), custom_call_target="tpu_custom_call" | custom-call | tf_op jit(solution)/shard_map/pallas_call | solution.py:614
  42.9 3.2 %collective-permute-done.1.above = f32[248,128]{1,0:T(8,128)S(1)} collective-permute-done((f32[248,128]{1,0:T(8,128)S(1)}, f32[248,128]{1,0:T(8,128)S(1)}, u32[]{:S(2)}, u32[]{:S(2)}) %collective-permute-start.1) | collective-permute-done | bytes 127008 | tf_op jit(solution)/shard_map/ppermute | solution.py:670
  46.1 1.2 %shard_map.63 = (f32[960,128]{1,0:T(8,128)}, f32[320,128]{1,0:T(8,128)S(1)}) custom-call(s32[1,32]{1,0:T(1,128)S(1)} %copy-done.4, s32[32,2]{1,0:T(8,128)S(1)} %copy.6.columns.columns_s, f32[1280,128]{1,0:T(8,128)S(1)} %bitcast.8, f32[640,128]{1,0:T(8,128)S(1)} %shard_map.62.ghost, f32[248,128]{1,0:T(8,128)S(1)} %collective-permute-done.below, ...), custom_call_target="tpu_custom_call" | custom-call | tf_op jit(solution)/shard_map/pallas_call | solution.py:614
  47.3 0.0 all-to-all-done.1
  47.3 5.4 %all-to-all-start.2 = ((f32[8,120,128]{2,1,0:T(8,128)}), f32[8,120,128]{2,1,0:T(8,128)S(1)}, u32[]{:S(2)}, u32[]{:S(2)}) async-start(f32[8,120,128]{2,1,0:T(8,128)} %bitcast.4), calls=%async_computation.2 | async-start | bytes 983040 | tf_op jit(solution)/shard_map/all_to_all | solution.py:666
  52.7 3.9 %shard_map.64 = (f32[184,128]{1,0:T(8,128)S(1)}, f32[184,128]{1,0:T(8,128)S(1)}, f32[184,128]{1,0:T(8,128)S(1)}, f32[184,128]{1,0:T(8,128)S(1)}, f32[184,128]{1,...) custom-call(s32[1,32]{1,0:T(1,128)S(1)} %copy-done.4, ...), custom_call_target="tpu_custom_call" | custom-call | tf_op jit(solution)/shard_map/pallas_call | solution.py:614
  56.6 1.2 %collective-permute-start.2 = (f32[184,128]{1,0:T(8,128)S(1)}, f32[184,128]{1,0:T(8,128)S(1)}, u32[]{:S(2)}, u32[]{:S(2)}) collective-permute-start(f32[184,128]{1,0:T(8,128)S(1)} %get-tuple-element.27), channel_id=1, source_target_pairs={{0,1},{1,2},{2,3},{3,4},{4,5},{5,6},{6,7},{7,0},{8,9},{9,10},{10,1... | collective-permute-start | bytes 282632 | tf_op jit(solution)/shard_map/ppermute | solution.py:707
  57.9 0.1 collective-permute-start.3
  57.9 1.4 %collective-permute-start.4 = (f32[184,128]{1,0:T(8,128)S(1)}, f32[184,128]{1,0:T(8,128)S(1)}, u32[]{:S(2)}, u32[]{:S(2)}) collective-permute-start(f32[184,128]{1,0:T(8,128)S(1)} %get-tuple-element.29), channel_id=1, source_target_pairs={{0,3},{1,4},{2,5},{3,6},{4,7},{5,0},{6,1},{7,2},{8,11},{9,12},{10,... | collective-permute-start | bytes 282632 | tf_op jit(solution)/shard_map/ppermute | solution.py:707
  59.3 2.1 %collective-permute-start.5 = (f32[184,128]{1,0:T(8,128)S(1)}, f32[184,128]{1,0:T(8,128)S(1)}, u32[]{:S(2)}, u32[]{:S(2)}) collective-permute-start(f32[184,128]{1,0:T(8,128)S(1)} %get-tuple-element.30), channel_id=1, source_target_pairs={{0,4},{1,5},{2,6},{3,7},{4,0},{5,1},{6,2},{7,3},{8,12},{9,13},{10,... | collective-permute-start | bytes 282632 | tf_op jit(solution)/shard_map/ppermute | solution.py:707
  61.4 1.2 %collective-permute-start.6 = (f32[184,128]{1,0:T(8,128)S(1)}, f32[184,128]{1,0:T(8,128)S(1)}, u32[]{:S(2)}, u32[]{:S(2)}) collective-permute-start(f32[184,128]{1,0:T(8,128)S(1)} %get-tuple-element.31), channel_id=1, source_target_pairs={{0,5},{1,6},{2,7},{3,0},{4,1},{5,2},{6,3},{7,4},{8,13},{9,14},{10,... | collective-permute-start | bytes 282632 | tf_op jit(solution)/shard_map/ppermute | solution.py:707
  62.6 10.2 %collective-permute-start.7 = (f32[184,128]{1,0:T(8,128)S(1)}, f32[184,128]{1,0:T(8,128)S(1)}, u32[]{:S(2)}, u32[]{:S(2)}) collective-permute-start(f32[184,128]{1,0:T(8,128)S(1)} %get-tuple-element.32), channel_id=1, source_target_pairs={{0,6},{1,7},{2,0},{3,1},{4,2},{5,3},{6,4},{7,5},{8,14},{9,15},{10,... | collective-permute-start | bytes 282632 | tf_op jit(solution)/shard_map/ppermute | solution.py:707
  72.8 2.5 %collective-permute-done.3.rest_2_ = f32[184,128]{1,0:T(8,128)S(1)} collective-permute-done((f32[184,128]{1,0:T(8,128)S(1)}, f32[184,128]{1,0:T(8,128)S(1)}, u32[]{:S(2)}, u32[]{:S(2)}) %collective-permute-start.3) | collective-permute-done | bytes 94240 | tf_op jit(solution)/shard_map/ppermute | solution.py:707
  75.3 0.1 collective-permute-done.4.rest_3_
  75.4 0.0 collective-permute-done.5.rest_4_
  75.4 1.4 %collective-permute-done.6.rest_5_ = f32[184,128]{1,0:T(8,128)S(1)} collective-permute-done((f32[184,128]{1,0:T(8,128)S(1)}, f32[184,128]{1,0:T(8,128)S(1)}, u32[]{:S(2)}, u32[]{:S(2)}) %collective-permute-start.6) | collective-permute-done | bytes 94240 | tf_op jit(solution)/shard_map/ppermute | solution.py:707
  76.8 1.0 %collective-permute-done.7.rest_6_ = f32[184,128]{1,0:T(8,128)S(1)} collective-permute-done((f32[184,128]{1,0:T(8,128)S(1)}, f32[184,128]{1,0:T(8,128)S(1)}, u32[]{:S(2)}, u32[]{:S(2)}) %collective-permute-start.7) | collective-permute-done | bytes 94240 | tf_op jit(solution)/shard_map/ppermute | solution.py:707
  77.8 2.5 %collective-permute-done.8.rest_7_ = f32[184,128]{1,0:T(8,128)S(1)} collective-permute-done((f32[184,128]{1,0:T(8,128)S(1)}, f32[184,128]{1,0:T(8,128)S(1)}, u32[]{:S(2)}, u32[]{:S(2)}) %collective-permute-start.8) | collective-permute-done | bytes 94240 | tf_op jit(solution)/shard_map/ppermute | solution.py:707
  80.4 1.1 %shard_map.65 = f32[5,16,16,128]{3,2,1,0:T(8,128)} custom-call(f32[5,16,16,128]{3,2,1,0:T(8,128)S(1)} %get-tuple-element.19.prov, f32[16,128]{1,0:T(8,128)S(1)} %get-tuple-element.20.bare, f32[5,2,16,128]{3,2,1,0:T(8,128)S(1)} %get-tuple-element.21.outer.coarse, f32[248,128]{1,0:T(8,128)S(1)} %collective-permute-done.below, ...), custom_call_target="tpu_custom_call" | custom-call | tf_op jit(solution)/shard_map/pallas_call | solution.py:614
  81.5 1.7 %copy-done.2 = f32[5,4,32,1024]{3,2,1,0:T(8,128)S(1)} copy-done((f32[5,4,32,1024]{3,2,1,0:T(8,128)S(1)}, f32[5,4,32,1024]{3,2,1,0:T(8,128)}, u32[]{:S(2)}) %copy-start.2) | copy-done | bytes 2621464
  83.2 3.1 %fine_edges.1 = f32[5,4,32,1024]{3,2,1,0:T(8,128)} custom-call(f32[5,4,32,1024]{3,2,1,0:T(8,128)S(1)} %copy-done.2, f32[960,128]{1,0:T(8,128)S(1)} %bitcast.10), custom_call_target="tpu_custom_call" | custom-call | tf_op jit(solution)/shard_map/fine_edges/pallas_call | solution.py:644
  (14 shorter events, 0.0 us)
Async XLA Ops:
  0.6 9.6 %copy-start = (f32[5,4,32,1024]{3,2,1,0:T(8,128)S(1)}, f32[5,4,32,1024]{3,2,1,0:T(8,128)}, u32[]{:S(2)}) copy-start(f32[5,4,32,1024]{3,2,1,0:T(8,128)} %fine.3) | copy-start | bytes 7864324
  4.6 26.8 %copy-start.5 = (s32[32,2]{0,1:T(2,128)S(1)}, s32[32,2]{0,1:T(2,128)}, u32[]{:S(2)}) copy-start(s32[32,2]{0,1:T(2,128)} %param.6) | copy-start | bytes 772
  4.6 31.2 %copy-start.4 = (s32[1,32]{1,0:T(1,128)S(1)}, s32[1,32]{1,0:T(1,128)}, u32[]{:S(2)}) copy-start(s32[1,32]{1,0:T(1,128)} %ids.7) | copy-start | bytes 388
  4.6 19.5 %all-to-all-start = ((f32[8,160,128]{2,1,0:T(8,128)}), f32[8,160,128]{2,1,0:T(8,128)S(1)}, u32[]{:S(2)}, u32[]{:S(2)}) async-start(f32[8,160,128]{2,1,0:T(8,128)} %bitcast.12), calls=%async_computation | async-start | bytes 1310720 | tf_op jit(solution)/shard_map/all_to_all | solution.py:666
  21.5 1.5 %copy-start.1 = (f32[5,4,32,1024]{3,2,1,0:T(8,128)}, f32[5,4,32,1024]{3,2,1,0:T(8,128)S(1)}, u32[]{:S(2)}) copy-start(f32[5,4,32,1024]{3,2,1,0:T(8,128)S(1)} %get-tuple-element.34.updated) | copy-start | bytes 7864324
  24.1 23.2 %all-to-all-start.1 = ((f32[8,80,128]{2,1,0:T(8,128)}), f32[8,80,128]{2,1,0:T(8,128)S(1)}, u32[]{:S(2)}, u32[]{:S(2)}) async-start(f32[8,80,128]{2,1,0:T(8,128)} %bitcast.13), calls=%async_computation.1 | async-start | bytes 655360 | tf_op jit(solution)/shard_map/all_to_all | solution.py:666
  31.4 1.1 %copy-start.3 = (f32[5,16,16,128]{3,2,1,0:T(8,128)S(1)}, f32[5,16,16,128]{3,2,1,0:T(8,128)}, u32[]{:S(2)}) copy-start(f32[5,16,16,128]{3,2,1,0:T(8,128)} %coarse.3) | copy-start | bytes 1966084
  35.8 7.2 %collective-permute-start = (f32[248,128]{1,0:T(8,128)S(1)}, f32[248,128]{1,0:T(8,128)S(1)}, u32[]{:S(2)}, u32[]{:S(2)}) collective-permute-start(f32[248,128]{1,0:T(8,128)S(1)} %get-tuple-element.22), channel_id=1, source_target_pairs={{0,8},{8,16},{16,24},{1,9},{9,17},{17,25},{2,10},{10,18},{18,26},{... | collective-permute-start | bytes 380936 | tf_op jit(solution)/shard_map/ppermute | solution.py:670
  39.8 6.2 %collective-permute-start.1 = (f32[248,128]{1,0:T(8,128)S(1)}, f32[248,128]{1,0:T(8,128)S(1)}, u32[]{:S(2)}, u32[]{:S(2)}) collective-permute-start(f32[248,128]{1,0:T(8,128)S(1)} %get-tuple-element.23), channel_id=1, source_target_pairs={{8,0},{16,8},{24,16},{9,1},{17,9},{25,17},{10,2},{18,10},{26,18},{... | collective-permute-start | bytes 380936 | tf_op jit(solution)/shard_map/ppermute | solution.py:670
  47.3 34.2 %all-to-all-start.2 = ((f32[8,120,128]{2,1,0:T(8,128)}), f32[8,120,128]{2,1,0:T(8,128)S(1)}, u32[]{:S(2)}, u32[]{:S(2)}) async-start(f32[8,120,128]{2,1,0:T(8,128)} %bitcast.4), calls=%async_computation.2 | async-start | bytes 983040 | tf_op jit(solution)/shard_map/all_to_all | solution.py:666
  56.6 6.0 %collective-permute-start.2 = (f32[184,128]{1,0:T(8,128)S(1)}, f32[184,128]{1,0:T(8,128)S(1)}, u32[]{:S(2)}, u32[]{:S(2)}) collective-permute-start(f32[184,128]{1,0:T(8,128)S(1)} %get-tuple-element.27), channel_id=1, source_target_pairs={{0,1},{1,2},{2,3},{3,4},{4,5},{5,6},{6,7},{7,0},{8,9},{9,10},{10,1... | collective-permute-start | bytes 282632 | tf_op jit(solution)/shard_map/ppermute | solution.py:707
  57.9 17.4 %collective-permute-start.3 = (f32[184,128]{1,0:T(8,128)S(1)}, f32[184,128]{1,0:T(8,128)S(1)}, u32[]{:S(2)}, u32[]{:S(2)}) collective-permute-start(f32[184,128]{1,0:T(8,128)S(1)} %get-tuple-element.28), channel_id=1, source_target_pairs={{0,2},{1,3},{2,4},{3,5},{4,6},{5,7},{6,0},{7,1},{8,10},{9,11},{10,... | collective-permute-start | bytes 282632 | tf_op jit(solution)/shard_map/ppermute | solution.py:707
  57.9 17.4 %collective-permute-start.4 = (f32[184,128]{1,0:T(8,128)S(1)}, f32[184,128]{1,0:T(8,128)S(1)}, u32[]{:S(2)}, u32[]{:S(2)}) collective-permute-start(f32[184,128]{1,0:T(8,128)S(1)} %get-tuple-element.29), channel_id=1, source_target_pairs={{0,3},{1,4},{2,5},{3,6},{4,7},{5,0},{6,1},{7,2},{8,11},{9,12},{10,... | collective-permute-start | bytes 282632 | tf_op jit(solution)/shard_map/ppermute | solution.py:707
  59.3 16.1 %collective-permute-start.5 = (f32[184,128]{1,0:T(8,128)S(1)}, f32[184,128]{1,0:T(8,128)S(1)}, u32[]{:S(2)}, u32[]{:S(2)}) collective-permute-start(f32[184,128]{1,0:T(8,128)S(1)} %get-tuple-element.30), channel_id=1, source_target_pairs={{0,4},{1,5},{2,6},{3,7},{4,0},{5,1},{6,2},{7,3},{8,12},{9,13},{10,... | collective-permute-start | bytes 282632 | tf_op jit(solution)/shard_map/ppermute | solution.py:707
  61.4 15.4 %collective-permute-start.6 = (f32[184,128]{1,0:T(8,128)S(1)}, f32[184,128]{1,0:T(8,128)S(1)}, u32[]{:S(2)}, u32[]{:S(2)}) collective-permute-start(f32[184,128]{1,0:T(8,128)S(1)} %get-tuple-element.31), channel_id=1, source_target_pairs={{0,5},{1,6},{2,7},{3,0},{4,1},{5,2},{6,3},{7,4},{8,13},{9,14},{10,... | collective-permute-start | bytes 282632 | tf_op jit(solution)/shard_map/ppermute | solution.py:707
  62.6 15.2 %collective-permute-start.7 = (f32[184,128]{1,0:T(8,128)S(1)}, f32[184,128]{1,0:T(8,128)S(1)}, u32[]{:S(2)}, u32[]{:S(2)}) collective-permute-start(f32[184,128]{1,0:T(8,128)S(1)} %get-tuple-element.32), channel_id=1, source_target_pairs={{0,6},{1,7},{2,0},{3,1},{4,2},{5,3},{6,4},{7,5},{8,14},{9,15},{10,... | collective-permute-start | bytes 282632 | tf_op jit(solution)/shard_map/ppermute | solution.py:707
  75.3 5.1 %collective-permute-start.8 = (f32[184,128]{1,0:T(8,128)S(1)}, f32[184,128]{1,0:T(8,128)S(1)}, u32[]{:S(2)}, u32[]{:S(2)}) collective-permute-start(f32[184,128]{1,0:T(8,128)S(1)} %get-tuple-element.33), channel_id=1, source_target_pairs={{0,7},{1,0},{2,1},{3,2},{4,3},{5,4},{6,5},{7,6},{8,15},{9,8},{10,9... | collective-permute-start | bytes 282632 | tf_op jit(solution)/shard_map/ppermute | solution.py:707
  81.5 1.7 %copy-start.2 = (f32[5,4,32,1024]{3,2,1,0:T(8,128)S(1)}, f32[5,4,32,1024]{3,2,1,0:T(8,128)}, u32[]{:S(2)}) copy-start(f32[5,4,32,1024]{3,2,1,0:T(8,128)} %copy-done.1) | copy-start | bytes 7864324

commit v5 on v4

--- a/solution.py
+++ b/solution.py
@@ -444,8 +444,7 @@
                 outf[k : k + z.own, :] = C[d * z.own : (d + 1) * z.own]
 
 
-def canvas_kernel(z, ids_s, columns_s, ids, columns, com, ghost, xc, avg, *rest):
-    outs, (canvas, ends) = rest[: z.n], rest[z.n :]
+def correct_kernel(z, ids, columns, ghost, canvas):
     S, f_of = z.S, z.P
     vx = 5 * z.xc
     _, gy, gz, gyr, gzr = positions(z, ids, columns)
@@ -490,6 +489,16 @@
         ysum = term if ysum is None else ysum + term
     for k in range(vx):
         canvas[k * z.NZ : (k + 1) * z.NZ, :] = zsum[:, k * LANES : (k + 1) * LANES] + ysum[k * z.NZ : (k + 1) * z.NZ, :]
+
+
+def canvas_kernel(z, ids_s, columns_s, ids, columns, com, start, xc, avg, *rest):
+    outs, (canvas, ends) = rest[: z.n], rest[z.n :]
+    S = z.S
+    vx = 5 * z.xc
+    _, gy, _, _, gzr = positions(z, ids, columns)
+    lane = lax.broadcasted_iota(jnp.int32, (S, LANES), 1)
+    in_y = lane // z.H == gy + 1
+    canvas[...] = start[...]
     rank = lax.broadcasted_iota(jnp.int32, (z.n, LANES), 0)
     rank_slot = lax.broadcasted_iota(jnp.int32, (z.n, S), 0)
     inside_y = in_y.astype(jnp.bfloat16)
@@ -687,6 +696,7 @@
     below = shifted(up, 1)
     above = shifted(dn, -1)
     (ghost,) = call(side_kernel, z, [faces], [("v", patch_ids), ("v", columns), ("p", com)], [faces])
+    (start,) = call(correct_kernel, z, [(5 * z.xc * z.NZ, LANES)], [("v", patch_ids), ("v", columns), ("p", ghost)])
     outf, xc = call(
         end_kernel,
         z,
@@ -700,7 +710,7 @@
         z,
         [(z.RK, LANES)] * n,
         [("s", patch_ids), ("s", columns), ("v", patch_ids), ("v", columns)]
-        + [("p", a) for a in (com, ghost, xc, avg)],
+        + [("p", a) for a in (com, start, xc, avg)],
         [(5 * z.xc * z.NZ, LANES), (10 * z.zcl, n, LANES)],
     ))
     for k in range(1, n):

time: 86.8 us -> 89.7 us (1.033)
  local copies, waits for them, and re-layouts: 4.42 us -> 8.2 us
  starting transfers between devices: 40.6 us -> 38.5 us
  Pallas kernels: 28.7 us -> 29.8 us
    unnamed x13 -> x33, local copies, waits for them, and re-layouts: 4.42 us -> 8.2 us
    ppermute x7, starting transfers between devices: 16.2 us -> 14.1 us  [level_step(): lax.ppermute(pieces[k], 'patch', [(i, (i + k) % n) for i in range(n)])]
    pallas_call x1, Pallas kernels: 3.1 us -> 4.14 us  [run_fine(): pl.pallas_call(functools.partial(fine_kernel, z), grid=(z.own,), out_shap...]
    pallas_call x7 -> x8, Pallas kernels: 14.4 us -> 14.4 us  [call(): pl.pallas_call(functools.partial(kernel, z), out_shape=[keep(s, jnp.float...]
  transfers between devices with their start and end apart: 12 -> 12, of which waited for: 7 -> 7; matrix products, arithmetic and copies ran while one was open for 0% -> 0% of each run, Pallas kernels for 25% -> 24%
where the time goes in v5:
time: 89.7 us; the launch traced here: 89.1 us
  starting transfers between devices  38.5 us (43%)
  Pallas kernels  29.8 us (33%)
  waiting for transfers between devices  11.9 us (13%)
  local copies, waits for them, and re-layouts  8.2 us (9%)
    all_to_all x3, starting transfers between devices, exchange(): return lax.all_to_all(a, 'patch', 0, 0, tiled=True)  18.4 us
    pallas_call x8, Pallas kernels, call(): pl.pallas_call(functools.partial(kernel, z), out_shape=[keep(s, jnp.float...  14.4 us
    ppermute x7, starting transfers between devices, level_step(): lax.ppermute(pieces[k], 'patch', [(i, (i + k) % n) for i in range(n)])  14.1 us
    pallas_call x1, Pallas kernels, run_advance(): pl.pallas_call(functools.partial(advance_kernel, z), grid=(z.own,), out_s...  11.2 us
    unnamed x33, local copies, waits for them, and re-layouts  8.2 us
    ppermute x7, waiting for transfers between devices, level_step(): lax.ppermute(pieces[k], 'patch', [(i, (i + k) % n) for i in range(n)])  7.54 us
    ppermute x2, starting transfers between devices, shifted(): return lax.ppermute(a, 'slab', pairs)  6.01 us
    pallas_call x1, Pallas kernels, run_fine(): pl.pallas_call(functools.partial(fine_kernel, z), grid=(z.own,), out_shap...  4.14 us
  transfers between devices with their start and end apart: 12, of which 7 were waited for; matrix products, arithmetic and copies ran while one was open for 0% of the time, Pallas kernels for 24%

profile of v5, /device:TPU:19, one launch (start us, length us, event | category | flops | bytes accessed | tf_op | source)
XLA Modules:
  0.0 89.1 jit_solution(5598184149785693332)
XLA Ops:
  0.6 3.9 %shard_map.60 = f32[1280,128]{1,0:T(8,128)} custom-call(f32[5,4,32,1024]{3,2,1,0:T(8,128)} %fine.3, f32[5,16,16,128]{3,2,1,0:T(8,128)} %coarse.3), custom_call_target="tpu_custom_call" | custom-call | tf_op jit(solution)/shard_map/pallas_call | solution.py:623
  4.6 5.7 %all-to-all-start = ((f32[8,160,128]{2,1,0:T(8,128)}), f32[8,160,128]{2,1,0:T(8,128)S(1)}, u32[]{:S(2)}, u32[]{:S(2)}) async-start(f32[8,160,128]{2,1,0:T(8,128)} %bitcast.11), calls=%async_computation | async-start | bytes 1310720 | tf_op jit(solution)/shard_map/all_to_all | solution.py:675
  10.2 11.2 %advance.1 = (f32[5,4,32,1024]{3,2,1,0:T(8,128)S(1)}, f32[640,128]{1,0:T(8,128)}) custom-call(f32[5,4,32,1024]{3,2,1,0:T(8,128)S(1)} %copy-done), custom_call_target="tpu_custom_call" | custom-call | tf_op jit(solution)/shard_map/advance/pallas_call | solution.py:636
  21.5 1.5 %copy-done.1 = f32[5,4,32,1024]{3,2,1,0:T(8,128)} copy-done((f32[5,4,32,1024]{3,2,1,0:T(8,128)}, f32[5,4,32,1024]{3,2,1,0:T(8,128)S(1)}, u32[]{:S(2)}) %copy-start.1) | copy-done | bytes 2621464
  22.9 1.2 %all-to-all-done = f32[8,160,128]{2,1,0:T(8,128)S(1)} async-done(((f32[8,160,128]{2,1,0:T(8,128)}), f32[8,160,128]{2,1,0:T(8,128)S(1)}, u32[]{:S(2)}, u32[]{:S(2)}) %all-to-all-start) | async-done | bytes 655392 | tf_op jit(solution)/shard_map/all_to_all | solution.py:675
  24.1 7.3 %all-to-all-start.1 = ((f32[8,80,128]{2,1,0:T(8,128)}), f32[8,80,128]{2,1,0:T(8,128)S(1)}, u32[]{:S(2)}, u32[]{:S(2)}) async-start(f32[8,80,128]{2,1,0:T(8,128)} %bitcast.12), calls=%async_computation.1 | async-start | bytes 655360 | tf_op jit(solution)/shard_map/all_to_all | solution.py:675
  31.4 1.1 %copy-done.3 = f32[5,16,16,128]{3,2,1,0:T(8,128)S(1)} copy-done((f32[5,16,16,128]{3,2,1,0:T(8,128)S(1)}, f32[5,16,16,128]{3,2,1,0:T(8,128)}, u32[]{:S(2)}) %copy-start.3) | copy-done | bytes 655384
  32.5 3.2 %shard_map.59 = (f32[5,16,16,128]{3,2,1,0:T(8,128)S(1)}, f32[16,128]{1,0:T(8,128)S(1)}, f32[5,2,16,128]{3,2,1,0:T(8,128)S(1)}) custom-call(s32[32,2]{1,0:T(8,128)S(1)} %copy.6.columns.columns_s, f32[5,16,16,128]{3,2,1,0:T(8,128)S(1)} %copy-done.3), custom_call_target="tpu_custom_call" | custom-call | tf_op jit(solution)/shard_map/pallas_call | solution.py:623
  35.7 0.8 copy-done.6
  36.6 4.1 %collective-permute-start = (f32[248,128]{1,0:T(8,128)S(1)}, f32[248,128]{1,0:T(8,128)S(1)}, u32[]{:S(2)}, u32[]{:S(2)}) collective-permute-start(f32[248,128]{1,0:T(8,128)S(1)} %get-tuple-element.22), channel_id=1, source_target_pairs={{0,8},{8,16},{16,24},{1,9},{9,17},{17,25},{2,10},{10,18},{18,26},{... | collective-permute-start | bytes 380936 | tf_op jit(solution)/shard_map/ppermute | solution.py:679
  40.7 1.9 %collective-permute-start.1 = (f32[248,128]{1,0:T(8,128)S(1)}, f32[248,128]{1,0:T(8,128)S(1)}, u32[]{:S(2)}, u32[]{:S(2)}) collective-permute-start(f32[248,128]{1,0:T(8,128)S(1)} %get-tuple-element.23), channel_id=1, source_target_pairs={{8,0},{16,8},{24,16},{9,1},{17,9},{25,17},{10,2},{18,10},{26,18},{... | collective-permute-start | bytes 380936 | tf_op jit(solution)/shard_map/ppermute | solution.py:679
  42.6 1.1 %shard_map.62.ghost = f32[640,128]{1,0:T(8,128)S(1)} custom-call(s32[1,32]{1,0:T(1,128)S(1)} %copy-done.12, s32[32,2]{1,0:T(8,128)S(1)} %copy.6.columns.columns_s, f32[1280,128]{1,0:T(8,128)S(1)} %bitcast.7), custom_call_target="tpu_custom_call" | custom-call | tf_op jit(solution)/shard_map/pallas_call | solution.py:623
  43.8 3.2 %collective-permute-done.1.above = f32[248,128]{1,0:T(8,128)S(1)} collective-permute-done((f32[248,128]{1,0:T(8,128)S(1)}, f32[248,128]{1,0:T(8,128)S(1)}, u32[]{:S(2)}, u32[]{:S(2)}) %collective-permute-start.1) | collective-permute-done | bytes 127008 | tf_op jit(solution)/shard_map/ppermute | solution.py:679
  46.9 1.2 %shard_map.64 = (f32[960,128]{1,0:T(8,128)}, f32[320,128]{1,0:T(8,128)S(1)}) custom-call(s32[1,32]{1,0:T(1,128)S(1)} %copy-done.12, s32[32,2]{1,0:T(8,128)S(1)} %copy.6.columns.columns_s, f32[1280,128]{1,0:T(8,128)S(1)} %bitcast.8, f32[640,128]{1,0:T(8,128)S(1)} %shard_map.62.ghost, f32[248,128]{1,0:T(8,128)S(1)} %collective-permute-done.below, ...), custom_call_target="tpu_custom_call" | custom-call | tf_op jit(solution)/shard_map/pallas_call | solution.py:623
  48.8 5.4 %all-to-all-start.2 = ((f32[8,120,128]{2,1,0:T(8,128)}), f32[8,120,128]{2,1,0:T(8,128)}, u32[]{:S(2)}, u32[]{:S(2)}) async-start(f32[8,120,128]{2,1,0:T(8,128)} %bitcast.4), calls=%async_computation.2 | async-start | bytes 983040 | tf_op jit(solution)/shard_map/all_to_all | solution.py:675
  54.2 0.9 %shard_map.63.start = f32[1280,128]{1,0:T(8,128)S(1)} custom-call(s32[1,32]{1,0:T(1,128)S(1)} %copy-done.12, s32[32,2]{1,0:T(8,128)S(1)} %copy.6.columns.columns_s, f32[640,128]{1,0:T(8,128)S(1)} %shard_map.62.ghost), custom_call_target="tpu_custom_call" | custom-call | tf_op jit(solution)/shard_map/pallas_call | solution.py:623
  55.2 1.1 %copy-done.5 = f32[8,80,128]{2,1,0:T(8,128)S(1)} copy-done((f32[8,80,128]{2,1,0:T(8,128)S(1)}, f32[8,80,128]{2,1,0:T(8,128)}, u32[]{:S(2)}) %copy-start.5) | copy-done | bytes 327704
  56.3 0.9 %copy-done.11 = f32[320,128]{1,0:T(8,128)S(1)} copy-done((f32[320,128]{1,0:T(8,128)S(1)}, f32[320,128]{1,0:T(8,128)}, u32[]{:S(2)}) %copy-start.11) | copy-done | bytes 163864
  57.2 3.0 %shard_map.65 = (f32[184,128]{1,0:T(8,128)S(1)}, f32[184,128]{1,0:T(8,128)S(1)}, f32[184,128]{1,0:T(8,128)S(1)}, f32[184,128]{1,0:T(8,128)S(1)}, f32[184,128]{1,...) custom-call(s32[1,32]{1,0:T(1,128)S(1)} %copy-done.12, ...), custom_call_target="tpu_custom_call" | custom-call | tf_op jit(solution)/shard_map/pallas_call | solution.py:623
  60.2 1.2 %collective-permute-start.2 = (f32[184,128]{1,0:T(8,128)S(1)}, f32[184,128]{1,0:T(8,128)S(1)}, u32[]{:S(2)}, u32[]{:S(2)}) collective-permute-start(f32[184,128]{1,0:T(8,128)S(1)} %get-tuple-element.27), channel_id=1, source_target_pairs={{0,1},{1,2},{2,3},{3,4},{4,5},{5,6},{6,7},{7,0},{8,9},{9,10},{10,1... | collective-permute-start | bytes 282632 | tf_op jit(solution)/shard_map/ppermute | solution.py:717
  61.5 1.4 %collective-permute-start.4 = (f32[184,128]{1,0:T(8,128)S(1)}, f32[184,128]{1,0:T(8,128)S(1)}, u32[]{:S(2)}, u32[]{:S(2)}) collective-permute-start(f32[184,128]{1,0:T(8,128)S(1)} %get-tuple-element.29), channel_id=1, source_target_pairs={{0,3},{1,4},{2,5},{3,6},{4,7},{5,0},{6,1},{7,2},{8,11},{9,12},{10,... | collective-permute-start | bytes 282632 | tf_op jit(solution)/shard_map/ppermute | solution.py:717
  62.9 2.1 %collective-permute-start.5 = (f32[184,128]{1,0:T(8,128)S(1)}, f32[184,128]{1,0:T(8,128)S(1)}, u32[]{:S(2)}, u32[]{:S(2)}) collective-permute-start(f32[184,128]{1,0:T(8,128)S(1)} %get-tuple-element.30), channel_id=1, source_target_pairs={{0,4},{1,5},{2,6},{3,7},{4,0},{5,1},{6,2},{7,3},{8,12},{9,13},{10,... | collective-permute-start | bytes 282632 | tf_op jit(solution)/shard_map/ppermute | solution.py:717
  65.0 1.2 %collective-permute-start.6 = (f32[184,128]{1,0:T(8,128)S(1)}, f32[184,128]{1,0:T(8,128)S(1)}, u32[]{:S(2)}, u32[]{:S(2)}) collective-permute-start(f32[184,128]{1,0:T(8,128)S(1)} %get-tuple-element.31), channel_id=1, source_target_pairs={{0,5},{1,6},{2,7},{3,0},{4,1},{5,2},{6,3},{7,4},{8,13},{9,14},{10,... | collective-permute-start | bytes 282632 | tf_op jit(solution)/shard_map/ppermute | solution.py:717
  66.2 8.2 %collective-permute-start.7 = (f32[184,128]{1,0:T(8,128)S(1)}, f32[184,128]{1,0:T(8,128)S(1)}, u32[]{:S(2)}, u32[]{:S(2)}) collective-permute-start(f32[184,128]{1,0:T(8,128)S(1)} %get-tuple-element.32), channel_id=1, source_target_pairs={{0,6},{1,7},{2,0},{3,1},{4,2},{5,3},{6,4},{7,5},{8,14},{9,15},{10,... | collective-permute-start | bytes 282632 | tf_op jit(solution)/shard_map/ppermute | solution.py:717
  74.3 2.5 %collective-permute-done.3.rest_2_ = f32[184,128]{1,0:T(8,128)S(1)} collective-permute-done((f32[184,128]{1,0:T(8,128)S(1)}, f32[184,128]{1,0:T(8,128)S(1)}, u32[]{:S(2)}, u32[]{:S(2)}) %collective-permute-start.3) | collective-permute-done | bytes 94240 | tf_op jit(solution)/shard_map/ppermute | solution.py:717
  76.9 1.4 %collective-permute-done.6.rest_5_ = f32[184,128]{1,0:T(8,128)S(1)} collective-permute-done((f32[184,128]{1,0:T(8,128)S(1)}, f32[184,128]{1,0:T(8,128)S(1)}, u32[]{:S(2)}, u32[]{:S(2)}) %collective-permute-start.6) | collective-permute-done | bytes 94240 | tf_op jit(solution)/shard_map/ppermute | solution.py:717
  78.3 1.0 %collective-permute-done.7.rest_6_ = f32[184,128]{1,0:T(8,128)S(1)} collective-permute-done((f32[184,128]{1,0:T(8,128)S(1)}, f32[184,128]{1,0:T(8,128)S(1)}, u32[]{:S(2)}, u32[]{:S(2)}) %collective-permute-start.7) | collective-permute-done | bytes 94240 | tf_op jit(solution)/shard_map/ppermute | solution.py:717
  79.4 2.5 %collective-permute-done.8.rest_7_ = f32[184,128]{1,0:T(8,128)S(1)} collective-permute-done((f32[184,128]{1,0:T(8,128)S(1)}, f32[184,128]{1,0:T(8,128)S(1)}, u32[]{:S(2)}, u32[]{:S(2)}) %collective-permute-start.8) | collective-permute-done | bytes 94240 | tf_op jit(solution)/shard_map/ppermute | solution.py:717
  81.9 1.1 %copy-done.7 = f32[5,16,16,128]{3,2,1,0:T(8,128)S(1)} copy-done((f32[5,16,16,128]{3,2,1,0:T(8,128)S(1)}, f32[5,16,16,128]{3,2,1,0:T(8,128)}, u32[]{:S(2)}) %copy-start.7) | copy-done | bytes 655384
  83.0 0.9 copy-done.9
  83.9 1.1 %shard_map.66 = f32[5,16,16,128]{3,2,1,0:T(8,128)} custom-call(f32[5,16,16,128]{3,2,1,0:T(8,128)S(1)} %copy-done.7, f32[16,128]{1,0:T(8,128)S(1)} %copy-done.14, f32[5,2,16,128]{3,2,1,0:T(8,128)S(1)} %copy-done.9, f32[248,128]{1,0:T(8,128)S(1)} %collective-permute-done.below, f32[248,128]{1,0:T(8,128)S(1)} %collective-permute-done.1.above, ...), custom_call_target="tpu_custom_call" | custom-call | tf_op jit(solution)/shard_map/pallas_call | solution.py:623
  85.0 4.1 %fine_edges.1 = f32[5,4,32,1024]{3,2,1,0:T(8,128)} custom-call(f32[5,4,32,1024]{3,2,1,0:T(8,128)S(1)} %copy-done.2, f32[960,128]{1,0:T(8,128)} %bitcast.5.recv), custom_call_target="tpu_custom_call" | custom-call | tf_op jit(solution)/shard_map/fine_edges/pallas_call | solution.py:653
  (35 shorter events, 1.0 us)
Async XLA Ops:
  0.6 9.6 %copy-start = (f32[5,4,32,1024]{3,2,1,0:T(8,128)S(1)}, f32[5,4,32,1024]{3,2,1,0:T(8,128)}, u32[]{:S(2)}) copy-start(f32[5,4,32,1024]{3,2,1,0:T(8,128)} %fine.3) | copy-start | bytes 7864324
  4.6 26.8 %copy-start.15 = (s32[32,2]{0,1:T(2,128)S(1)}, s32[32,2]{0,1:T(2,128)}, u32[]{:S(2)}) copy-start(s32[32,2]{0,1:T(2,128)} %param.6) | copy-start | bytes 772
  4.6 32.0 %copy-start.12 = (s32[1,32]{1,0:T(1,128)S(1)}, s32[1,32]{1,0:T(1,128)}, u32[]{:S(2)}) copy-start(s32[1,32]{1,0:T(1,128)} %ids.9) | copy-start | bytes 388
  4.6 19.5 %all-to-all-start = ((f32[8,160,128]{2,1,0:T(8,128)}), f32[8,160,128]{2,1,0:T(8,128)S(1)}, u32[]{:S(2)}, u32[]{:S(2)}) async-start(f32[8,160,128]{2,1,0:T(8,128)} %bitcast.11), calls=%async_computation | async-start | bytes 1310720 | tf_op jit(solution)/shard_map/all_to_all | solution.py:675
  21.5 1.5 %copy-start.1 = (f32[5,4,32,1024]{3,2,1,0:T(8,128)}, f32[5,4,32,1024]{3,2,1,0:T(8,128)S(1)}, u32[]{:S(2)}) copy-start(f32[5,4,32,1024]{3,2,1,0:T(8,128)S(1)} %get-tuple-element.34.updated) | copy-start | bytes 7864324
  24.1 24.7 %all-to-all-start.1 = ((f32[8,80,128]{2,1,0:T(8,128)}), f32[8,80,128]{2,1,0:T(8,128)S(1)}, u32[]{:S(2)}, u32[]{:S(2)}) async-start(f32[8,80,128]{2,1,0:T(8,128)} %bitcast.12), calls=%async_computation.1 | async-start | bytes 655360 | tf_op jit(solution)/shard_map/all_to_all | solution.py:675
  31.4 1.1 %copy-start.3 = (f32[5,16,16,128]{3,2,1,0:T(8,128)S(1)}, f32[5,16,16,128]{3,2,1,0:T(8,128)}, u32[]{:S(2)}) copy-start(f32[5,16,16,128]{3,2,1,0:T(8,128)} %coarse.3) | copy-start | bytes 1966084
  35.7 0.8 copy-start.6
  36.5 4.1 %copy-start.8 = (f32[5,2,16,128]{3,2,1,0:T(8,128)}, f32[5,2,16,128]{3,2,1,0:T(8,128)S(1)}, u32[]{:S(2)}) copy-start(f32[5,2,16,128]{3,2,1,0:T(8,128)S(1)} %get-tuple-element.21.outer.coarse) | copy-start | bytes 245764
  36.6 10.4 %copy-start.13 = (f32[16,128]{1,0:T(8,128)}, f32[16,128]{1,0:T(8,128)S(1)}, u32[]{:S(2)}) copy-start(f32[16,128]{1,0:T(8,128)S(1)} %get-tuple-element.20.bare) | copy-start | bytes 24580
  36.6 7.2 %collective-permute-start = (f32[248,128]{1,0:T(8,128)S(1)}, f32[248,128]{1,0:T(8,128)S(1)}, u32[]{:S(2)}, u32[]{:S(2)}) collective-permute-start(f32[248,128]{1,0:T(8,128)S(1)} %get-tuple-element.22), channel_id=1, source_target_pairs={{0,8},{8,16},{16,24},{1,9},{9,17},{17,25},{2,10},{10,18},{18,26},{... | collective-permute-start | bytes 380936 | tf_op jit(solution)/shard_map/ppermute | solution.py:679
  40.7 6.2 %collective-permute-start.1 = (f32[248,128]{1,0:T(8,128)S(1)}, f32[248,128]{1,0:T(8,128)S(1)}, u32[]{:S(2)}, u32[]{:S(2)}) collective-permute-start(f32[248,128]{1,0:T(8,128)S(1)} %get-tuple-element.23), channel_id=1, source_target_pairs={{8,0},{16,8},{24,16},{9,1},{17,9},{25,17},{10,2},{18,10},{26,18},{... | collective-permute-start | bytes 380936 | tf_op jit(solution)/shard_map/ppermute | solution.py:679
  48.1 0.7 copy-start.10
  48.8 5.4 %copy-start.4 = (f32[8,80,128]{2,1,0:T(8,128)}, f32[8,80,128]{2,1,0:T(8,128)S(1)}, u32[]{:S(2)}) copy-start(f32[8,80,128]{2,1,0:T(8,128)S(1)} %all-to-all-done.1) | copy-start | bytes 983044
  48.8 36.2 %all-to-all-start.2 = ((f32[8,120,128]{2,1,0:T(8,128)}), f32[8,120,128]{2,1,0:T(8,128)}, u32[]{:S(2)}, u32[]{:S(2)}) async-start(f32[8,120,128]{2,1,0:T(8,128)} %bitcast.4), calls=%async_computation.2 | async-start | bytes 983040 | tf_op jit(solution)/shard_map/all_to_all | solution.py:675
  54.2 27.7 %copy-start.14 = (f32[16,128]{1,0:T(8,128)S(1)}, f32[16,128]{1,0:T(8,128)}, u32[]{:S(2)}) copy-start(f32[16,128]{1,0:T(8,128)} %copy-done.13) | copy-start | bytes 24580
  55.1 29.8 %copy-start.2 = (f32[5,4,32,1024]{3,2,1,0:T(8,128)S(1)}, f32[5,4,32,1024]{3,2,1,0:T(8,128)}, u32[]{:S(2)}) copy-start(f32[5,4,32,1024]{3,2,1,0:T(8,128)} %copy-done.1) | copy-start | bytes 7864324
  55.2 1.1 %copy-start.5 = (f32[8,80,128]{2,1,0:T(8,128)S(1)}, f32[8,80,128]{2,1,0:T(8,128)}, u32[]{:S(2)}) copy-start(f32[8,80,128]{2,1,0:T(8,128)} %copy-done.4) | copy-start | bytes 983044
  56.3 0.9 %copy-start.11 = (f32[320,128]{1,0:T(8,128)S(1)}, f32[320,128]{1,0:T(8,128)}, u32[]{:S(2)}) copy-start(f32[320,128]{1,0:T(8,128)} %copy-done.10) | copy-start | bytes 491524
  60.2 6.0 %collective-permute-start.2 = (f32[184,128]{1,0:T(8,128)S(1)}, f32[184,128]{1,0:T(8,128)S(1)}, u32[]{:S(2)}, u32[]{:S(2)}) collective-permute-start(f32[184,128]{1,0:T(8,128)S(1)} %get-tuple-element.27), channel_id=1, source_target_pairs={{0,1},{1,2},{2,3},{3,4},{4,5},{5,6},{6,7},{7,0},{8,9},{9,10},{10,1... | collective-permute-start | bytes 282632 | tf_op jit(solution)/shard_map/ppermute | solution.py:717
  61.4 15.4 %collective-permute-start.3 = (f32[184,128]{1,0:T(8,128)S(1)}, f32[184,128]{1,0:T(8,128)S(1)}, u32[]{:S(2)}, u32[]{:S(2)}) collective-permute-start(f32[184,128]{1,0:T(8,128)S(1)} %get-tuple-element.28), channel_id=1, source_target_pairs={{0,2},{1,3},{2,4},{3,5},{4,6},{5,7},{6,0},{7,1},{8,10},{9,11},{10,... | collective-permute-start | bytes 282632 | tf_op jit(solution)/shard_map/ppermute | solution.py:717
  61.5 15.3 %collective-permute-start.4 = (f32[184,128]{1,0:T(8,128)S(1)}, f32[184,128]{1,0:T(8,128)S(1)}, u32[]{:S(2)}, u32[]{:S(2)}) collective-permute-start(f32[184,128]{1,0:T(8,128)S(1)} %get-tuple-element.29), channel_id=1, source_target_pairs={{0,3},{1,4},{2,5},{3,6},{4,7},{5,0},{6,1},{7,2},{8,11},{9,12},{10,... | collective-permute-start | bytes 282632 | tf_op jit(solution)/shard_map/ppermute | solution.py:717
  62.9 14.0 %collective-permute-start.5 = (f32[184,128]{1,0:T(8,128)S(1)}, f32[184,128]{1,0:T(8,128)S(1)}, u32[]{:S(2)}, u32[]{:S(2)}) collective-permute-start(f32[184,128]{1,0:T(8,128)S(1)} %get-tuple-element.30), channel_id=1, source_target_pairs={{0,4},{1,5},{2,6},{3,7},{4,0},{5,1},{6,2},{7,3},{8,12},{9,13},{10,... | collective-permute-start | bytes 282632 | tf_op jit(solution)/shard_map/ppermute | solution.py:717
  65.0 13.4 %collective-permute-start.6 = (f32[184,128]{1,0:T(8,128)S(1)}, f32[184,128]{1,0:T(8,128)S(1)}, u32[]{:S(2)}, u32[]{:S(2)}) collective-permute-start(f32[184,128]{1,0:T(8,128)S(1)} %get-tuple-element.31), channel_id=1, source_target_pairs={{0,5},{1,6},{2,7},{3,0},{4,1},{5,2},{6,3},{7,4},{8,13},{9,14},{10,... | collective-permute-start | bytes 282632 | tf_op jit(solution)/shard_map/ppermute | solution.py:717
  66.2 13.2 %collective-permute-start.7 = (f32[184,128]{1,0:T(8,128)S(1)}, f32[184,128]{1,0:T(8,128)S(1)}, u32[]{:S(2)}, u32[]{:S(2)}) collective-permute-start(f32[184,128]{1,0:T(8,128)S(1)} %get-tuple-element.32), channel_id=1, source_target_pairs={{0,6},{1,7},{2,0},{3,1},{4,2},{5,3},{6,4},{7,5},{8,14},{9,15},{10,... | collective-permute-start | bytes 282632 | tf_op jit(solution)/shard_map/ppermute | solution.py:717
  76.8 5.1 %collective-permute-start.8 = (f32[184,128]{1,0:T(8,128)S(1)}, f32[184,128]{1,0:T(8,128)S(1)}, u32[]{:S(2)}, u32[]{:S(2)}) collective-permute-start(f32[184,128]{1,0:T(8,128)S(1)} %get-tuple-element.33), channel_id=1, source_target_pairs={{0,7},{1,0},{2,1},{3,2},{4,3},{5,4},{6,5},{7,6},{8,15},{9,8},{10,9... | collective-permute-start | bytes 282632 | tf_op jit(solution)/shard_map/ppermute | solution.py:717
  81.9 1.1 %copy-start.7 = (f32[5,16,16,128]{3,2,1,0:T(8,128)S(1)}, f32[5,16,16,128]{3,2,1,0:T(8,128)}, u32[]{:S(2)}) copy-start(f32[5,16,16,128]{3,2,1,0:T(8,128)} %copy-done.6) | copy-start | bytes 1966084
  83.0 0.9 copy-start.9
